TPU v7x, 128 devices: a 2x2x16 block of a 8x8x16 slice. The times are simulated.
128 devices in a mesh: groups: 4 (over y, x), row: 16 (over z), col: 2 (over core).
Axes of the slice: x: 2, y: 2, z: 16, core: 2. Of those that a mesh axis runs over, the one named last changes fastest.
The devices are a block of a 8x8x16 slice.
Arguments:
- cell_index: int32 [4096, 128], P(('groups', 'row', 'col')), parts along dimension 0, may hold values from 0 to 262143
- weights: bfloat16 [4096, 512], P(('groups', 'row', 'col')), parts along dimension 0, may hold values from -6 to 6
- block_tile: int32 [4096], P(('groups', 'row', 'col')), parts along dimension 0, may hold values from 0 to 31, as said below
- spread: float32 [2, 4], replicated, may hold values from 3 to 8
Outputs:
- density: float32 [4, 16384, 2048], P(None, ('groups', 'row'), 'col'), parts along dimension 1
There are 4 independent parts, one for each index of `groups`. A program takes and returns all parts, laid end to end along the dimension named above; an argument that names none is the same for every part. Nothing has to cross between parts.
Inputs may be any that keep to these rules, and one draw needn't show every extreme that they name: `block_tile`: among the 32 blocks of one device no tile is named more than 3 times; in every draw some tile is named exactly 3 times by the blocks of every device.
All inputs are finite; a program needn't handle non-finite values.
Results may differ from a plain program's by a relative error of at most 0.0003.
Values may be sent and summed in bfloat16 or wider, within the bound.
A program may use at most 64 MiB of HBM per device.

v0:
```python
import jax
import jax.numpy as jnp
from jax import lax
from jax.sharding import PartitionSpec as P

REACH = 16
TILE_ROWS = 256
TILE_COLS = 1024
CAPACITY = 3


def in_blocks(value, dim, count):
    before, after = (value.shape[:dim], value.shape[dim + 1 :])
    return jnp.moveaxis(value.reshape(*before, count, -1, *after), dim, 0)


def in_order(tiles, dim):
    shape = list(tiles.shape[1:])
    shape[dim] *= tiles.shape[0]
    return jnp.moveaxis(tiles, 0, dim).reshape(shape)


def exchange_both(value, axis, axes, splits, concats):
    sizes = [lax.axis_size(a) for a in axes]
    tiles = in_blocks(value, splits[0], sizes[0])
    tiles = jnp.moveaxis(in_blocks(tiles, splits[1] + 1, sizes[1]), 0, 1)
    inside = tiles.shape[2:]
    tiles = tiles.reshape(-1, *inside)
    tiles = lax.all_to_all(tiles, axis, split_axis=0, concat_axis=0, tiled=True)
    tiles = in_order(tiles.reshape(*sizes, *inside), concats[0] + 1)
    return in_order(tiles, concats[1])


def with_halo(value, sides, width):
    for axis, dim in sides:
        count, length = (lax.axis_size(axis), value.shape[dim])
        up = [(i, (i + 1) % count) for i in range(count - 1)]
        down = [(j, i) for i, j in up]
        last = lax.slice_in_dim(value, length - width, length, axis=dim)
        first = lax.slice_in_dim(value, 0, width, axis=dim)
        before = lax.ppermute(last, axis, up)
        after = lax.ppermute(first, axis, down)
        value = jnp.concatenate([before, value, after], axis=dim)
    return value


def band_matrix(width, length):
    source = lax.broadcasted_iota(jnp.int32, (length + 2 * REACH, length), 0)
    target = lax.broadcasted_iota(jnp.int32, (length + 2 * REACH, length), 1)
    offsets = (source - target - REACH).astype(jnp.float32)
    values = jnp.exp(
        -(offsets * offsets)[None] / (2.0 * width[:, None, None] * width[:, None, None])
    )
    inside = jnp.abs(source - target - REACH) <= REACH
    return jnp.where(inside[None], values, 0.0)


def smooth_columns(padded, band):
    chan_count, row_total, wide = padded.shape
    span = wide - 2 * REACH
    stride = band.shape[2]
    count = span // stride
    highest = lax.Precision.HIGHEST
    leading = padded[:, :, :span].reshape(chan_count, row_total, count, stride)
    rest = padded[:, :, stride:]
    rest = jnp.pad(rest, ((0, 0), (0, 0), (0, stride - 2 * REACH)))
    trailing = rest.reshape(chan_count, row_total, count, stride)[:, :, :, : 2 * REACH]
    result = jnp.einsum("krnb,kbc->krnc", leading, band[:, :stride, :], precision=highest)
    result = result + jnp.einsum("krnb,kbc->krnc", trailing, band[:, stride:, :], precision=highest)
    return result.reshape(chan_count, row_total, span)


def shards(cell_index, weights, block_tile, spread):
    row_count = lax.axis_size("row")
    col_count = lax.axis_size("col")
    tile_count = row_count * col_count
    block_count, points = cell_index.shape
    chan_count = weights.shape[1] // points
    tile_hot = (block_tile[:, None] == jnp.arange(tile_count, dtype=jnp.int32)[None, :]).astype(
        jnp.int32
    )
    earlier = jnp.cumsum(tile_hot, axis=0) - tile_hot
    ranking = jnp.sum(earlier * tile_hot, axis=1)
    slots = block_tile * CAPACITY + ranking
    send_cells = jnp.zeros((tile_count * CAPACITY, points), jnp.int32).at[slots].set(cell_index)
    send_weights = (
        jnp.zeros((tile_count * CAPACITY, chan_count * points), jnp.bfloat16).at[slots].set(weights)
    )
    shaped = (
        send_cells.reshape(row_count, col_count, CAPACITY, points),
        send_weights.reshape(row_count, col_count, CAPACITY, chan_count * points),
    )
    got_cells, got_weights = (
        exchange_both(shaped[0], ("row", "col"), ("row", "col"), (0, 1), (0, 1)),
        exchange_both(shaped[1], ("row", "col"), ("row", "col"), (0, 1), (0, 1)),
    )
    received = tile_count * CAPACITY
    group = 16
    while received // group > 24 and received % (group * 2) == 0:
        group = group * 2
    turns = received // group
    cells_grouped = got_cells.reshape(turns, group * points)
    weights_grouped = jnp.transpose(
        got_weights.reshape(turns, group, chan_count, points), (0, 1, 3, 2)
    ).reshape(turns, group * points, chan_count)
    row_iota = jnp.arange(TILE_ROWS, dtype=jnp.int32)
    col_iota = jnp.arange(TILE_COLS, dtype=jnp.int32)

    def accumulate(running, element):
        cells, values = element
        row_hot = ((cells // TILE_COLS)[:, None] == row_iota[None, :]).astype(jnp.bfloat16)
        col_hot = ((cells % TILE_COLS)[:, None] == col_iota[None, :]).astype(jnp.bfloat16)
        scaled = (values[:, :, None] * row_hot[:, None, :]).reshape(
            row_hot.shape[0], chan_count * TILE_ROWS
        )
        layer = lax.dot_general(
            scaled, col_hot, (((0,), (0,)), ((), ())), preferred_element_type=jnp.float32
        )
        return (running + layer.reshape(chan_count, TILE_ROWS, TILE_COLS), None)

    initial = jnp.zeros((chan_count, TILE_ROWS, TILE_COLS), jnp.float32)
    density_raw, unused = lax.scan(accumulate, initial, (cells_grouped, weights_grouped))
    col_stride = 128
    col_band = band_matrix(spread[1], col_stride)
    row_band = band_matrix(spread[0], TILE_ROWS)
    highest = lax.Precision.HIGHEST
    padded = with_halo(density_raw, (("col", 2),), REACH)
    smoothed = smooth_columns(padded, col_band)
    smoothed = with_halo(smoothed, (("row", 1),), REACH)
    return jnp.einsum("kji,kjc->kic", row_band, smoothed, precision=highest)


def solution(mesh):
    return jax.shard_map(
        shards,
        mesh=mesh,
        in_specs=(
            P(("groups", "row", "col"), None),
            P(("groups", "row", "col"), None),
            P(("groups", "row", "col")),
            P(),
        ),
        out_specs=P(None, ("groups", "row"), "col"),
        check_vma=False,
    )
```

profile of v0, /device:TPU:69, one launch (start us, length us, event | category | flops | bytes accessed | tf_op | source)
XLA Modules:
  0.0 170.9 jit_solution(14475149943217974379)
XLA Ops:
  0.0 0.7 fusion.38
  0.7 0.1 reduce_window_sum.11
  0.8 0.8 select_reduce_fusion
  1.6 0.7 compare_select_fusion
  2.3 1.4 scatter_custom_fusion.1
  3.7 18.5 %all-to-all-start.1 = ((s32[32,1,1,3,128]{4,2,3,1,0:T(1,128)}), s32[32,1,1,3,128]{4,2,3,1,0:T(1,128)S(1)}, u32[]{:S(2)}, u32[]{:S(2)}) async-start(s32[32,1,1,3,128]{4,2,3,1,0:T(1,128)} %bitcast.8), calls=%async_computation.1 | async-start | bytes 98304 | tf_op jit(solution)/shard_map/all_to_all | solution.py:29
  22.2 1.0 scatter_custom_fusion
  23.2 0.7 reshape_transpose_transpose_reshape_reshape_reshape.6
  23.9 10.4 %all-to-all-done.1 = s32[32,1,1,3,128]{4,2,3,1,0:T(1,128)S(1)} async-done(((s32[32,1,1,3,128]{4,2,3,1,0:T(1,128)}), s32[32,1,1,3,128]{4,2,3,1,0:T(1,128)S(1)}, u32[]{:S(2)}, u32[]{:S(2)}) %all-to-all-start.1) | async-done | bytes 49184 | tf_op jit(solution)/shard_map/all_to_all | solution.py:29
  34.4 5.3 %all-to-all-start = ((bf16[32,1,1,3,512]{4,3,2,1,0:T(4,128)(2,1)}), bf16[32,1,1,3,512]{4,3,2,1,0:T(4,128)(2,1)S(1)}, u32[]{:S(2)}, u32[]{:S(2)}) async-start(bf16[32,1,1,3,512]{4,3,2,1,0:T(4,128)(2,1)} %bitcast.1), calls=%async_computation | async-start | bytes 262144 | tf_op jit(solution)/shard_map/all_to_all | solution.py:29
  39.8 0.8 multiply_multiply_fusion.1
  40.6 15.0 %all-to-all-done = bf16[32,1,1,3,512]{4,3,2,1,0:T(4,128)(2,1)S(1)} async-done(((bf16[32,1,1,3,512]{4,3,2,1,0:T(4,128)(2,1)}), bf16[32,1,1,3,512]{4,3,2,1,0:T(4,128)(2,1)S(1)}, u32[]{:S(2)}, u32[]{:S(2)}) %all-to-all-start) | async-done | bytes 98336 | tf_op jit(solution)/shard_map/all_to_all | solution.py:29
  55.6 0.1 reshape_reshape.6
  55.7 53.0 %while.13 = (s32[]{:T(128)}, f32[4,256,1024]{2,1,0:T(8,128)}, bf16[6,2048,4]{1,2,0:T(4,128)(2,1)S(1)}, s32[6,2048]{1,0:T(8,128)S(1)}, s32[]{:T(128)}, /*index=5*/s32[]{:T(128)}) while((s32[]{:T(128)}, f32[4,256,1024]{2,1,0:T(8,128)}, bf16[6,2048,4]{1,2,0:T(4,128)(2,1)S(1)}, s32[6,2048]{1,0:T(8,128)S(1)}, s32[]{:T(128)}, ...), condition=%wide.region_5.6_spmd.clone, body=%wide.region_4.5_spmd.clone.sunk | while | flops 4302346240 | bytes 10592343 | solution.py:122
  55.7 0.2 fusion.48
  56.0 6.7 %select_add_fusion.2 = f32[4,256,1024]{2,1,0:T(8,128)} fusion(f32[4,256,1024]{2,1,0:T(8,128)} %get-tuple-element.155, pred[]{:T(512)S(6)} %compare.16, s32[2048]{0:T(1024)S(1)} %get-tuple-element.146, bf16[2048,256]{0,1:T(8,128)(2,1)S(1)} %fusion.48, bf16[2048,4]{0,1:T(4,128)(2,1)S(1)} %dynamic-slice_bitcast_fusion.2), kind=kOutput, calls=%fused_computation.8.clone.1 | convolution fusion | flops 4301258752 | bytes 9461761 | tf_op jit(solution)/shard_map/while/body/eval_jaxpr/dot_general | solution.py:116
  62.7 0.2 fusion.48
  63.0 8.9 %select_add_fusion.2 = f32[4,256,1024]{2,1,0:T(8,128)} fusion(f32[4,256,1024]{2,1,0:T(8,128)} %get-tuple-element.155, pred[]{:T(512)S(6)} %compare.16, s32[2048]{0:T(1024)S(1)} %get-tuple-element.146, bf16[2048,256]{0,1:T(8,128)(2,1)S(1)} %fusion.48, bf16[2048,4]{0,1:T(4,128)(2,1)S(1)} %dynamic-slice_bitcast_fusion.2), kind=kOutput, calls=%fused_computation.8.clone.1 | convolution fusion | flops 4301258752 | bytes 9461761 | tf_op jit(solution)/shard_map/while/body/eval_jaxpr/dot_general | solution.py:116
  71.9 0.2 fusion.48
  72.2 8.9 %select_add_fusion.2 = f32[4,256,1024]{2,1,0:T(8,128)} fusion(f32[4,256,1024]{2,1,0:T(8,128)} %get-tuple-element.155, pred[]{:T(512)S(6)} %compare.16, s32[2048]{0:T(1024)S(1)} %get-tuple-element.146, bf16[2048,256]{0,1:T(8,128)(2,1)S(1)} %fusion.48, bf16[2048,4]{0,1:T(4,128)(2,1)S(1)} %dynamic-slice_bitcast_fusion.2), kind=kOutput, calls=%fused_computation.8.clone.1 | convolution fusion | flops 4301258752 | bytes 9461761 | tf_op jit(solution)/shard_map/while/body/eval_jaxpr/dot_general | solution.py:116
  81.1 0.2 fusion.48
  81.4 8.9 %select_add_fusion.2 = f32[4,256,1024]{2,1,0:T(8,128)} fusion(f32[4,256,1024]{2,1,0:T(8,128)} %get-tuple-element.155, pred[]{:T(512)S(6)} %compare.16, s32[2048]{0:T(1024)S(1)} %get-tuple-element.146, bf16[2048,256]{0,1:T(8,128)(2,1)S(1)} %fusion.48, bf16[2048,4]{0,1:T(4,128)(2,1)S(1)} %dynamic-slice_bitcast_fusion.2), kind=kOutput, calls=%fused_computation.8.clone.1 | convolution fusion | flops 4301258752 | bytes 9461761 | tf_op jit(solution)/shard_map/while/body/eval_jaxpr/dot_general | solution.py:116
  90.3 0.2 fusion.48
  90.6 8.9 %select_add_fusion.2 = f32[4,256,1024]{2,1,0:T(8,128)} fusion(f32[4,256,1024]{2,1,0:T(8,128)} %get-tuple-element.155, pred[]{:T(512)S(6)} %compare.16, s32[2048]{0:T(1024)S(1)} %get-tuple-element.146, bf16[2048,256]{0,1:T(8,128)(2,1)S(1)} %fusion.48, bf16[2048,4]{0,1:T(4,128)(2,1)S(1)} %dynamic-slice_bitcast_fusion.2), kind=kOutput, calls=%fused_computation.8.clone.1 | convolution fusion | flops 4301258752 | bytes 9461761 | tf_op jit(solution)/shard_map/while/body/eval_jaxpr/dot_general | solution.py:116
  99.5 0.2 fusion.48
  99.8 8.9 %select_add_fusion.2 = f32[4,256,1024]{2,1,0:T(8,128)} fusion(f32[4,256,1024]{2,1,0:T(8,128)} %get-tuple-element.155, pred[]{:T(512)S(6)} %compare.16, s32[2048]{0:T(1024)S(1)} %get-tuple-element.146, bf16[2048,256]{0,1:T(8,128)(2,1)S(1)} %fusion.48, bf16[2048,4]{0,1:T(4,128)(2,1)S(1)} %dynamic-slice_bitcast_fusion.2), kind=kOutput, calls=%fused_computation.8.clone.1 | convolution fusion | flops 4301258752 | bytes 9461761 | tf_op jit(solution)/shard_map/while/body/eval_jaxpr/dot_general | solution.py:116
  108.7 1.1 slice.40
  109.8 3.4 %collective-permute-start.1 = (f32[4,256,16]{2,1,0:T(8,128)S(1)}, f32[4,256,16]{2,1,0:T(8,128)S(1)}, u32[]{:S(2)}, u32[]{:S(2)}) collective-permute-start(f32[4,256,16]{2,1,0:T(8,128)S(1)} %slice.40), channel_id=1, source_target_pairs={{1,0},{3,2},{5,4},{7,6},{9,8},{11,10},{13,12},{15,14},{17,16},{19,... | collective-permute-start | bytes 196616 | tf_op jit(solution)/shard_map/ppermute | solution.py:42
  113.2 0.2 fusion.33
  113.4 5.4 %copy.21 = f32[4,256,1024]{1,2,0:T(8,128)} copy(f32[4,256,1024]{2,1,0:T(8,128)} %get-tuple-element.85) | data formatting | bytes 8388608 | tf_op jit(solution)/shard_map/while | solution.py:122
  118.8 0.8 slice.46
  119.7 1.5 collective-permute-start
  121.1 0.0 collective-permute-done.1
  121.1 5.4 %pad_maximum_fusion = f32[4,256,928]{2,1,0:T(8,128)} fusion(f32[4,256,16]{2,1,0:T(8,128)S(1)} %collective-permute-done.1, f32[4,256,1024]{2,1,0:T(8,128)} %get-tuple-element.85), kind=kLoop, calls=%fused_computation.31 | loop fusion | flops 950272 | bytes 8060928 | tf_op jit(solution)/shard_map/concatenate | solution.py:43
  126.6 5.2 %copy.34 = f32[4,256,928]{1,2,0:T(8,128)} copy(f32[4,256,928]{2,1,0:T(8,128)} %pad_maximum_fusion) | data formatting | bytes 7602176
  131.8 2.4 %pad.4.clone = f32[4,256,1024]{1,2,0:T(8,128)S(1)} pad(f32[4,256,928]{1,2,0:T(8,128)} %copy.34, f32[]{:T(128)} %constant.77.clone.1), padding=0_0x0_0x0_96 | pad | bytes 7995396 | tf_op jit(solution)/shard_map/jit(_pad)/pad | solution.py:66
  134.3 3.5 %fusion.27 = f32[4,256,8,128]{1,3,2,0:T(8,128)S(1)} fusion(f32[4,256,8,128]{1,3,2,0:T(8,128)S(1)} %bitcast.69, f32[4,160,128]{1,2,0:T(8,128)S(1)} %fusion.33), kind=kOutput, calls=%fused_computation.36 | convolution fusion | flops 402653184 | bytes 5505024 | tf_op jit(solution)/shard_map/krnb,kbc->krnc/dot_general | solution.py:69
  137.8 0.3 pad_maximum_fusion.1
  138.1 5.3 %convolution_add_fusion = f32[4,256,8,128]{1,3,2,0:T(8,128)} fusion(f32[4,256,8,128]{1,3,2,0:T(8,128)S(1)} %fusion.27, f32[4,256,8,128]{1,3,2,0:T(8,128)S(1)} %bitcast.67, f32[4,160,128]{1,2,0:T(8,128)S(1)} %fusion.33), kind=kOutput, calls=%fused_computation.33 | convolution fusion | flops 1611661312 | bytes 12845056 | tf_op jit(solution)/shard_map/krnb,kbc->krnc/dot_general | solution.py:68
  143.4 5.4 %copy.26 = f32[4,256,1024]{2,1,0:T(8,128)} copy(f32[4,256,1024]{1,2,0:T(8,128)} %bitcast.68) | data formatting | bytes 8388608 | tf_op jit(solution)/shard_map/reshape | solution.py:70
  148.8 1.1 fusion.41
  149.9 2.4 %collective-permute-start.2 = (f32[4,16,1024]{2,1,0:T(8,128)S(1)}, f32[4,16,1024]{2,1,0:T(8,128)S(1)}, u32[]{:S(2)}, u32[]{:S(2)}) collective-permute-start(f32[4,16,1024]{2,1,0:T(8,128)S(1)} %get-tuple-element.115), channel_id=1, source_target_pairs={{0,2},{2,4},{4,6},{6,8},{8,10},{10,12},{12,14},{14,16},{16,18},{18... | collective-permute-start | bytes 786440 | tf_op jit(solution)/shard_map/ppermute | solution.py:41
  152.3 1.5 collective-permute-start.3
  153.8 0.1 abs_compare_fusion
  153.9 0.1 multiply_negate_fusion
  154.0 2.8 %collective-permute-done.2 = f32[4,16,1024]{2,1,0:T(8,128)S(1)} collective-permute-done((f32[4,16,1024]{2,1,0:T(8,128)S(1)}, f32[4,16,1024]{2,1,0:T(8,128)S(1)}, u32[]{:S(2)}, u32[]{:S(2)}) %collective-permute-start.2) | collective-permute-done | bytes 262176 | tf_op jit(solution)/shard_map/ppermute | solution.py:41
  156.8 3.9 %collective-permute-done.3 = f32[4,16,1024]{2,1,0:T(8,128)S(1)} collective-permute-done((f32[4,16,1024]{2,1,0:T(8,128)S(1)}, f32[4,16,1024]{2,1,0:T(8,128)S(1)}, u32[]{:S(2)}, u32[]{:S(2)}) %collective-permute-start.3) | collective-permute-done | bytes 262176 | tf_op jit(solution)/shard_map/ppermute | solution.py:42
  160.7 10.2 %fusion.19 = f32[4,256,1024]{2,1,0:T(8,128)} fusion(f32[4,16,1024]{2,1,0:T(8,128)S(1)} %collective-permute-done.3, f32[4,256,1024]{2,1,0:T(8,128)} %copy.26, f32[4,16,1024]{2,1,0:T(8,128)S(1)} %collective-permute-done.2, f32[4]{0:T(128)S(1)} %get-tuple-element.117, f32[288,256]{1,0:T(8,128)S(1)} %multiply_negate_fusion, ...), kind=kOutput, calls=%fused_computation.25 | convolution fusion | flops 3626827776 | bytes 9281552 | tf_op jit(solution)/shard_map/kji,kjc->kic/dot_general | solution.py:130
  (26 shorter events, 0.3 us)
Async XLA Ops:
  3.7 30.7 %all-to-all-start.1 = ((s32[32,1,1,3,128]{4,2,3,1,0:T(1,128)}), s32[32,1,1,3,128]{4,2,3,1,0:T(1,128)S(1)}, u32[]{:S(2)}, u32[]{:S(2)}) async-start(s32[32,1,1,3,128]{4,2,3,1,0:T(1,128)} %bitcast.8), calls=%async_computation.1 | async-start | bytes 98304 | tf_op jit(solution)/shard_map/all_to_all | solution.py:29
  34.4 21.2 %all-to-all-start = ((bf16[32,1,1,3,512]{4,3,2,1,0:T(4,128)(2,1)}), bf16[32,1,1,3,512]{4,3,2,1,0:T(4,128)(2,1)S(1)}, u32[]{:S(2)}, u32[]{:S(2)}) async-start(bf16[32,1,1,3,512]{4,3,2,1,0:T(4,128)(2,1)} %bitcast.1), calls=%async_computation | async-start | bytes 262144 | tf_op jit(solution)/shard_map/all_to_all | solution.py:29
  109.8 11.4 %collective-permute-start.1 = (f32[4,256,16]{2,1,0:T(8,128)S(1)}, f32[4,256,16]{2,1,0:T(8,128)S(1)}, u32[]{:S(2)}, u32[]{:S(2)}) collective-permute-start(f32[4,256,16]{2,1,0:T(8,128)S(1)} %slice.40), channel_id=1, source_target_pairs={{1,0},{3,2},{5,4},{7,6},{9,8},{11,10},{13,12},{15,14},{17,16},{19,... | collective-permute-start | bytes 196616 | tf_op jit(solution)/shard_map/ppermute | solution.py:42
  119.7 18.1 %collective-permute-start = (f32[4,256,16]{1,2,0:T(8,128)S(1)}, f32[4,256,16]{1,2,0:T(8,128)S(1)}, u32[]{:S(2)}, u32[]{:S(2)}) collective-permute-start(f32[4,256,16]{1,2,0:T(8,128)S(1)} %slice.46), channel_id=1, source_target_pairs={{0,1},{2,3},{4,5},{6,7},{8,9},{10,11},{12,13},{14,15},{16,17},{18,... | collective-permute-start | bytes 196616 | tf_op jit(solution)/shard_map/ppermute | solution.py:41
  134.3 3.5 %copy-start = (f32[4,256,1024]{1,2,0:T(8,128)S(1)}, f32[4,256,1024]{1,2,0:T(8,128)}, u32[]{:S(2)}) copy-start(f32[4,256,1024]{1,2,0:T(8,128)} %copy.21) | copy-start | bytes 12582916
  149.9 6.9 %collective-permute-start.2 = (f32[4,16,1024]{2,1,0:T(8,128)S(1)}, f32[4,16,1024]{2,1,0:T(8,128)S(1)}, u32[]{:S(2)}, u32[]{:S(2)}) collective-permute-start(f32[4,16,1024]{2,1,0:T(8,128)S(1)} %get-tuple-element.115), channel_id=1, source_target_pairs={{0,2},{2,4},{4,6},{6,8},{8,10},{10,12},{12,14},{14,16},{16,18},{18... | collective-permute-start | bytes 786440 | tf_op jit(solution)/shard_map/ppermute | solution.py:41
  152.3 8.4 %collective-permute-start.3 = (f32[4,16,1024]{2,1,0:T(8,128)S(1)}, f32[4,16,1024]{2,1,0:T(8,128)S(1)}, u32[]{:S(2)}, u32[]{:S(2)}) collective-permute-start(f32[4,16,1024]{2,1,0:T(8,128)S(1)} %get-tuple-element.116), channel_id=1, source_target_pairs={{2,0},{4,2},{6,4},{8,6},{10,8},{12,10},{14,12},{16,14},{18,16},{20... | collective-permute-start | bytes 786440 | tf_op jit(solution)/shard_map/ppermute | solution.py:42
where the time goes:
time: 173 us; the launch traced here: 171 us
  matrix products  70.3 us (41%)
  starting transfers between devices  32.7 us (19%)
  waiting for transfers between devices  32.1 us (19%)
  local copies, waits for them, and re-layouts  24.9 us (14%)
  other arithmetic  10.5 us (6%)
    dot_general x6, matrix products, accumulate(): lax.dot_general(scaled, col_hot, (((0,), (0,)), ((), ())), preferred_elem...  51.3 us
    all_to_all x2, waiting for transfers between devices, exchange_both(): tiles = lax.all_to_all(tiles, axis, split_axis=0, concat_axis=0, tiled=True)  25.5 us
    all_to_all x2, starting transfers between devices, exchange_both(): tiles = lax.all_to_all(tiles, axis, split_axis=0, concat_axis=0, tiled=True)  23.8 us
    dot_general x1, matrix products, shards(): return jnp.einsum('kji,kjc->kic', row_band, smoothed, precision=highest)  10.2 us
    concatenate x2, other arithmetic, with_halo(): value = jnp.concatenate([before, value, after], axis=dim)  5.75 us
    while x1, local copies, waits for them, and re-layouts, shards(): lax.scan(accumulate, initial, (cells_grouped, weights_grouped))  5.43 us
    reshape x1, local copies, waits for them, and re-layouts, smooth_columns(): return result.reshape(chan_count, row_total, span)  5.42 us
    dot_general x1, matrix products, smooth_columns(): jnp.einsum('krnb,kbc->krnc', leading, band[:, :stride, :], precision=high...  5.33 us
  transfers between devices with their start and end apart: 6, of which 4 were waited for; matrix products, arithmetic and copies ran while one was open for 15% of the time, Pallas kernels for 0%

commit v1 on v0

v1 whole, which is shorter than its diff:
```python
import functools

import jax
import jax.numpy as jnp
from jax import lax
from jax.experimental import pallas as pl
from jax.experimental.pallas import tpu as pltpu
from jax.sharding import PartitionSpec as P

REACH = 16
TILE_ROWS = 256
TILE_COLS = 1024
CAPACITY = 3
LANES = 128
WINDOW = 88
MESH = pl.DeviceIdType.MESH
F32 = jnp.float32
BF16 = jnp.bfloat16


def iota(shape, dim):
    return lax.broadcasted_iota(jnp.int32, shape, dim)


def exchange_kernel(
    rows_n, cols_n, cell_ref, weight_ref, tile_ref, cells_out, weights_out,
    ranks, values, sorted_points, send_cells, send_weights, send_sem, recv_sem, local_sem
):
    blocks, points = cell_ref.shape
    channels = weight_ref.shape[1] // points
    peers = rows_n * cols_n
    my_row, my_col = lax.axis_index("row"), lax.axis_index("col")
    me = my_row * cols_n + my_col

    offsets = []
    for distance in range(rows_n // 2, 0, -1):
        for step in (distance, rows_n - distance):
            if step not in [o[0] for o in offsets]:
                offsets += [(step, c) for c in range(cols_n)]
    offsets += [(0, c) for c in range(1, cols_n)]

    barrier = pltpu.get_barrier_semaphore()
    targets = []
    for step, turn in offsets:
        row = lax.rem(my_row + step, rows_n)
        col = lax.rem(my_col + turn, cols_n)
        targets.append((row, col))
        pl.semaphore_signal(
            barrier, inc=1, device_id={"row": row, "col": col}, device_id_type=MESH
        )

    cells = cell_ref[...]
    point_row = cells // TILE_COLS
    col = cells % TILE_COLS
    key = (point_row * points + iota(cells.shape, 1)).astype(F32)
    pad = jnp.zeros((points - blocks, points), F32)
    key_t = jnp.transpose(jnp.concatenate([key, pad], axis=0))
    weights = weight_ref[...].astype(F32)
    values[0] = point_row.astype(F32)
    values[1] = (col // LANES).astype(F32)
    values[2] = (col % LANES).astype(F32)
    for c in range(channels):
        values[3 + c] = weights[:, c * points : (c + 1) * points]
    quarter = points // 4
    position = iota((points, points), 0)
    for b in range(blocks):
        less = (key_t[:, b : b + 1] < key[b : b + 1, :]).astype(F32)
        rank = jnp.sum(less, axis=0, keepdims=True).astype(jnp.int32)
        lane = (rank % 4) * quarter + rank // 4
        hot = (position == lane).astype(BF16)
        piece = jnp.concatenate(
            [values[v, b : b + 1, :] for v in range(3 + channels)]
            + [jnp.zeros((1, points), F32)],
            axis=0,
        ).astype(BF16)
        sorted_points[b] = lax.dot_general(
            piece, hot, (((1,), (1,)), ((), ())), preferred_element_type=F32
        )

    tile = tile_ref[...]
    tile_down = jnp.sum(
        jnp.where(iota((blocks, blocks), 0) == iota((blocks, blocks), 1), tile, 0),
        axis=1,
        keepdims=True,
    )
    earlier = (tile_down == tile) & (iota((blocks, blocks), 0) < iota((blocks, blocks), 1))
    turn_of = jnp.sum(earlier.astype(jnp.int32), axis=0, keepdims=True)
    for k in range(CAPACITY):
        place = (
            (iota((peers, blocks), 0) == tile) & (turn_of == k)
        ).astype(BF16)
        placed = [
            lax.dot_general(
                place,
                sorted_points[:, v, :].astype(BF16),
                (((1,), (0,)), ((), ())),
                preferred_element_type=F32,
            )
            for v in range(3 + channels)
        ]
        cell = placed[0] * TILE_COLS + placed[1] * LANES + placed[2]
        send_cells[:, k, :] = cell.astype(jnp.int32)
        for c in range(channels):
            send_weights[:, k * channels + c, :] = placed[3 + c].astype(BF16)

    own = [
        pltpu.make_async_copy(send_cells.at[me], cells_out.at[me], local_sem.at[0]),
        pltpu.make_async_copy(send_weights.at[me], weights_out.at[me], local_sem.at[1]),
    ]
    pl.semaphore_wait(barrier, peers - 1)
    copies = []
    for i, (row, col) in enumerate(targets):
        peer = row * cols_n + col
        for a, (source, out) in enumerate(
            ((send_cells, cells_out), (send_weights, weights_out))
        ):
            copy = pltpu.make_async_remote_copy(
                src_ref=source.at[peer],
                dst_ref=out.at[me],
                send_sem=send_sem.at[a, i],
                recv_sem=recv_sem.at[a, i],
                device_id={"row": row, "col": col},
                device_id_type=MESH,
            )
            copy.start()
            copies.append(copy)
    for copy in own:
        copy.start()
    for copy in own:
        copy.wait()
    for copy in copies:
        copy.wait_recv()
    for copy in copies:
        copy.wait_send()


def exchange(cell_index, weights, block_tile, rows_n, cols_n):
    blocks, points = cell_index.shape
    channels = weights.shape[1] // points
    peers = rows_n * cols_n
    vmem = pl.BlockSpec(memory_space=pltpu.VMEM)
    return pl.pallas_call(
        functools.partial(exchange_kernel, rows_n, cols_n),
        name="exchange",
        out_shape=(
            jax.ShapeDtypeStruct((peers, CAPACITY, points), jnp.int32),
            jax.ShapeDtypeStruct((peers, CAPACITY * channels, points), BF16),
        ),
        in_specs=[vmem] * 3,
        out_specs=(vmem, vmem),
        scratch_shapes=[
            pltpu.VMEM((blocks, points), F32),
            pltpu.VMEM((3 + channels, blocks, points), F32),
            pltpu.VMEM((blocks, 8, points), F32),
            pltpu.VMEM((peers, CAPACITY, points), jnp.int32),
            pltpu.VMEM((peers, CAPACITY * channels, points), BF16),
            pltpu.SemaphoreType.DMA((2, peers - 1)),
            pltpu.SemaphoreType.DMA((2, peers - 1)),
            pltpu.SemaphoreType.DMA((2,)),
        ],
        compiler_params=pltpu.CompilerParams(collective_id=0, has_side_effects=True),
    )(cell_index, weights, block_tile.reshape(1, -1))


def turned(slots, quarter):
    wide = jnp.concatenate(
        [
            jnp.concatenate([s[:, v * quarter : (v + 1) * quarter] for v in range(4)], axis=0)
            for s in slots
        ]
        + [jnp.zeros((LANES, LANES - len(slots) * quarter), F32)],
        axis=1,
    )
    return jnp.transpose(wide)


def scatter_kernel(cells_ref, weights_ref, raw_ref, rows_s, cols_s, weights_s, wide_s):
    senders, slots, points = cells_ref.shape
    channels = weights_ref.shape[1] // slots
    quarter = points // 4
    raw_ref[...] = jnp.zeros_like(raw_ref)
    wide_s[...] = weights_ref[...].astype(F32)
    cells = turned([cells_ref[:, k, :].astype(F32) for k in range(slots)], quarter).astype(jnp.int32)
    rows_s[...] = cells // TILE_COLS
    cols_s[...] = cells % TILE_COLS
    for c in range(channels):
        weights_s[c] = turned([wide_s[:, k * channels + c, :] for k in range(slots)], quarter)
    chunk_rows = 2
    chunks = quarter // chunk_rows
    span = 256

    def chunk(j, carry):
        def take(ref):
            return jnp.concatenate(
                [
                    ref[pl.ds(quarter * k + chunk_rows * j + i, 1), :]
                    for k in range(slots)
                    for i in range(chunk_rows)
                ],
                axis=1,
            )

        row = take(rows_s)
        col = take(cols_s)
        weight = [take(weights_s.at[c]) for c in range(channels)]
        first = jnp.min(row) // 8 * 8
        last = jnp.max(row)
        count = row.shape[1]

        def window(low):
            base = pl.multiple_of(jnp.minimum(low, TILE_ROWS - WINDOW), 8)
            offset = jnp.where(row >= low, row - base, -1)
            hot = iota((WINDOW, count), 0) == offset
            left = jnp.concatenate(
                [jnp.where(hot, weight[c], 0.0).astype(BF16) for c in range(channels)], axis=0
            )
            for g in range(TILE_COLS // span):
                right = (iota((span, count), 0) == col - g * span).astype(F32).astype(BF16)
                layer = lax.dot_general(
                    left, right, (((1,), (1,)), ((), ())), preferred_element_type=F32
                )
                for c in range(channels):
                    raw_ref[c, pl.ds(base, WINDOW), g * span : (g + 1) * span] += layer[
                        c * WINDOW : (c + 1) * WINDOW
                    ]
            return low + WINDOW

        lax.while_loop(lambda low: low <= last, window, first)
        return carry

    lax.fori_loop(0, chunks, chunk, 0)


def scatter(cells, weights):
    senders, slots, points = cells.shape
    channels = weights.shape[1] // slots
    vmem = pl.BlockSpec(memory_space=pltpu.VMEM)
    return pl.pallas_call(
        scatter_kernel,
        name="scatter",
        out_shape=jax.ShapeDtypeStruct((channels, TILE_ROWS, TILE_COLS), F32),
        in_specs=[vmem] * 2,
        out_specs=vmem,
        scratch_shapes=[
            pltpu.VMEM((LANES, LANES), jnp.int32),
            pltpu.VMEM((LANES, LANES), jnp.int32),
            pltpu.VMEM((channels, LANES, LANES), F32),
            pltpu.VMEM((senders, slots * channels, points), F32),
        ],
        cost_estimate=pl.CostEstimate(
            flops=2 * channels * WINDOW * TILE_COLS * senders * slots * points,
            bytes_accessed=4 * channels * TILE_ROWS * TILE_COLS,
            transcendentals=0,
        ),
    )(cells, weights)


def split(value):
    high = value.astype(BF16)
    return high, (value - high.astype(F32)).astype(BF16)


def tap(offset, width):
    near = jnp.abs(offset) <= REACH
    far = offset.astype(F32)
    return jnp.where(near, jnp.exp(-(far * far) / (2.0 * width * width)), 0.0)


def dot(a, b):
    return lax.dot_general(a, b, (((1,), (0,)), ((), ())), preferred_element_type=F32)


def smooth_kernel(spread_ref, raw_ref, up_ref, down_ref, side_ref, out_ref, tall, rows_done):
    c = pl.program_id(0)
    half = TILE_ROWS // 2
    tall_rows = TILE_ROWS + 2 * REACH
    wide = TILE_COLS + LANES
    tall[0:REACH, :TILE_COLS] = up_ref[0]
    tall[REACH : REACH + TILE_ROWS, :TILE_COLS] = raw_ref[0]
    tall[REACH + TILE_ROWS :, :TILE_COLS] = down_ref[0]
    tall[:, TILE_COLS:] = side_ref[0]
    row_width = spread_ref[0, c]
    col_width = spread_ref[1, c]
    for h in range(2):
        top = h * 2 * REACH
        depth = TILE_ROWS
        target = iota((half, depth), 0) + h * half
        source = iota((half, depth), 1) + top - REACH
        band_high, band_low = split(tap(source - target, row_width))
        x_high, x_low = split(tall[top : top + depth, :])
        both = dot(jnp.concatenate([band_high, band_low], axis=0), x_high)
        rows_done[h * half : (h + 1) * half, :] = (
            both[:half] + both[half:] + dot(band_high, x_low)
        )
    source = iota((2 * LANES, LANES), 0)
    target = iota((2 * LANES, LANES), 1)
    source = jnp.where(
        source < LANES + LANES // 2, source, source - 2 * LANES
    )
    band_high, band_low = split(tap(source - target, col_width))
    band = jnp.concatenate([band_high, band_low], axis=1)
    lanes = iota((TILE_ROWS, LANES), 1)
    count = TILE_COLS // LANES
    for n in range(count):
        before = n - 1 if n else count
        after = n + 1 if n + 1 < count else count
        own = rows_done[:, n * LANES : (n + 1) * LANES]
        edge = jnp.where(
            lanes < LANES // 2,
            rows_done[:, after * LANES : (after + 1) * LANES],
            rows_done[:, before * LANES : (before + 1) * LANES],
        )
        x_high, x_low = split(jnp.concatenate([own, edge], axis=1))
        both = dot(x_high, band)
        out_ref[0, :, n * LANES : (n + 1) * LANES] = (
            both[:, :LANES] + both[:, LANES:] + dot(x_low, band_high)
        )


def smooth(spread, raw, up, down, side):
    channels = raw.shape[0]
    tall = TILE_ROWS + 2 * REACH

    def block(rows, cols):
        return pl.BlockSpec((1, rows, cols), lambda c: (c, 0, 0))

    return pl.pallas_call(
        smooth_kernel,
        name="smooth",
        grid=(channels,),
        out_shape=jax.ShapeDtypeStruct((channels, TILE_ROWS, TILE_COLS), F32),
        in_specs=[
            pl.BlockSpec(memory_space=pltpu.SMEM),
            block(TILE_ROWS, TILE_COLS),
            block(REACH, TILE_COLS),
            block(REACH, TILE_COLS),
            block(tall, LANES),
        ],
        out_specs=block(TILE_ROWS, TILE_COLS),
        scratch_shapes=[
            pltpu.VMEM((tall, TILE_COLS + LANES), F32),
            pltpu.VMEM((TILE_ROWS, TILE_COLS + LANES), F32),
        ],
    )(spread, raw, up, down, side)


def neighbours(value, axis, dim, width):
    count, length = lax.axis_size(axis), value.shape[dim]
    up = [(i, i + 1) for i in range(count - 1)]
    down = [(j, i) for i, j in up]
    last = lax.slice_in_dim(value, length - width, length, axis=dim)
    first = lax.slice_in_dim(value, 0, width, axis=dim)
    return lax.ppermute(last, axis, up), lax.ppermute(first, axis, down)


def shards(cell_index, weights, block_tile, spread):
    rows_n, cols_n = lax.axis_size("row"), lax.axis_size("col")
    cells, points = exchange(cell_index, weights, block_tile, rows_n, cols_n)
    raw = scatter(cells, points)
    up, down = neighbours(raw, "row", 1, REACH)
    edges = jnp.concatenate(
        [
            jnp.concatenate([a[:, :, :REACH], a[:, :, -REACH:]], axis=2)
            for a in (up, raw, down)
        ],
        axis=1,
    )
    left, right = neighbours(edges, "col", 2, REACH)
    middle = jnp.zeros(edges.shape[:2] + (LANES - 2 * REACH,), F32)
    side = jnp.concatenate([right, middle, left], axis=2)
    return smooth(spread, raw, up, down, side)


def solution(mesh):
    return jax.shard_map(
        shards,
        mesh=mesh,
        in_specs=(
            P(("groups", "row", "col"), None),
            P(("groups", "row", "col"), None),
            P(("groups", "row", "col")),
            P(),
        ),
        out_specs=P(None, ("groups", "row"), "col"),
        check_vma=False,
    )
```

time: 173 us -> 91.4 us (0.53)
  matrix products: 70.3 us -> 0 us
  Pallas kernels: 0 us -> 57.3 us
  waiting for transfers between devices: 32.1 us -> 1.91 us
  local copies, waits for them, and re-layouts: 24.9 us -> 3.64 us
  other arithmetic: 10.5 us -> 1.35 us
  starting transfers between devices: 32.7 us -> 25.5 us
    dot_general x9 -> x0, matrix products: 70.3 us -> none  [the longest x6 51.3 us: accumulate(): lax.dot_general(scaled, col_hot, (((0,), (0,)), ((), ())), preferred_elem...]
    pallas_call x0 -> x3, Pallas kernels: none -> 57.3 us  [the longest x1 29.4 us: exchange(): pl.pallas_call(functools.partial(exchange_kernel, rows_n, cols_n), name='...]
    all_to_all x2 -> x0, waiting for transfers between devices: 25.5 us -> none  [exchange_both(): tiles = lax.all_to_all(tiles, axis, split_axis=0, concat_axis=0, tiled=True)]
    all_to_all x2 -> x0, starting transfers between devices: 23.8 us -> none  [exchange_both(): tiles = lax.all_to_all(tiles, axis, split_axis=0, concat_axis=0, tiled=True)]
    ppermute x4, starting transfers between devices: 8.84 us -> 25.5 us  [neighbours(): return (lax.ppermute(last, axis, up), lax.ppermute(first, axis, down))]
    reshape x2 -> x0, local copies, waits for them, and re-layouts: 5.43 us -> none  [the longest x1 5.42 us: smooth_columns(): return result.reshape(chan_count, row_total, span)]
    while x1 -> x0, local copies, waits for them, and re-layouts: 5.43 us -> none  [shards(): lax.scan(accumulate, initial, (cells_grouped, weights_grouped))]
    unnamed x3 -> x4, local copies, waits for them, and re-layouts: 5.23 us -> 0.01 us
  transfers between devices with their start and end apart: 6 -> 4, of which waited for: 4 -> 2; matrix products, arithmetic and copies ran while one was open for 15% -> 3% of each run, Pallas kernels for 0% -> 0%
where the time goes in v1:
time: 91.4 us; the launch traced here: 89.8 us
  Pallas kernels  57.3 us (63%)
  starting transfers between devices  25.5 us (28%)
  local copies, waits for them, and re-layouts  3.64 us (4%)
  waiting for transfers between devices  1.91 us (2%)
  other arithmetic  1.35 us (1%)
    pallas_call x1, Pallas kernels, exchange(): pl.pallas_call(functools.partial(exchange_kernel, rows_n, cols_n), name='...  29.4 us
    ppermute x4, starting transfers between devices, neighbours(): return (lax.ppermute(last, axis, up), lax.ppermute(first, axis, down))  25.5 us
    pallas_call x1, Pallas kernels, scatter(): pl.pallas_call(scatter_kernel, name='scatter', out_shape=jax.ShapeDtypeSt...  19.8 us
    pallas_call x1, Pallas kernels, smooth(): pl.pallas_call(smooth_kernel, name='smooth', grid=(channels,), out_shape=...  8.11 us
    ppermute x4, waiting for transfers between devices, neighbours(): return (lax.ppermute(last, axis, up), lax.ppermute(first, axis, down))  1.91 us
  transfers between devices with their start and end apart: 4, of which 2 were waited for; matrix products, arithmetic and copies ran while one was open for 3% of the time, Pallas kernels for 0%

profile of v1, /device:TPU:69, one launch (start us, length us, event | category | flops | bytes accessed | tf_op | source)
XLA Modules:
  0.0 89.8 jit_solution(12111074289518405938)
XLA Ops:
  0.0 29.4 %exchange.1 = (s32[32,3,128]{2,1,0:T(4,128)}, bf16[32,12,128]{2,1,0:T(8,128)(2,1)}) custom-call(s32[32,128]{1,0:T(8,128)} %cell_ref.1, bf16[32,512]{1,0:T(8,128)(2,1)} %weight_ref.1, s32[1,32]{1,0:T(1,128)} %bitcast.1), custom_call_target="tpu_custom_call" | custom-call | tf_op jit(solution)/shard_map/exchange/pallas_call | solution.py:142
  29.4 19.8 %scatter.1.raw_ref = f32[4,256,1024]{2,1,0:T(8,128)} custom-call(s32[32,3,128]{2,1,0:T(4,128)} %get-tuple-element.7.cells_ref, bf16[32,12,128]{2,1,0:T(8,128)(2,1)} %get-tuple-element.8.weights_ref), custom_call_target="tpu_custom_call" | custom-call | flops 8858370048 | bytes 4194304 | tf_op jit(solution)/shard_map/scatter/pallas_call | solution.py:238
  49.2 1.1 %fusion.1 = (f32[4,16,1024]{2,1,0:T(8,128)S(1)}, f32[4,16,1024]{2,1,0:T(8,128)S(1)}) fusion(f32[4,256,1024]{2,1,0:T(8,128)} %scatter.1.raw_ref), kind=kLoop, calls=%fused_computation.5 | loop fusion | bytes 1048576 | tf_op jit(solution)/shard_map/slice | solution.py:352
  50.2 1.3 %collective-permute-start.1 = (f32[4,16,1024]{2,1,0:T(8,128)S(1)}, f32[4,16,1024]{2,1,0:T(8,128)S(1)}, u32[]{:S(2)}, u32[]{:S(2)}) collective-permute-start(f32[4,16,1024]{2,1,0:T(8,128)S(1)} %get-tuple-element.11), channel_id=1, source_target_pairs={{2,0},{4,2},{6,4},{8,6},{10,8},{12,10},{14,12},{16,14},{18,16},{20... | collective-permute-start | bytes 786440 | tf_op jit(solution)/shard_map/ppermute | solution.py:353
  51.6 4.0 %collective-permute-start = (f32[4,16,1024]{2,1,0:T(8,128)S(1)}, f32[4,16,1024]{2,1,0:T(8,128)S(1)}, u32[]{:S(2)}, u32[]{:S(2)}) collective-permute-start(f32[4,16,1024]{2,1,0:T(8,128)S(1)} %get-tuple-element.12), channel_id=1, source_target_pairs={{0,2},{2,4},{4,6},{6,8},{8,10},{10,12},{12,14},{14,16},{16,18},{18... | collective-permute-start | bytes 786440 | tf_op jit(solution)/shard_map/ppermute | solution.py:353
  55.6 1.4 %fusion = (f32[4,256,16]{2,1,0:T(8,128)S(1)}, f32[4,256,16]{2,1,0:T(8,128)S(1)}) fusion(f32[4,256,1024]{2,1,0:T(8,128)} %scatter.1.raw_ref), kind=kLoop, calls=%fused_computation.4 | loop fusion | bytes 262144 | tf_op jit(solution)/shard_map/slice | solution.py:363
  57.0 0.2 copy.5
  57.2 0.2 copy.6
  57.4 0.0 collective-permute-done.1.down_ref
  57.4 0.0 copy-start
  57.4 0.1 fusion.3
  57.5 0.1 pad_maximum_fusion.3
  57.5 0.1 copy.8
  57.6 1.3 %collective-permute-done.up_ref = f32[4,16,1024]{2,1,0:T(8,128)S(1)} collective-permute-done((f32[4,16,1024]{2,1,0:T(8,128)S(1)}, f32[4,16,1024]{2,1,0:T(8,128)S(1)}, u32[]{:S(2)}, u32[]{:S(2)}) %collective-permute-start) | collective-permute-done | bytes 262176 | tf_op jit(solution)/shard_map/ppermute | solution.py:353
  58.9 0.0 copy-start.1
  58.9 0.1 fusion.2
  59.0 0.1 pad_maximum_fusion.2
  59.0 0.1 copy.7
  59.1 0.1 pad_maximum_fusion.1
  59.3 1.3 %collective-permute-start.3 = (f32[4,288,16]{1,2,0:T(8,128)S(1)}, f32[4,288,16]{1,2,0:T(8,128)S(1)}, u32[]{:S(2)}, u32[]{:S(2)}) collective-permute-start(f32[4,288,16]{1,2,0:T(8,128)S(1)} %get-tuple-element.18), channel_id=1, source_target_pairs={{0,1},{2,3},{4,5},{6,7},{8,9},{10,11},{12,13},{14,15},{16,17},{18,... | collective-permute-start | bytes 221192 | tf_op jit(solution)/shard_map/ppermute | solution.py:353
  60.6 18.8 %collective-permute-start.2 = (f32[4,288,16]{1,2,0:T(8,128)S(1)}, f32[4,288,16]{1,2,0:T(8,128)S(1)}, u32[]{:S(2)}, u32[]{:S(2)}) collective-permute-start(f32[4,288,16]{1,2,0:T(8,128)S(1)} %get-tuple-element.17), channel_id=1, source_target_pairs={{1,0},{3,2},{5,4},{7,6},{9,8},{11,10},{13,12},{15,14},{17,16},{19,... | collective-permute-start | bytes 221192 | tf_op jit(solution)/shard_map/ppermute | solution.py:353
  79.5 0.1 pad.1.clone
  79.5 0.0 collective-permute-done.3
  79.5 0.2 copy.10
  79.8 0.6 collective-permute-done.2
  80.4 0.2 copy.9
  80.6 1.0 %pad_maximum_fusion.side_ref = f32[4,288,128]{2,1,0:T(8,128)} fusion(f32[4,288,16]{2,1,0:T(8,128)S(1)} %copy.10, f32[4,288,16]{2,1,0:T(8,128)S(1)} %copy.9, f32[128]{0:T(128)S(1)} %pad.1.clone), kind=kLoop, calls=%fused_computation | loop fusion | flops 294912 | bytes 737792 | tf_op jit(solution)/shard_map/concatenate | solution.py:370
  81.6 0.0 copy-done
  81.6 0.0 copy-done.1
  81.6 8.1 %smooth.1 = f32[4,256,1024]{2,1,0:T(8,128)} custom-call(f32[2,4]{1,0:T(2,128)} %spread_ref.1, f32[4,256,1024]{2,1,0:T(8,128)} %scatter.1.raw_ref, f32[4,16,1024]{2,1,0:T(8,128)} %copy-done.1, f32[4,16,1024]{2,1,0:T(8,128)} %copy-done, f32[4,288,128]{2,1,0:T(8,128)} %pad_maximum_fusion.side_ref), custom_call_target="tpu_custom_call" | custom-call | tf_op jit(solution)/shard_map/smooth/pallas_call | solution.py:327
  (2 shorter events, 0.0 us)
Async XLA Ops:
  50.2 7.1 %collective-permute-start.1 = (f32[4,16,1024]{2,1,0:T(8,128)S(1)}, f32[4,16,1024]{2,1,0:T(8,128)S(1)}, u32[]{:S(2)}, u32[]{:S(2)}) collective-permute-start(f32[4,16,1024]{2,1,0:T(8,128)S(1)} %get-tuple-element.11), channel_id=1, source_target_pairs={{2,0},{4,2},{6,4},{8,6},{10,8},{12,10},{14,12},{16,14},{18,16},{20... | collective-permute-start | bytes 786440 | tf_op jit(solution)/shard_map/ppermute | solution.py:353
  51.6 7.3 %collective-permute-start = (f32[4,16,1024]{2,1,0:T(8,128)S(1)}, f32[4,16,1024]{2,1,0:T(8,128)S(1)}, u32[]{:S(2)}, u32[]{:S(2)}) collective-permute-start(f32[4,16,1024]{2,1,0:T(8,128)S(1)} %get-tuple-element.12), channel_id=1, source_target_pairs={{0,2},{2,4},{4,6},{6,8},{8,10},{10,12},{12,14},{14,16},{16,18},{18... | collective-permute-start | bytes 786440 | tf_op jit(solution)/shard_map/ppermute | solution.py:353
  57.4 24.3 %copy-start = (f32[4,16,1024]{2,1,0:T(8,128)}, f32[4,16,1024]{2,1,0:T(8,128)S(1)}, u32[]{:S(2)}) copy-start(f32[4,16,1024]{2,1,0:T(8,128)S(1)} %collective-permute-done.1.down_ref) | copy-start | bytes 786436
  58.9 22.8 %copy-start.1 = (f32[4,16,1024]{2,1,0:T(8,128)}, f32[4,16,1024]{2,1,0:T(8,128)S(1)}, u32[]{:S(2)}) copy-start(f32[4,16,1024]{2,1,0:T(8,128)S(1)} %collective-permute-done.up_ref) | copy-start | bytes 786436
  59.3 20.2 %collective-permute-start.3 = (f32[4,288,16]{1,2,0:T(8,128)S(1)}, f32[4,288,16]{1,2,0:T(8,128)S(1)}, u32[]{:S(2)}, u32[]{:S(2)}) collective-permute-start(f32[4,288,16]{1,2,0:T(8,128)S(1)} %get-tuple-element.18), channel_id=1, source_target_pairs={{0,1},{2,3},{4,5},{6,7},{8,9},{10,11},{12,13},{14,15},{16,17},{18,... | collective-permute-start | bytes 221192 | tf_op jit(solution)/shard_map/ppermute | solution.py:353
  60.6 19.8 %collective-permute-start.2 = (f32[4,288,16]{1,2,0:T(8,128)S(1)}, f32[4,288,16]{1,2,0:T(8,128)S(1)}, u32[]{:S(2)}, u32[]{:S(2)}) collective-permute-start(f32[4,288,16]{1,2,0:T(8,128)S(1)} %get-tuple-element.17), channel_id=1, source_target_pairs={{1,0},{3,2},{5,4},{7,6},{9,8},{11,10},{13,12},{15,14},{17,16},{19,... | collective-permute-start | bytes 221192 | tf_op jit(solution)/shard_map/ppermute | solution.py:353

commit v2 on v1

--- a/solution.py
+++ b/solution.py
@@ -12,7 +12,7 @@
 TILE_COLS = 1024
 CAPACITY = 3
 LANES = 128
-WINDOW = 88
+WINDOW = 80
 MESH = pl.DeviceIdType.MESH
 F32 = jnp.float32
 BF16 = jnp.bfloat16
@@ -85,10 +85,12 @@
     )
     earlier = (tile_down == tile) & (iota((blocks, blocks), 0) < iota((blocks, blocks), 1))
     turn_of = jnp.sum(earlier.astype(jnp.int32), axis=0, keepdims=True)
+    lane = iota((1, points), 1)
+    ramp = ((lane % quarter) * 4 + lane // quarter) * (TILE_ROWS // points) * TILE_COLS
     for k in range(CAPACITY):
-        place = (
-            (iota((peers, blocks), 0) == tile) & (turn_of == k)
-        ).astype(BF16)
+        chosen = ((iota((peers, blocks), 0) == tile) & (turn_of == k)).astype(F32)
+        empty = jnp.sum(chosen, axis=1, keepdims=True) < 0.5
+        place = chosen.astype(BF16)
         placed = [
             lax.dot_general(
                 place,
@@ -99,7 +101,7 @@
             for v in range(3 + channels)
         ]
         cell = placed[0] * TILE_COLS + placed[1] * LANES + placed[2]
-        send_cells[:, k, :] = cell.astype(jnp.int32)
+        send_cells[:, k, :] = jnp.where(empty, ramp, cell.astype(jnp.int32))
         for c in range(channels):
             send_weights[:, k * channels + c, :] = placed[3 + c].astype(BF16)
 
@@ -158,7 +160,7 @@
             pltpu.SemaphoreType.DMA((2, peers - 1)),
             pltpu.SemaphoreType.DMA((2,)),
         ],
-        compiler_params=pltpu.CompilerParams(collective_id=0, has_side_effects=True),
+        compiler_params=pltpu.CompilerParams(collective_id=0, has_side_effects=True, vmem_limit_bytes=8 << 20),
     )(cell_index, weights, block_tile.reshape(1, -1))
 
 
@@ -247,6 +249,7 @@
             pltpu.VMEM((channels, LANES, LANES), F32),
             pltpu.VMEM((senders, slots * channels, points), F32),
         ],
+        compiler_params=pltpu.CompilerParams(vmem_limit_bytes=16 << 20),
         cost_estimate=pl.CostEstimate(
             flops=2 * channels * WINDOW * TILE_COLS * senders * slots * points,
             bytes_accessed=4 * channels * TILE_ROWS * TILE_COLS,
@@ -270,105 +273,156 @@
     return lax.dot_general(a, b, (((1,), (0,)), ((), ())), preferred_element_type=F32)
 
 
-def smooth_kernel(spread_ref, raw_ref, up_ref, down_ref, side_ref, out_ref, tall, rows_done):
-    c = pl.program_id(0)
-    half = TILE_ROWS // 2
-    tall_rows = TILE_ROWS + 2 * REACH
-    wide = TILE_COLS + LANES
-    tall[0:REACH, :TILE_COLS] = up_ref[0]
-    tall[REACH : REACH + TILE_ROWS, :TILE_COLS] = raw_ref[0]
-    tall[REACH + TILE_ROWS :, :TILE_COLS] = down_ref[0]
-    tall[:, TILE_COLS:] = side_ref[0]
-    row_width = spread_ref[0, c]
-    col_width = spread_ref[1, c]
-    for h in range(2):
-        top = h * 2 * REACH
-        depth = TILE_ROWS
-        target = iota((half, depth), 0) + h * half
-        source = iota((half, depth), 1) + top - REACH
-        band_high, band_low = split(tap(source - target, row_width))
-        x_high, x_low = split(tall[top : top + depth, :])
-        both = dot(jnp.concatenate([band_high, band_low], axis=0), x_high)
-        rows_done[h * half : (h + 1) * half, :] = (
-            both[:half] + both[half:] + dot(band_high, x_low)
-        )
-    source = iota((2 * LANES, LANES), 0)
-    target = iota((2 * LANES, LANES), 1)
-    source = jnp.where(
-        source < LANES + LANES // 2, source, source - 2 * LANES
-    )
-    band_high, band_low = split(tap(source - target, col_width))
-    band = jnp.concatenate([band_high, band_low], axis=1)
-    lanes = iota((TILE_ROWS, LANES), 1)
-    count = TILE_COLS // LANES
-    for n in range(count):
-        before = n - 1 if n else count
-        after = n + 1 if n + 1 < count else count
-        own = rows_done[:, n * LANES : (n + 1) * LANES]
-        edge = jnp.where(
-            lanes < LANES // 2,
-            rows_done[:, after * LANES : (after + 1) * LANES],
-            rows_done[:, before * LANES : (before + 1) * LANES],
-        )
-        x_high, x_low = split(jnp.concatenate([own, edge], axis=1))
-        both = dot(x_high, band)
-        out_ref[0, :, n * LANES : (n + 1) * LANES] = (
-            both[:, :LANES] + both[:, LANES:] + dot(x_low, band_high)
-        )
-
-
-def smooth(spread, raw, up, down, side):
-    channels = raw.shape[0]
-    tall = TILE_ROWS + 2 * REACH
-
-    def block(rows, cols):
-        return pl.BlockSpec((1, rows, cols), lambda c: (c, 0, 0))
-
+def smooth_kernel(
+    rows_n, cols_n, spread_ref, raw_ref, out_ref, tall, side, above, below, send_sem, recv_sem
+):
+    channels, height, width = raw_ref.shape
+    my_row, my_col = lax.axis_index("row"), lax.axis_index("col")
+    other = lax.rem(my_col + 1, cols_n)
+    prev = lax.rem(my_row + rows_n - 1, rows_n)
+    following = lax.rem(my_row + 1, rows_n)
+
+    def at(row, col):
+        return {"row": row, "col": col}
+
+    barrier = pltpu.get_barrier_semaphore()
+    peers = [at(prev, my_col), at(following, my_col), at(prev, other), at(following, other), at(my_row, other)]
+    for peer in peers:
+        pl.semaphore_signal(barrier, inc=1, device_id=peer, device_id_type=MESH)
+    pl.semaphore_wait(barrier, len(peers))
+    near = pl.ds(pl.multiple_of((1 - my_col) * (width - LANES), LANES), LANES)
+    main = pl.ds(0, width)
+    beyond = pl.ds(width, LANES)
+    top, bottom = pl.ds(0, REACH), pl.ds(height - REACH, REACH)
+
+    def copies(c, only=slice(0, 5)):
+        plan = [
+            (raw_ref.at[c, :, near], side.at[c], peers[4]),
+            (raw_ref.at[c, bottom, near], above.at[c, :, beyond], peers[3]),
+            (raw_ref.at[c, top, near], below.at[c, :, beyond], peers[2]),
+            (raw_ref.at[c, bottom, main], above.at[c, :, main], peers[1]),
+            (raw_ref.at[c, top, main], below.at[c, :, main], peers[0]),
+        ]
+        return [
+            pltpu.make_async_remote_copy(
+                src_ref=source, dst_ref=target, send_sem=send_sem.at[i, c], recv_sem=recv_sem.at[i, c],
+                device_id=peer, device_id_type=MESH,
+            )
+            for i, (source, target, peer) in list(enumerate(plan))[only]
+        ]
+
+    for c in range(channels):
+        for copy in copies(c):
+            copy.start()
+
+    def row_band(c):
+        return split(tap(iota((height, height), 1) - iota((height, height), 0), spread_ref[0, c]))
+
+    def along_rows(c, high, low, x):
+        x_high, x_low = split(x)
+        both = dot(jnp.concatenate([high, low], axis=0), x_high)
+        return both[:height] + both[height:] + dot(high, x_low)
+
+    step = 2 * LANES
+
+    def own_rows(c, carry):
+        high, low = row_band(c)
+        for g in range(width // step):
+            cols = slice(g * step, (g + 1) * step)
+            tall[c, :, cols] = along_rows(c, high, low, raw_ref[c, :, cols])
+        return carry
+
+    lax.fori_loop(0, channels, own_rows, 0)
+
+    lane = iota((height, LANES), 1)
+    count = width // LANES
+
+    def along_cols(c, rows):
+        size = rows.stop - rows.start
+        source = iota((2 * LANES, LANES), 0)
+        source = jnp.where(source < LANES + LANES // 2, source, source - 2 * LANES)
+        high, low = split(tap(source - iota((2 * LANES, LANES), 1), spread_ref[1, c]))
+        band = jnp.concatenate([high, low], axis=1)
+        outer = tall[c, rows, width:]
+        for n in range(count):
+            if n:
+                before = tall[c, rows, (n - 1) * LANES : n * LANES]
+            else:
+                before = jnp.where(my_col > 0, outer, 0.0)
+            if n + 1 < count:
+                after = tall[c, rows, (n + 1) * LANES : (n + 2) * LANES]
+            else:
+                after = jnp.where(my_col + 1 < cols_n, outer, 0.0)
+            edge = jnp.where(lane[:size] < LANES // 2, after, before)
+            own = tall[c, rows, n * LANES : (n + 1) * LANES]
+            x_high, x_low = split(jnp.concatenate([own, edge], axis=1))
+            both = dot(x_high, band)
+            out_ref[c, rows, n * LANES : (n + 1) * LANES] = (
+                both[:, :LANES] + both[:, LANES:] + dot(x_low, high)
+            )
+
+    def inner(c, carry):
+        for copy in copies(c, slice(0, 1)):
+            copy.wait_recv()
+        high, low = row_band(c)
+        tall[c, :, width:] = along_rows(c, high, low, side[c])
+        along_cols(c, slice(REACH, height - REACH))
+        return carry
+
+    lax.fori_loop(0, channels, inner, 0)
+
+    def outer_rows(c, carry):
+        for copy in copies(c, slice(1, 5)):
+            copy.wait_recv()
+        part = iota((REACH, 3 * REACH), 1)
+        offset = part % REACH - iota((REACH, 3 * REACH), 0)
+        for halo, rows, shift, real in (
+            (above, slice(0, REACH), -REACH, my_row > 0),
+            (below, slice(height - REACH, height), REACH, my_row + 1 < rows_n),
+        ):
+            taps = tap(offset + shift, spread_ref[0, c])
+            taps = jnp.where(real, taps, 0.0)
+            high = taps.astype(BF16).astype(F32)
+            taps = jnp.where(part // REACH == 1, taps - high, high).astype(BF16)
+            x_high, x_low = split(halo[c])
+            tall[c, rows, :] += dot(taps, jnp.concatenate([x_high, x_high, x_low], axis=0))
+            along_cols(c, rows)
+        return carry
+
+    lax.fori_loop(0, channels, outer_rows, 0)
+    for c in range(channels):
+        for copy in copies(c):
+            copy.wait_send()
+
+
+def smooth(spread, raw, rows_n, cols_n):
+    channels, height, width = raw.shape
+    vmem = pl.BlockSpec(memory_space=pltpu.VMEM)
     return pl.pallas_call(
-        smooth_kernel,
+        functools.partial(smooth_kernel, rows_n, cols_n),
         name="smooth",
-        grid=(channels,),
-        out_shape=jax.ShapeDtypeStruct((channels, TILE_ROWS, TILE_COLS), F32),
-        in_specs=[
-            pl.BlockSpec(memory_space=pltpu.SMEM),
-            block(TILE_ROWS, TILE_COLS),
-            block(REACH, TILE_COLS),
-            block(REACH, TILE_COLS),
-            block(tall, LANES),
+        out_shape=jax.ShapeDtypeStruct(raw.shape, F32),
+        in_specs=[pl.BlockSpec(memory_space=pltpu.SMEM), vmem],
+        out_specs=vmem,
+        scratch_shapes=[
+            pltpu.VMEM((channels, height, width + LANES), F32),
+            pltpu.VMEM((channels, height, LANES), F32),
+            pltpu.VMEM((channels, REACH, width + LANES), F32),
+            pltpu.VMEM((channels, REACH, width + LANES), F32),
+            pltpu.SemaphoreType.DMA((5, channels)),
+            pltpu.SemaphoreType.DMA((5, channels)),
         ],
-        out_specs=block(TILE_ROWS, TILE_COLS),
-        scratch_shapes=[
-            pltpu.VMEM((tall, TILE_COLS + LANES), F32),
-            pltpu.VMEM((TILE_ROWS, TILE_COLS + LANES), F32),
-        ],
-    )(spread, raw, up, down, side)
-
-
-def neighbours(value, axis, dim, width):
-    count, length = lax.axis_size(axis), value.shape[dim]
-    up = [(i, i + 1) for i in range(count - 1)]
-    down = [(j, i) for i, j in up]
-    last = lax.slice_in_dim(value, length - width, length, axis=dim)
-    first = lax.slice_in_dim(value, 0, width, axis=dim)
-    return lax.ppermute(last, axis, up), lax.ppermute(first, axis, down)
+        compiler_params=pltpu.CompilerParams(
+            collective_id=1, has_side_effects=True, vmem_limit_bytes=24 << 20
+        ),
+    )(spread, raw)
 
 
 def shards(cell_index, weights, block_tile, spread):
     rows_n, cols_n = lax.axis_size("row"), lax.axis_size("col")
     cells, points = exchange(cell_index, weights, block_tile, rows_n, cols_n)
     raw = scatter(cells, points)
-    up, down = neighbours(raw, "row", 1, REACH)
-    edges = jnp.concatenate(
-        [
-            jnp.concatenate([a[:, :, :REACH], a[:, :, -REACH:]], axis=2)
-            for a in (up, raw, down)
-        ],
-        axis=1,
-    )
-    left, right = neighbours(edges, "col", 2, REACH)
-    middle = jnp.zeros(edges.shape[:2] + (LANES - 2 * REACH,), F32)
-    side = jnp.concatenate([right, middle, left], axis=2)
-    return smooth(spread, raw, up, down, side)
+    return smooth(spread, raw, rows_n, cols_n)
 
 
 def solution(mesh):

time: 91.4 us -> 62.5 us (0.68)
  starting transfers between devices: 25.5 us -> 0 us
  waiting for transfers between devices: 1.91 us -> 0 us
  other arithmetic: 1.35 us -> 0 us
    ppermute x4 -> x0, starting transfers between devices: 25.5 us -> none  [neighbours(): return (lax.ppermute(last, axis, up), lax.ppermute(first, axis, down))]
    pallas_call x1, Pallas kernels: 8.11 us -> 13.7 us  [smooth(): pl.pallas_call(functools.partial(smooth_kernel, rows_n, cols_n), name='sm...]
    unnamed x4 -> x9, local copies, waits for them, and re-layouts: 0.01 us -> 4.15 us
    pallas_call x1, Pallas kernels: 19.8 us -> 15.9 us  [scatter(): pl.pallas_call(scatter_kernel, name='scatter', out_shape=jax.ShapeDtypeSt...]
    slice x7 -> x0, local copies, waits for them, and re-layouts: 2.98 us -> none  [the longest x4 1.73 us: shards(): a[:, :, :REACH]]
    ppermute x4 -> x0, waiting for transfers between devices: 1.91 us -> none  [neighbours(): return (lax.ppermute(last, axis, up), lax.ppermute(first, axis, down))]
    pallas_call x1, Pallas kernels: 29.4 us -> 27.9 us  [exchange(): pl.pallas_call(functools.partial(exchange_kernel, rows_n, cols_n), name='...]
    concatenate x4 -> x0, other arithmetic: 1.35 us -> none  [the longest x1 1.05 us: shards(): side = jnp.concatenate([right, middle, left], axis=2)]
  transfers between devices with their start and end apart: 4 -> 0, of which waited for: 2 -> 0; matrix products, arithmetic and copies ran while one was open for 3% -> 0% of each run, Pallas kernels for 0% -> 0%
where the time goes in v2:
time: 62.5 us; the launch traced here: 61.7 us
  Pallas kernels  57.5 us (92%)
  local copies, waits for them, and re-layouts  4.15 us (7%)
    pallas_call x1, Pallas kernels, exchange(): pl.pallas_call(functools.partial(exchange_kernel, rows_n, cols_n), name='...  27.9 us
    pallas_call x1, Pallas kernels, scatter(): pl.pallas_call(scatter_kernel, name='scatter', out_shape=jax.ShapeDtypeSt...  15.9 us
    pallas_call x1, Pallas kernels, smooth(): pl.pallas_call(functools.partial(smooth_kernel, rows_n, cols_n), name='sm...  13.7 us
    unnamed x9, local copies, waits for them, and re-layouts  4.15 us

profile of v2, /device:TPU:69, one launch (start us, length us, event | category | flops | bytes accessed | tf_op | source)
XLA Modules:
  0.0 61.7 jit_solution(14629768658907008419)
XLA Ops:
  0.0 0.0 copy-start
  0.0 0.8 %copy-done = bf16[32,512]{1,0:T(8,128)(2,1)S(1)} copy-done((bf16[32,512]{1,0:T(8,128)(2,1)S(1)}, bf16[32,512]{1,0:T(8,128)(2,1)}, u32[]{:S(2)}) %copy-start) | copy-done | bytes 32792
  0.8 0.0 copy-start.1
  0.8 0.7 %copy-done.1 = s32[32,128]{1,0:T(8,128)S(1)} copy-done((s32[32,128]{1,0:T(8,128)S(1)}, s32[32,128]{1,0:T(8,128)}, u32[]{:S(2)}) %copy-start.1) | copy-done | bytes 16408
  1.5 0.0 copy-start.3
  1.5 0.7 %copy-done.3 = s32[32]{0:T(128)S(1)} copy-done((s32[32]{0:T(128)S(1)}, s32[32]{0:T(128)}, u32[]{:S(2)}) %copy-start.3) | copy-done | bytes 152
  2.1 27.9 %exchange.1 = (s32[32,3,128]{2,1,0:T(4,128)S(1)}, bf16[32,12,128]{2,1,0:T(8,128)(2,1)S(1)}) custom-call(s32[32,128]{1,0:T(8,128)S(1)} %copy-done.1, bf16[32,512]{1,0:T(8,128)(2,1)S(1)} %copy-done, s32[1,32]{1,0:T(1,128)S(1)} %bitcast.1), custom_call_target="tpu_custom_call" | custom-call | tf_op jit(solution)/shard_map/exchange/pallas_call | solution.py:144
  30.1 0.0 copy-start.2
  30.1 15.9 %scatter.1.raw_ref = f32[4,256,1024]{2,1,0:T(8,128)S(1)} custom-call(s32[32,3,128]{2,1,0:T(4,128)S(1)} %get-tuple-element.7.cells_ref, bf16[32,12,128]{2,1,0:T(8,128)(2,1)S(1)} %get-tuple-element.8.weights_ref), custom_call_target="tpu_custom_call" | custom-call | flops 8053063680 | bytes 4194304 | tf_op jit(solution)/shard_map/scatter/pallas_call | solution.py:240
  46.0 0.0 copy-done.2
  46.0 13.7 %smooth.1 = f32[4,256,1024]{2,1,0:T(8,128)S(1)} custom-call(f32[2,4]{1,0:T(2,128)S(1)} %copy-done.2, f32[4,256,1024]{2,1,0:T(8,128)S(1)} %scatter.1.raw_ref), custom_call_target="tpu_custom_call" | custom-call | tf_op jit(solution)/shard_map/smooth/pallas_call | solution.py:401
  59.7 2.0 %copy.6 = f32[4,256,1024]{2,1,0:T(8,128)} copy(f32[4,256,1024]{2,1,0:T(8,128)S(1)} %smooth.1) | data formatting | bytes 8388608
Async XLA Ops:
  0.0 0.8 %copy-start = (bf16[32,512]{1,0:T(8,128)(2,1)S(1)}, bf16[32,512]{1,0:T(8,128)(2,1)}, u32[]{:S(2)}) copy-start(bf16[32,512]{1,0:T(8,128)(2,1)} %weight_ref.1) | copy-start | bytes 98308
  0.8 0.7 %copy-start.1 = (s32[32,128]{1,0:T(8,128)S(1)}, s32[32,128]{1,0:T(8,128)}, u32[]{:S(2)}) copy-start(s32[32,128]{1,0:T(8,128)} %cell_ref.1) | copy-start | bytes 49156
  1.5 0.7 %copy-start.3 = (s32[32]{0:T(128)S(1)}, s32[32]{0:T(128)}, u32[]{:S(2)}) copy-start(s32[32]{0:T(128)} %param.6) | copy-start | bytes 388
  30.1 15.9 %copy-start.2 = (f32[2,4]{1,0:T(2,128)S(1)}, f32[2,4]{1,0:T(2,128)}, u32[]{:S(2)}) copy-start(f32[2,4]{1,0:T(2,128)} %spread_ref.1) | copy-start | bytes 100

commit v3 on v2

--- a/solution.py
+++ b/solution.py
@@ -13,6 +13,7 @@
 CAPACITY = 3
 LANES = 128
 WINDOW = 80
+UNROLL = 4
 MESH = pl.DeviceIdType.MESH
 F32 = jnp.float32
 BF16 = jnp.bfloat16
@@ -23,9 +24,18 @@
 
 
 def exchange_kernel(
-    rows_n, cols_n, cell_ref, weight_ref, tile_ref, cells_out, weights_out,
-    ranks, values, sorted_points, send_cells, send_weights, send_sem, recv_sem, local_sem
+    rows_n, cols_n, cell_hbm, weight_hbm, tile_hbm, cells_out, weights_out,
+    cell_ref, weight_ref, tile_ref, values, sorted_points, send_cells, send_weights,
+    send_sem, recv_sem, local_sem
 ):
+    loads = [
+        pltpu.make_async_copy(source, target, local_sem.at[2 + i])
+        for i, (source, target) in enumerate(
+            ((cell_hbm, cell_ref), (weight_hbm, weight_ref), (tile_hbm, tile_ref))
+        )
+    ]
+    for load in loads:
+        load.start()
     blocks, points = cell_ref.shape
     channels = weight_ref.shape[1] // points
     peers = rows_n * cols_n
@@ -49,6 +59,8 @@
             barrier, inc=1, device_id={"row": row, "col": col}, device_id_type=MESH
         )
 
+    for load in loads:
+        load.wait()
     cells = cell_ref[...]
     point_row = cells // TILE_COLS
     col = cells % TILE_COLS
@@ -148,17 +160,19 @@
             jax.ShapeDtypeStruct((peers, CAPACITY, points), jnp.int32),
             jax.ShapeDtypeStruct((peers, CAPACITY * channels, points), BF16),
         ),
-        in_specs=[vmem] * 3,
+        in_specs=[pl.BlockSpec(memory_space=pltpu.MemorySpace.HBM)] * 3,
         out_specs=(vmem, vmem),
         scratch_shapes=[
-            pltpu.VMEM((blocks, points), F32),
+            pltpu.VMEM(cell_index.shape, jnp.int32),
+            pltpu.VMEM(weights.shape, BF16),
+            pltpu.VMEM((1, blocks), jnp.int32),
             pltpu.VMEM((3 + channels, blocks, points), F32),
             pltpu.VMEM((blocks, 8, points), F32),
             pltpu.VMEM((peers, CAPACITY, points), jnp.int32),
             pltpu.VMEM((peers, CAPACITY * channels, points), BF16),
             pltpu.SemaphoreType.DMA((2, peers - 1)),
             pltpu.SemaphoreType.DMA((2, peers - 1)),
-            pltpu.SemaphoreType.DMA((2,)),
+            pltpu.SemaphoreType.DMA((5,)),
         ],
         compiler_params=pltpu.CompilerParams(collective_id=0, has_side_effects=True, vmem_limit_bytes=8 << 20),
     )(cell_index, weights, block_tile.reshape(1, -1))
@@ -176,22 +190,34 @@
     return jnp.transpose(wide)
 
 
-def scatter_kernel(cells_ref, weights_ref, raw_ref, rows_s, cols_s, weights_s, wide_s):
+def scatter_kernel(cells_ref, weights_ref, raw_ref, rows_s, cols_s, weights_s, wide_s, first_s, last_s):
     senders, slots, points = cells_ref.shape
     channels = weights_ref.shape[1] // slots
     quarter = points // 4
-    raw_ref[...] = jnp.zeros_like(raw_ref)
-    wide_s[...] = weights_ref[...].astype(F32)
-    cells = turned([cells_ref[:, k, :].astype(F32) for k in range(slots)], quarter).astype(jnp.int32)
-    rows_s[...] = cells // TILE_COLS
-    cols_s[...] = cells % TILE_COLS
-    for c in range(channels):
-        weights_s[c] = turned([wide_s[:, k * channels + c, :] for k in range(slots)], quarter)
     chunk_rows = 2
     chunks = quarter // chunk_rows
     span = 256
-
-    def chunk(j, carry):
+    wide_s[...] = weights_ref[...].astype(F32)
+    cells = turned([cells_ref[:, k, :].astype(F32) for k in range(slots)], quarter).astype(jnp.int32)
+    rows = cells >> (TILE_COLS.bit_length() - 1)
+    rows_s[...] = rows
+    cols_s[...] = cells & (TILE_COLS - 1)
+    for c in range(channels):
+        weights_s[c] = turned([wide_s[:, k * channels + c, :] for k in range(slots)], quarter)
+    low, high = rows[:quarter], rows[:quarter]
+    for k in range(1, slots):
+        low = jnp.minimum(low, rows[quarter * k : quarter * (k + 1)])
+        high = jnp.maximum(high, rows[quarter * k : quarter * (k + 1)])
+    low = jnp.min(low, axis=1, keepdims=True)
+    high = jnp.max(high, axis=1, keepdims=True)
+    for j in range(chunks):
+        lows = [low[chunk_rows * j + i, 0] for i in range(chunk_rows)]
+        highs = [high[chunk_rows * j + i, 0] for i in range(chunk_rows)]
+        first_s[j] = (functools.reduce(jnp.minimum, lows) >> 3) << 3
+        last_s[j] = functools.reduce(jnp.maximum, highs)
+    raw_ref[...] = jnp.zeros_like(raw_ref)
+
+    def window(j, low):
         def take(ref):
             return jnp.concatenate(
                 [
@@ -204,33 +230,39 @@
 
         row = take(rows_s)
         col = take(cols_s)
-        weight = [take(weights_s.at[c]) for c in range(channels)]
-        first = jnp.min(row) // 8 * 8
-        last = jnp.max(row)
         count = row.shape[1]
-
-        def window(low):
-            base = pl.multiple_of(jnp.minimum(low, TILE_ROWS - WINDOW), 8)
-            offset = jnp.where(row >= low, row - base, -1)
-            hot = iota((WINDOW, count), 0) == offset
-            left = jnp.concatenate(
-                [jnp.where(hot, weight[c], 0.0).astype(BF16) for c in range(channels)], axis=0
-            )
-            for g in range(TILE_COLS // span):
-                right = (iota((span, count), 0) == col - g * span).astype(F32).astype(BF16)
-                layer = lax.dot_general(
-                    left, right, (((1,), (1,)), ((), ())), preferred_element_type=F32
-                )
-                for c in range(channels):
-                    raw_ref[c, pl.ds(base, WINDOW), g * span : (g + 1) * span] += layer[
-                        c * WINDOW : (c + 1) * WINDOW
-                    ]
+        base = pl.multiple_of(jnp.minimum(low, TILE_ROWS - WINDOW), 8)
+        offset = jnp.where(row >= low, row - base, -1)
+        hot = iota((WINDOW, count), 0) == offset
+        left = jnp.concatenate(
+            [jnp.where(hot, take(weights_s.at[c]), 0.0).astype(BF16) for c in range(channels)],
+            axis=0,
+        )
+        for g in range(TILE_COLS // span):
+            right = (iota((span, count), 0) == col - g * span).astype(F32).astype(BF16)
+            layer = lax.dot_general(
+                left, right, (((1,), (1,)), ((), ())), preferred_element_type=F32
+            )
+            for c in range(channels):
+                raw_ref[c, pl.ds(base, WINDOW), g * span : (g + 1) * span] += layer[
+                    c * WINDOW : (c + 1) * WINDOW
+                ]
+
+    def common(j, carry):
+        window(j, first_s[j])
+        return carry
+
+    lax.fori_loop(0, chunks, common, 0, unroll=UNROLL)
+
+    def rest(j, carry):
+        def more(low):
+            window(j, low)
             return low + WINDOW
 
-        lax.while_loop(lambda low: low <= last, window, first)
+        lax.while_loop(lambda low: low <= last_s[j], more, first_s[j] + WINDOW)
         return carry
 
-    lax.fori_loop(0, chunks, chunk, 0)
+    lax.fori_loop(0, chunks, rest, 0)
 
 
 def scatter(cells, weights):
@@ -248,6 +280,8 @@
             pltpu.VMEM((LANES, LANES), jnp.int32),
             pltpu.VMEM((channels, LANES, LANES), F32),
             pltpu.VMEM((senders, slots * channels, points), F32),
+            pltpu.SMEM((points // 8,), jnp.int32),
+            pltpu.SMEM((points // 8,), jnp.int32),
         ],
         compiler_params=pltpu.CompilerParams(vmem_limit_bytes=16 << 20),
         cost_estimate=pl.CostEstimate(

time: 62.5 us -> 55.6 us (0.89)
  Pallas kernels: 57.5 us -> 50.5 us
    pallas_call x1, Pallas kernels: 15.9 us -> 10.2 us  [scatter(): pl.pallas_call(scatter_kernel, name='scatter', out_shape=jax.ShapeDtypeSt...]
    pallas_call x1, Pallas kernels: 13.7 us -> 12.4 us  [smooth(): pl.pallas_call(functools.partial(smooth_kernel, rows_n, cols_n), name='sm...]
where the time goes in v3:
time: 55.6 us; the launch traced here: 54.7 us
  Pallas kernels  50.5 us (91%)
  local copies, waits for them, and re-layouts  4.15 us (7%)
    pallas_call x1, Pallas kernels, exchange(): pl.pallas_call(functools.partial(exchange_kernel, rows_n, cols_n), name='...  27.9 us
    pallas_call x1, Pallas kernels, smooth(): pl.pallas_call(functools.partial(smooth_kernel, rows_n, cols_n), name='sm...  12.4 us
    pallas_call x1, Pallas kernels, scatter(): pl.pallas_call(scatter_kernel, name='scatter', out_shape=jax.ShapeDtypeSt...  10.2 us
    unnamed x9, local copies, waits for them, and re-layouts  4.15 us

profile of v3, /device:TPU:69, one launch (start us, length us, event | category | flops | bytes accessed | tf_op | source)
XLA Modules:
  0.0 54.7 jit_solution(10467564237127238973)
XLA Ops:
  0.0 0.0 copy-start
  0.0 0.8 %copy-done = bf16[32,512]{1,0:T(8,128)(2,1)S(1)} copy-done((bf16[32,512]{1,0:T(8,128)(2,1)S(1)}, bf16[32,512]{1,0:T(8,128)(2,1)}, u32[]{:S(2)}) %copy-start) | copy-done | bytes 32792
  0.8 0.0 copy-start.1
  0.8 0.7 %copy-done.1 = s32[32,128]{1,0:T(8,128)S(1)} copy-done((s32[32,128]{1,0:T(8,128)S(1)}, s32[32,128]{1,0:T(8,128)}, u32[]{:S(2)}) %copy-start.1) | copy-done | bytes 16408
  1.5 0.0 copy-start.3
  1.5 0.7 %copy-done.3 = s32[32]{0:T(128)S(1)} copy-done((s32[32]{0:T(128)S(1)}, s32[32]{0:T(128)}, u32[]{:S(2)}) %copy-start.3) | copy-done | bytes 152
  2.1 27.9 %exchange.1 = (s32[32,3,128]{2,1,0:T(4,128)S(1)}, bf16[32,12,128]{2,1,0:T(8,128)(2,1)S(1)}) custom-call(s32[32,128]{1,0:T(8,128)S(1)} %copy-done.1, bf16[32,512]{1,0:T(8,128)(2,1)S(1)} %copy-done, s32[1,32]{1,0:T(1,128)S(1)} %bitcast.1), custom_call_target="tpu_custom_call" | custom-call | tf_op jit(solution)/shard_map/exchange/pallas_call | solution.py:156
  30.1 0.0 copy-start.2
  30.1 10.2 %scatter.1.raw_ref = f32[4,256,1024]{2,1,0:T(8,128)S(1)} custom-call(s32[32,3,128]{2,1,0:T(4,128)S(1)} %get-tuple-element.7.cells_ref, bf16[32,12,128]{2,1,0:T(8,128)(2,1)S(1)} %get-tuple-element.8.weights_ref), custom_call_target="tpu_custom_call" | custom-call | flops 8053063680 | bytes 4194304 | tf_op jit(solution)/shard_map/scatter/pallas_call | solution.py:272
  40.3 0.0 copy-done.2
  40.3 12.4 %smooth.1 = f32[4,256,1024]{2,1,0:T(8,128)S(1)} custom-call(f32[2,4]{1,0:T(2,128)S(1)} %copy-done.2, f32[4,256,1024]{2,1,0:T(8,128)S(1)} %scatter.1.raw_ref), custom_call_target="tpu_custom_call" | custom-call | tf_op jit(solution)/shard_map/smooth/pallas_call | solution.py:435
  52.7 2.0 %copy.6 = f32[4,256,1024]{2,1,0:T(8,128)} copy(f32[4,256,1024]{2,1,0:T(8,128)S(1)} %smooth.1) | data formatting | bytes 8388608
Async XLA Ops:
  0.0 0.8 %copy-start = (bf16[32,512]{1,0:T(8,128)(2,1)S(1)}, bf16[32,512]{1,0:T(8,128)(2,1)}, u32[]{:S(2)}) copy-start(bf16[32,512]{1,0:T(8,128)(2,1)} %weight_hbm.1) | copy-start | bytes 98308
  0.8 0.7 %copy-start.1 = (s32[32,128]{1,0:T(8,128)S(1)}, s32[32,128]{1,0:T(8,128)}, u32[]{:S(2)}) copy-start(s32[32,128]{1,0:T(8,128)} %cell_hbm.1) | copy-start | bytes 49156
  1.5 0.7 %copy-start.3 = (s32[32]{0:T(128)S(1)}, s32[32]{0:T(128)}, u32[]{:S(2)}) copy-start(s32[32]{0:T(128)} %param.6) | copy-start | bytes 388
  30.1 10.2 %copy-start.2 = (f32[2,4]{1,0:T(2,128)S(1)}, f32[2,4]{1,0:T(2,128)}, u32[]{:S(2)}) copy-start(f32[2,4]{1,0:T(2,128)} %spread_ref.1) | copy-start | bytes 100

commit v4 on v3

v4 whole, which is shorter than its diff:
```python
import functools

import jax
import jax.numpy as jnp
from jax import lax
from jax.experimental import pallas as pl
from jax.experimental.pallas import tpu as pltpu
from jax.sharding import PartitionSpec as P

REACH = 16
TILE_ROWS = 256
TILE_COLS = 1024
CAPACITY = 3
LANES = 128
WINDOW = 64
LEAD = 24
CHUNK_ROWS = 2
UNROLL = 5
MESH = pl.DeviceIdType.MESH
F32 = jnp.float32
BF16 = jnp.bfloat16


def iota(shape, dim):
    return lax.broadcasted_iota(jnp.int32, shape, dim)


def in_hbm(value):
    return pltpu.with_memory_space_constraint(value, pltpu.MemorySpace.HBM)


def dot(a, b):
    return lax.dot_general(a, b, (((1,), (0,)), ((), ())), preferred_element_type=F32)


def exchange_kernel(
    rows_n, cols_n, cell_hbm, weight_hbm, tile_hbm, cells_out, weights_out,
    cell_ref, weight_ref, tile_ref, values, keys_t, sorted_points, send_cells, send_weights,
    send_sem, recv_sem, local_sem
):
    loads = [
        pltpu.make_async_copy(source, target, local_sem.at[2 + i])
        for i, (source, target) in enumerate(
            ((cell_hbm, cell_ref), (weight_hbm, weight_ref), (tile_hbm, tile_ref))
        )
    ]
    for load in loads:
        load.start()
    blocks, points = cell_ref.shape
    channels = weight_ref.shape[1] // points
    peers = rows_n * cols_n
    my_row, my_col = lax.axis_index("row"), lax.axis_index("col")
    me = my_row * cols_n + my_col

    offsets = []
    for distance in range(rows_n // 2, 0, -1):
        for step in (distance, rows_n - distance):
            if step not in [o[0] for o in offsets]:
                offsets += [(step, c) for c in range(cols_n)]
    offsets += [(0, c) for c in range(1, cols_n)]

    barrier = pltpu.get_barrier_semaphore()
    targets = []
    for step, turn in offsets:
        row = lax.rem(my_row + step, rows_n)
        col = lax.rem(my_col + turn, cols_n)
        targets.append((row, col))
        pl.semaphore_signal(
            barrier, inc=1, device_id={"row": row, "col": col}, device_id_type=MESH
        )

    for load in loads:
        load.wait()
    tile = tile_ref[...]
    square = (blocks, blocks)
    tile_down = jnp.sum(
        jnp.where(iota(square, 0) == iota(square, 1), tile, 0), axis=1, keepdims=True
    )
    earlier = (tile_down == tile) & (iota(square, 0) < iota(square, 1))
    turn_of = jnp.sum(earlier.astype(jnp.int32), axis=0, keepdims=True)
    cells = cell_ref[...]
    within = cells & (TILE_COLS - 1)
    parts = [weight_ref[:, c * points : (c + 1) * points] for c in range(channels)] + [
        part.astype(F32).astype(BF16)
        for part in (
            cells >> (TILE_COLS.bit_length() - 1),
            within >> (LANES.bit_length() - 1),
            within & (LANES - 1),
        )
    ]
    group = CAPACITY * points
    ramp = (iota((1, points), 1) * (TILE_ROWS // points)).astype(F32)
    keys = []
    for k in range(CAPACITY):
        chosen = ((iota((peers, blocks), 0) == tile) & (turn_of == k)).astype(F32)
        empty = jnp.sum(chosen, axis=1, keepdims=True) < 0.5
        placed = dot(chosen.astype(BF16), jnp.concatenate(parts, axis=1))
        for v in range(channels + 3):
            piece = placed[:, v * points : (v + 1) * points]
            if v == channels:
                piece = jnp.where(empty, ramp, piece)
                keys.append(piece * 512.0 + (iota((1, points), 1) + k * points).astype(F32))
            values[v, :, k * points : (k + 1) * points] = piece
    pad = jnp.zeros((points - peers, points), F32)
    keys_t[...] = jnp.concatenate(
        [jnp.transpose(jnp.concatenate([key, pad], axis=0)) for key in keys], axis=0
    )
    keys = jnp.concatenate(keys, axis=1)
    quarter = points // 4
    chunks = quarter // CHUNK_ROWS
    share = group // chunks
    for t in range(peers):
        less = (keys_t[:, t : t + 1] < keys[t : t + 1, :]).astype(F32)
        rank = jnp.sum(less, axis=0, keepdims=True).astype(jnp.int32)
        chunk = (rank * (65536 // share + 1)) >> 16
        inside = rank - chunk * share
        third = (inside * (512 // CAPACITY + 1)) >> 9
        lane = (inside - third * CAPACITY) * points
        lane = lane + (third & 3) * quarter + chunk * CHUNK_ROWS + (third >> 2)
        hot = (iota((group, group), 0) == lane).astype(F32).astype(BF16)
        piece = jnp.concatenate(
            [values[v, t : t + 1, :] for v in range(channels + 3)] + [jnp.zeros((1, group), F32)],
            axis=0,
        ).astype(BF16)
        sorted_points[t] = lax.dot_general(
            piece, hot, (((1,), (1,)), ((), ())), preferred_element_type=F32
        )
    for k in range(CAPACITY):
        part = slice(k * points, (k + 1) * points)
        cell = sorted_points[:, channels, part] * TILE_COLS
        cell = cell + sorted_points[:, channels + 1, part] * LANES + sorted_points[:, channels + 2, part]
        send_cells[:, k, :] = cell.astype(jnp.int32)
        for c in range(channels):
            send_weights[:, k * channels + c, :] = sorted_points[:, c, part].astype(BF16)

    own = [
        pltpu.make_async_copy(send_cells.at[me], cells_out.at[me], local_sem.at[0]),
        pltpu.make_async_copy(send_weights.at[me], weights_out.at[me], local_sem.at[1]),
    ]
    pl.semaphore_wait(barrier, peers - 1)
    copies = []
    for i, (row, col) in enumerate(targets):
        peer = row * cols_n + col
        for a, (source, out) in enumerate(
            ((send_cells, cells_out), (send_weights, weights_out))
        ):
            copy = pltpu.make_async_remote_copy(
                src_ref=source.at[peer],
                dst_ref=out.at[me],
                send_sem=send_sem.at[a, i],
                recv_sem=recv_sem.at[a, i],
                device_id={"row": row, "col": col},
                device_id_type=MESH,
            )
            copy.start()
            copies.append(copy)
    for copy in own:
        copy.start()
    for copy in own:
        copy.wait()
    for copy in copies:
        copy.wait_recv()
    for copy in copies:
        copy.wait_send()


def exchange(cell_index, weights, block_tile, rows_n, cols_n):
    blocks, points = cell_index.shape
    channels = weights.shape[1] // points
    peers = rows_n * cols_n
    vmem = pl.BlockSpec(memory_space=pltpu.VMEM)
    return pl.pallas_call(
        functools.partial(exchange_kernel, rows_n, cols_n),
        name="exchange",
        out_shape=(
            jax.ShapeDtypeStruct((peers, CAPACITY, points), jnp.int32),
            jax.ShapeDtypeStruct((peers, CAPACITY * channels, points), BF16),
        ),
        in_specs=[pl.BlockSpec(memory_space=pltpu.MemorySpace.HBM)] * 3,
        out_specs=(vmem, vmem),
        scratch_shapes=[
            pltpu.VMEM(cell_index.shape, jnp.int32),
            pltpu.VMEM(weights.shape, BF16),
            pltpu.VMEM((1, blocks), jnp.int32),
            pltpu.VMEM((3 + channels, peers, CAPACITY * points), F32),
            pltpu.VMEM((CAPACITY * points, points), F32),
            pltpu.VMEM((peers, 8, CAPACITY * points), F32),
            pltpu.VMEM((peers, CAPACITY, points), jnp.int32),
            pltpu.VMEM((peers, CAPACITY * channels, points), BF16),
            pltpu.SemaphoreType.DMA((2, peers - 1)),
            pltpu.SemaphoreType.DMA((2, peers - 1)),
            pltpu.SemaphoreType.DMA((5,)),
        ],
        compiler_params=pltpu.CompilerParams(collective_id=0, has_side_effects=True, vmem_limit_bytes=8 << 20),
    )(*(in_hbm(x) for x in (cell_index, weights, block_tile.reshape(1, -1))))


def turned(slots, quarter):
    wide = jnp.concatenate(
        [
            jnp.concatenate([s[:, v * quarter : (v + 1) * quarter] for v in range(4)], axis=0)
            for s in slots
        ]
        + [jnp.zeros((LANES, LANES - len(slots) * quarter), F32)],
        axis=1,
    )
    return jnp.transpose(wide)


def add_window(raw_ref, rows_s, cols_s, weights_s, j, low, stop, base):
    channels = raw_ref.shape[0]
    quarter = LANES // 4
    span = 256

    def take(ref):
        return jnp.concatenate(
            [
                ref[pl.ds(quarter * k + CHUNK_ROWS * j + i, 1), :]
                for k in range(CAPACITY)
                for i in range(CHUNK_ROWS)
            ],
            axis=1,
        )

    row = take(rows_s)
    col = take(cols_s)
    count = row.shape[1]
    offset = jnp.where((row >= low) & (row < stop), row - base, -1)
    hot = iota((WINDOW, count), 0) == offset
    left = jnp.concatenate(
        [jnp.where(hot, take(weights_s.at[c]), 0.0).astype(BF16) for c in range(channels)],
        axis=0,
    )
    for g in range(TILE_COLS // span):
        right = (iota((span, count), 0) == col - g * span).astype(F32).astype(BF16)
        layer = lax.dot_general(
            left, right, (((1,), (1,)), ((), ())), preferred_element_type=F32
        )
        for c in range(channels):
            raw_ref[c, pl.ds(base, WINDOW), g * span : (g + 1) * span] += layer[
                c * WINDOW : (c + 1) * WINDOW
            ]


def inner_chunks(chunks):
    tall = TILE_ROWS // chunks
    inner = [
        j
        for j in range(chunks)
        if tall * j - LEAD >= REACH and tall * j - LEAD + WINDOW <= TILE_ROWS - REACH
    ]
    return tall, inner[0], inner[-1] + 1


def outer_kernel(
    cells_ref, weights_ref, raw_ref, rows_s, cols_s, weights_s, wide_s, first_s, last_s, next_s
):
    senders, slots, points = cells_ref.shape
    channels = weights_ref.shape[1] // slots
    quarter = points // 4
    chunks = quarter // CHUNK_ROWS
    wide_s[...] = weights_ref[...].astype(F32)
    cells = turned([cells_ref[:, k, :].astype(F32) for k in range(slots)], quarter).astype(jnp.int32)
    rows = cells >> (TILE_COLS.bit_length() - 1)
    rows_s[...] = rows
    cols_s[...] = cells & (TILE_COLS - 1)
    for c in range(channels):
        weights_s[c] = turned([wide_s[:, k * channels + c, :] for k in range(slots)], quarter)
    low, high = rows[:quarter], rows[:quarter]
    for k in range(1, slots):
        low = jnp.minimum(low, rows[quarter * k : quarter * (k + 1)])
        high = jnp.maximum(high, rows[quarter * k : quarter * (k + 1)])
    low = jnp.min(low, axis=1, keepdims=True)
    high = jnp.max(high, axis=1, keepdims=True)
    tall, begin, end = inner_chunks(chunks)
    for j in range(chunks):
        lows = [low[CHUNK_ROWS * j + i, 0] for i in range(CHUNK_ROWS)]
        highs = [high[CHUNK_ROWS * j + i, 0] for i in range(CHUNK_ROWS)]
        first = (functools.reduce(jnp.minimum, lows) >> 3) << 3
        done = tall * j - LEAD if begin <= j < end else first
        first_s[j] = first
        last_s[j] = functools.reduce(jnp.maximum, highs)
        next_s[j] = jnp.where(first < done, first, done + WINDOW)
    raw_ref[...] = jnp.zeros_like(raw_ref)

    def add(j, low, stop):
        base = pl.multiple_of(jnp.minimum(low, TILE_ROWS - WINDOW), 8)
        add_window(raw_ref, rows_s, cols_s, weights_s, j, low, stop, base)

    def common(i, carry):
        j = jnp.where(i < begin, i, i + end - begin)
        low = first_s[j]
        add(j, low, low + WINDOW)
        return carry

    lax.fori_loop(0, chunks - (end - begin), common, 0, unroll=True)

    def rest(j, carry):
        done = jnp.where((j >= begin) & (j < end), tall * j - LEAD, first_s[j])

        def more(low):
            stop = jnp.where(low < done, jnp.minimum(low + WINDOW, done), low + WINDOW)
            add(j, low, stop)
            return jnp.where(stop == done, done + WINDOW, stop)

        lax.while_loop(lambda low: low <= last_s[j], more, next_s[j])
        return carry

    lax.fori_loop(0, chunks, rest, 0)


def outer(cells, weights):
    senders, slots, points = cells.shape
    channels = weights.shape[1] // slots
    vmem = pl.BlockSpec(memory_space=pltpu.VMEM)
    turns = points // 4 // CHUNK_ROWS
    return pl.pallas_call(
        outer_kernel,
        name="outer",
        out_shape=(
            jax.ShapeDtypeStruct((channels, TILE_ROWS, TILE_COLS), F32),
            jax.ShapeDtypeStruct((LANES, LANES), jnp.int32),
            jax.ShapeDtypeStruct((LANES, LANES), jnp.int32),
            jax.ShapeDtypeStruct((channels, LANES, LANES), F32),
        ),
        in_specs=[vmem] * 2,
        out_specs=(vmem,) * 4,
        scratch_shapes=[pltpu.VMEM((senders, slots * channels, points), F32)]
        + [pltpu.SMEM((turns,), jnp.int32)] * 3,
        compiler_params=pltpu.CompilerParams(vmem_limit_bytes=16 << 20),
    )(cells, weights)


def split(value):
    high = value.astype(BF16)
    return high, (value - high.astype(F32)).astype(BF16)


def tap(offset, width):
    near = jnp.abs(offset) <= REACH
    far = offset.astype(F32)
    return jnp.where(near, jnp.exp(-(far * far) / (2.0 * width * width)), 0.0)


def col_band(width):
    source = iota((2 * LANES, LANES), 0)
    source = jnp.where(source < LANES + LANES // 2, source, source - 2 * LANES)
    high, low = split(tap(source - iota((2 * LANES, LANES), 1), width))
    return jnp.concatenate([high, low], axis=1), high


def along_cols(block, beyond, count, my_col, cols_n, band, high, store):
    for n in range(count):
        own = block(n)
        before = block(n - 1) if n else jnp.where(my_col > 0, beyond, 0.0)
        after = block(n + 1) if n + 1 < count else jnp.where(my_col + 1 < cols_n, beyond, 0.0)
        edge = jnp.where(iota(own.shape, 1) < LANES // 2, after, before)
        x_high, x_low = split(jnp.concatenate([own, edge], axis=1))
        both = dot(x_high, band)
        store(n, both[:, :LANES] + both[:, LANES:] + dot(x_low, high))


def inner_kernel(
    rows_n, cols_n, spread_hbm, raw_ref, rows_s, cols_s, weights_s,
    out_ref, tall, above, below, spread_ref, acc, side, send_sem, recv_sem, load_sem
):
    channels, height, width = raw_ref.shape
    my_row, my_col = lax.axis_index("row"), lax.axis_index("col")
    other = lax.rem(my_col + 1, cols_n)
    prev = lax.rem(my_row + rows_n - 1, rows_n)
    following = lax.rem(my_row + 1, rows_n)

    def at(row, col):
        return {"row": row, "col": col}

    barrier = pltpu.get_barrier_semaphore()
    peers = [at(prev, my_col), at(following, my_col), at(prev, other), at(following, other), at(my_row, other)]
    for peer in peers:
        pl.semaphore_signal(barrier, inc=1, device_id=peer, device_id_type=MESH)
    pl.semaphore_wait(barrier, len(peers))
    near = pl.ds(pl.multiple_of((1 - my_col) * (width - LANES), LANES), LANES)
    main = pl.ds(0, width)
    beyond = pl.ds(width, LANES)
    top, bottom = pl.ds(0, REACH), pl.ds(height - REACH, REACH)

    def remote(i, source, target, peer):
        return pltpu.make_async_remote_copy(
            src_ref=source, dst_ref=target, send_sem=send_sem.at[i], recv_sem=recv_sem.at[i],
            device_id=peer, device_id_type=MESH,
        )

    halo = [
        remote(0, raw_ref.at[:, bottom, main], above.at[:, :, main], peers[1]),
        remote(1, raw_ref.at[:, top, main], below.at[:, :, main], peers[0]),
        remote(2, raw_ref.at[:, bottom, near], above.at[:, :, beyond], peers[3]),
        remote(3, raw_ref.at[:, top, near], below.at[:, :, beyond], peers[2]),
    ]
    for copy in halo:
        copy.start()
    load = pltpu.make_async_copy(spread_hbm, spread_ref, load_sem)
    load.start()

    acc[...] = raw_ref[...]
    tall_rows, begin, end = inner_chunks(LANES // 4 // CHUNK_ROWS)

    def chunk(j, carry):
        base = pl.multiple_of(tall_rows * j - LEAD, 8)
        add_window(acc, rows_s, cols_s, weights_s, j, base, base + WINDOW, base)
        return carry

    lax.fori_loop(begin, end, chunk, 0, unroll=UNROLL)

    def row_band(c):
        return split(tap(iota((height, height), 1) - iota((height, height), 0), spread_ref[0, c]))

    def along_rows(high, low, x):
        x_high, x_low = split(x)
        both = dot(jnp.concatenate([high, low], axis=0), x_high)
        return both[:height] + both[height:] + dot(high, x_low)

    step = 2 * LANES
    load.wait()

    def own_rows(c, carry):
        high, low = row_band(c)
        for g in range(width // step):
            cols = slice(g * step, (g + 1) * step)
            tall[c, :, cols] = along_rows(high, low, acc[c, :, cols])
        return carry

    own_rows(0, 0)
    partner = remote(4, acc.at[:, :, near], side, peers[4])
    partner.start()
    lax.fori_loop(1, channels, own_rows, 0)
    partner.wait_recv()

    def inner_cols(c, carry):
        high, low = row_band(c)
        tall[c, :, width:] = along_rows(high, low, side[c])
        band, high = col_band(spread_ref[1, c])
        rows = slice(REACH, height - REACH)

        def block(n):
            return tall[c, rows, n * LANES : (n + 1) * LANES]

        def store(n, value):
            out_ref[c, rows, n * LANES : (n + 1) * LANES] = value

        count = width // LANES
        along_cols(block, block(count), count, my_col, cols_n, band, high, store)
        return carry

    lax.fori_loop(0, channels, inner_cols, 0)
    for copy in halo:
        copy.wait_recv()
    for copy in halo + [partner]:
        copy.wait_send()


def inner(spread, raw, rows, cols, weights, rows_n, cols_n):
    channels, height, width = raw.shape
    vmem = pl.BlockSpec(memory_space=pltpu.VMEM)
    return pl.pallas_call(
        functools.partial(inner_kernel, rows_n, cols_n),
        name="inner",
        out_shape=(
            jax.ShapeDtypeStruct(raw.shape, F32),
            jax.ShapeDtypeStruct((channels, height, width + LANES), F32),
            jax.ShapeDtypeStruct((channels, REACH, width + LANES), F32),
            jax.ShapeDtypeStruct((channels, REACH, width + LANES), F32),
        ),
        in_specs=[pl.BlockSpec(memory_space=pltpu.MemorySpace.HBM)] + [vmem] * 4,
        out_specs=(vmem,) * 4,
        scratch_shapes=[
            pltpu.SMEM(spread.shape, F32),
            pltpu.VMEM(raw.shape, F32),
            pltpu.VMEM((channels, height, LANES), F32),
            pltpu.SemaphoreType.DMA((5,)),
            pltpu.SemaphoreType.DMA((5,)),
            pltpu.SemaphoreType.DMA,
        ],
        compiler_params=pltpu.CompilerParams(
            collective_id=1, has_side_effects=True, vmem_limit_bytes=24 << 20
        ),
    )(in_hbm(spread), raw, rows, cols, weights)


def finish_kernel(
    rows_n, cols_n, spread_ref, done_ref, tall, above, below, out_ref, edge, inner_sem, edge_sem
):
    channels, height, width = done_ref.shape
    my_row, my_col = lax.axis_index("row"), lax.axis_index("col")
    copies = []
    for c in range(channels):
        rows = pl.ds(REACH, height - 2 * REACH)
        copies.append(
            pltpu.make_async_copy(done_ref.at[c, rows], out_ref.at[c, rows], inner_sem.at[c])
        )
        copies[-1].start()
    shape = (REACH, 3 * REACH)
    part = iota(shape, 1) >> (REACH.bit_length() - 1)
    offset = (iota(shape, 1) & (REACH - 1)) - iota(shape, 0)
    for c in range(channels):
        sides = []
        for halo, start, shift, real in (
            (above, 0, -REACH, my_row > 0),
            (below, height - REACH, REACH, my_row + 1 < rows_n),
        ):
            taps = jnp.where(real, tap(offset + shift, spread_ref[0, c]), 0.0)
            high = taps.astype(BF16).astype(F32)
            taps = jnp.where(part == 1, taps - high, high).astype(BF16)
            x_high, x_low = split(halo[c])
            sides.append(
                tall[c, start : start + REACH, :]
                + dot(taps, jnp.concatenate([x_high, x_high, x_low], axis=0))
            )
        rows = jnp.concatenate(sides, axis=0)
        band, high = col_band(spread_ref[1, c])

        def block(n):
            return rows[:, n * LANES : (n + 1) * LANES]

        def store(n, value):
            edge[c, :, n * LANES : (n + 1) * LANES] = value

        count = width // LANES
        along_cols(block, block(count), count, my_col, cols_n, band, high, store)
        for i, start in enumerate((0, height - REACH)):
            copies.append(
                pltpu.make_async_copy(
                    edge.at[c, pl.ds(i * REACH, REACH)],
                    out_ref.at[c, pl.ds(start, REACH)],
                    edge_sem.at[i, c],
                )
            )
            copies[-1].start()
    for copy in copies:
        copy.wait()


def finish(spread, done, tall, above, below, rows_n, cols_n):
    channels, height, width = done.shape
    vmem = pl.BlockSpec(memory_space=pltpu.VMEM)
    return pl.pallas_call(
        functools.partial(finish_kernel, rows_n, cols_n),
        name="finish",
        out_shape=jax.ShapeDtypeStruct(done.shape, F32),
        in_specs=[pl.BlockSpec(memory_space=pltpu.SMEM)] + [vmem] * 4,
        out_specs=pl.BlockSpec(memory_space=pltpu.MemorySpace.HBM),
        scratch_shapes=[
            pltpu.VMEM((channels, 2 * REACH, width), F32),
            pltpu.SemaphoreType.DMA((channels,)),
            pltpu.SemaphoreType.DMA((2, channels)),
        ],
        compiler_params=pltpu.CompilerParams(vmem_limit_bytes=12 << 20),
    )(spread, done, tall, above, below)


def shards(cell_index, weights, block_tile, spread):
    rows_n, cols_n = lax.axis_size("row"), lax.axis_size("col")
    cells, points = exchange(cell_index, weights, block_tile, rows_n, cols_n)
    raw, rows, cols, values = outer(cells, points)
    done = inner(spread, raw, rows, cols, values, rows_n, cols_n)
    return finish(spread, *done, rows_n, cols_n)


def solution(mesh):
    return jax.shard_map(
        shards,
        mesh=mesh,
        in_specs=(
            P(("groups", "row", "col"), None),
            P(("groups", "row", "col"), None),
            P(("groups", "row", "col")),
            P(),
        ),
        out_specs=P(None, ("groups", "row"), "col"),
        check_vma=False,
    )
```

time: 55.6 us -> 48.5 us (0.87); the launches traced: 54.7 us -> 48.4 us
  local copies, waits for them, and re-layouts: 4.15 us -> 0.01 us
  Pallas kernels: 50.5 us -> 48.2 us
    unnamed x9 -> x2, local copies, waits for them, and re-layouts: 4.15 us -> 0.01 us
    pallas_call x2 -> x3, Pallas kernels: 22.6 us -> 19.4 us  [the longest x1 12.9 us: inner(): pl.pallas_call(functools.partial(inner_kernel, rows_n, cols_n), name='inn...]
    pallas_call x1, Pallas kernels: 27.9 us -> 28.8 us  [exchange(): pl.pallas_call(functools.partial(exchange_kernel, rows_n, cols_n), name='...]
where the time goes in v4:
time: 48.5 us; the launch traced here: 48.4 us
  Pallas kernels  48.2 us (99%)
    pallas_call x1, Pallas kernels, exchange(): pl.pallas_call(functools.partial(exchange_kernel, rows_n, cols_n), name='...  28.8 us
    pallas_call x1, Pallas kernels, inner(): pl.pallas_call(functools.partial(inner_kernel, rows_n, cols_n), name='inn...  12.9 us
    pallas_call x1, Pallas kernels, outer(): pl.pallas_call(outer_kernel, name='outer', out_shape=(jax.ShapeDtypeStruc...  3.72 us
    pallas_call x1, Pallas kernels, finish(): pl.pallas_call(functools.partial(finish_kernel, rows_n, cols_n), name='fi...  2.77 us

profile of v4, /device:TPU:69, one launch (start us, length us, event | category | flops | bytes accessed | tf_op | source)
XLA Modules:
  0.0 48.4 jit_solution(18250764534407157210)
XLA Ops:
  0.0 0.0 copy-start
  0.0 28.8 %exchange.1 = (s32[32,3,128]{2,1,0:T(4,128)S(1)}, bf16[32,12,128]{2,1,0:T(8,128)(2,1)S(1)}) custom-call(s32[32,128]{1,0:T(8,128)} %cell_hbm.1, bf16[32,512]{1,0:T(8,128)(2,1)} %weight_hbm.1, s32[1,32]{1,0:T(1,128)} %bitcast.1), custom_call_target="tpu_custom_call" | custom-call | tf_op jit(solution)/shard_map/exchange/pallas_call | solution.py:172
  28.8 3.7 %outer.1 = (f32[4,256,1024]{2,1,0:T(8,128)S(1)}, s32[128,128]{1,0:T(8,128)S(1)}, s32[128,128]{1,0:T(8,128)S(1)}, f32[4,128,128]{2,1,0:T(8,128)S(1)}) custom-call(s32[32,3,128]{2,1,0:T(4,128)S(1)} %get-tuple-element.15.cells_ref, bf16[32,12,128]{2,1,0:T(8,128)(2,1)S(1)} %get-tuple-element.16.weights_ref), custom_call_target="tpu_custom_call" | custom-call | tf_op jit(solution)/shard_map/outer/pallas_call | solution.py:317
  32.5 12.9 %inner.1 = (f32[4,256,1024]{2,1,0:T(8,128)S(1)}, f32[4,256,1152]{2,1,0:T(8,128)S(1)}, f32[4,16,1152]{2,1,0:T(8,128)S(1)}, f32[4,16,1152]{2,1,0:T(8,128)S(1)}) custom-call(f32[2,4]{1,0:T(2,128)} %spread_ref.1, f32[4,256,1024]{2,1,0:T(8,128)S(1)} %get-tuple-element.17.raw_ref, s32[128,128]{1,0:T(8,128)S(1)} %get-tuple-element.18.rows_s, ...), custom_call_target="tpu_custom_call" | custom-call | tf_op jit(solution)/shard_map/inner/pallas_call | solution.py:463
  45.4 0.0 copy-done
  45.4 2.8 %finish.1 = f32[4,256,1024]{2,1,0:T(8,128)} custom-call(f32[2,4]{1,0:T(2,128)S(1)} %copy-done, f32[4,256,1024]{2,1,0:T(8,128)S(1)} %get-tuple-element.21.done_ref, f32[4,256,1152]{2,1,0:T(8,128)S(1)} %get-tuple-element.22.tall, f32[4,16,1152]{2,1,0:T(8,128)S(1)} %get-tuple-element.23.above, f32[4,16,1152]{2,1,0:T(8,128)S(1)} %get-tuple-element.24.below), custom_call_target="tpu_custom_call" | custom-call | tf_op jit(solution)/shard_map/finish/pallas_call | solution.py:544
Async XLA Ops:
  0.0 45.4 %copy-start = (f32[2,4]{1,0:T(2,128)S(1)}, f32[2,4]{1,0:T(2,128)}, u32[]{:S(2)}) copy-start(f32[2,4]{1,0:T(2,128)} %spread_ref.1) | copy-start | bytes 100

commit v5 on v4

--- a/solution.py
+++ b/solution.py
@@ -14,6 +14,8 @@
 LANES = 128
 WINDOW = 64
 LEAD = 24
+BITS = 9
+HALF = 1 << (BITS - 1)
 CHUNK_ROWS = 2
 UNROLL = 5
 MESH = pl.DeviceIdType.MESH
@@ -34,12 +36,12 @@
 
 
 def exchange_kernel(
-    rows_n, cols_n, cell_hbm, weight_hbm, tile_hbm, cells_out, weights_out,
-    cell_ref, weight_ref, tile_ref, values, keys_t, sorted_points, send_cells, send_weights,
+    rows_n, cols_n, cell_hbm, weight_hbm, tile_hbm, message_out,
+    cell_ref, weight_ref, tile_ref, values, keys_t, sorted_points, send_message,
     send_sem, recv_sem, local_sem
 ):
     loads = [
-        pltpu.make_async_copy(source, target, local_sem.at[2 + i])
+        pltpu.make_async_copy(source, target, local_sem.at[i])
         for i, (source, target) in enumerate(
             ((cell_hbm, cell_ref), (weight_hbm, weight_ref), (tile_hbm, tile_ref))
         )
@@ -79,27 +81,26 @@
     earlier = (tile_down == tile) & (iota(square, 0) < iota(square, 1))
     turn_of = jnp.sum(earlier.astype(jnp.int32), axis=0, keepdims=True)
     cells = cell_ref[...]
-    within = cells & (TILE_COLS - 1)
+    rows_each = channels + 2
     parts = [weight_ref[:, c * points : (c + 1) * points] for c in range(channels)] + [
-        part.astype(F32).astype(BF16)
-        for part in (
-            cells >> (TILE_COLS.bit_length() - 1),
-            within >> (LANES.bit_length() - 1),
-            within & (LANES - 1),
-        )
+        (part - HALF).astype(F32).astype(BF16)
+        for part in (cells >> BITS, cells & (2 * HALF - 1))
     ]
     group = CAPACITY * points
-    ramp = (iota((1, points), 1) * (TILE_ROWS // points)).astype(F32)
+    ramp = (iota((1, points), 1) * (TILE_ROWS // points * TILE_COLS // (2 * HALF)) - HALF).astype(F32)
     keys = []
     for k in range(CAPACITY):
         chosen = ((iota((peers, blocks), 0) == tile) & (turn_of == k)).astype(F32)
         empty = jnp.sum(chosen, axis=1, keepdims=True) < 0.5
         placed = dot(chosen.astype(BF16), jnp.concatenate(parts, axis=1))
-        for v in range(channels + 3):
+        for v in range(rows_each):
             piece = placed[:, v * points : (v + 1) * points]
             if v == channels:
                 piece = jnp.where(empty, ramp, piece)
-                keys.append(piece * 512.0 + (iota((1, points), 1) + k * points).astype(F32))
+                index = (iota((1, points), 1) + k * points).astype(F32)
+                keys.append((piece + float(HALF)) * 512.0 + index)
+            if v == channels + 1:
+                piece = jnp.where(empty, -float(HALF), piece)
             values[v, :, k * points : (k + 1) * points] = piece
     pad = jnp.zeros((points - peers, points), F32)
     keys_t[...] = jnp.concatenate(
@@ -119,7 +120,8 @@
         lane = lane + (third & 3) * quarter + chunk * CHUNK_ROWS + (third >> 2)
         hot = (iota((group, group), 0) == lane).astype(F32).astype(BF16)
         piece = jnp.concatenate(
-            [values[v, t : t + 1, :] for v in range(channels + 3)] + [jnp.zeros((1, group), F32)],
+            [values[v, t : t + 1, :] for v in range(rows_each)]
+            + [jnp.zeros((8 - rows_each, group), F32)],
             axis=0,
         ).astype(BF16)
         sorted_points[t] = lax.dot_general(
@@ -127,37 +129,25 @@
         )
     for k in range(CAPACITY):
         part = slice(k * points, (k + 1) * points)
-        cell = sorted_points[:, channels, part] * TILE_COLS
-        cell = cell + sorted_points[:, channels + 1, part] * LANES + sorted_points[:, channels + 2, part]
-        send_cells[:, k, :] = cell.astype(jnp.int32)
-        for c in range(channels):
-            send_weights[:, k * channels + c, :] = sorted_points[:, c, part].astype(BF16)
-
-    own = [
-        pltpu.make_async_copy(send_cells.at[me], cells_out.at[me], local_sem.at[0]),
-        pltpu.make_async_copy(send_weights.at[me], weights_out.at[me], local_sem.at[1]),
-    ]
+        for v in range(rows_each):
+            send_message[:, k * rows_each + v, :] = sorted_points[:, v, part].astype(BF16)
+
+    own = pltpu.make_async_copy(send_message.at[me], message_out.at[me], local_sem.at[3])
     pl.semaphore_wait(barrier, peers - 1)
     copies = []
     for i, (row, col) in enumerate(targets):
-        peer = row * cols_n + col
-        for a, (source, out) in enumerate(
-            ((send_cells, cells_out), (send_weights, weights_out))
-        ):
-            copy = pltpu.make_async_remote_copy(
-                src_ref=source.at[peer],
-                dst_ref=out.at[me],
-                send_sem=send_sem.at[a, i],
-                recv_sem=recv_sem.at[a, i],
-                device_id={"row": row, "col": col},
-                device_id_type=MESH,
-            )
-            copy.start()
-            copies.append(copy)
-    for copy in own:
+        copy = pltpu.make_async_remote_copy(
+            src_ref=send_message.at[row * cols_n + col],
+            dst_ref=message_out.at[me],
+            send_sem=send_sem.at[i],
+            recv_sem=recv_sem.at[i],
+            device_id={"row": row, "col": col},
+            device_id_type=MESH,
+        )
         copy.start()
-    for copy in own:
-        copy.wait()
+        copies.append(copy)
+    own.start()
+    own.wait()
     for copy in copies:
         copy.wait_recv()
     for copy in copies:
@@ -168,35 +158,33 @@
     blocks, points = cell_index.shape
     channels = weights.shape[1] // points
     peers = rows_n * cols_n
-    vmem = pl.BlockSpec(memory_space=pltpu.VMEM)
+    message = (peers, CAPACITY * (channels + 2), points)
     return pl.pallas_call(
         functools.partial(exchange_kernel, rows_n, cols_n),
         name="exchange",
-        out_shape=(
-            jax.ShapeDtypeStruct((peers, CAPACITY, points), jnp.int32),
-            jax.ShapeDtypeStruct((peers, CAPACITY * channels, points), BF16),
-        ),
+        out_shape=jax.ShapeDtypeStruct(message, BF16),
         in_specs=[pl.BlockSpec(memory_space=pltpu.MemorySpace.HBM)] * 3,
-        out_specs=(vmem, vmem),
+        out_specs=pl.BlockSpec(memory_space=pltpu.VMEM),
         scratch_shapes=[
             pltpu.VMEM(cell_index.shape, jnp.int32),
             pltpu.VMEM(weights.shape, BF16),
             pltpu.VMEM((1, blocks), jnp.int32),
-            pltpu.VMEM((3 + channels, peers, CAPACITY * points), F32),
+            pltpu.VMEM((channels + 2, peers, CAPACITY * points), F32),
             pltpu.VMEM((CAPACITY * points, points), F32),
             pltpu.VMEM((peers, 8, CAPACITY * points), F32),
-            pltpu.VMEM((peers, CAPACITY, points), jnp.int32),
-            pltpu.VMEM((peers, CAPACITY * channels, points), BF16),
-            pltpu.SemaphoreType.DMA((2, peers - 1)),
-            pltpu.SemaphoreType.DMA((2, peers - 1)),
-            pltpu.SemaphoreType.DMA((5,)),
+            pltpu.VMEM(message, BF16),
+            pltpu.SemaphoreType.DMA((peers - 1,)),
+            pltpu.SemaphoreType.DMA((peers - 1,)),
+            pltpu.SemaphoreType.DMA((4,)),
         ],
-        compiler_params=pltpu.CompilerParams(collective_id=0, has_side_effects=True, vmem_limit_bytes=8 << 20),
+        compiler_params=pltpu.CompilerParams(
+            collective_id=0, has_side_effects=True, vmem_limit_bytes=8 << 20
+        ),
     )(*(in_hbm(x) for x in (cell_index, weights, block_tile.reshape(1, -1))))
 
 
-def turned(slots, quarter):
-    wide = jnp.concatenate(
+def widened(slots, quarter):
+    return jnp.concatenate(
         [
             jnp.concatenate([s[:, v * quarter : (v + 1) * quarter] for v in range(4)], axis=0)
             for s in slots
@@ -204,7 +192,6 @@
         + [jnp.zeros((LANES, LANES - len(slots) * quarter), F32)],
         axis=1,
     )
-    return jnp.transpose(wide)
 
 
 def add_window(raw_ref, rows_s, cols_s, weights_s, j, low, stop, base):
@@ -223,8 +210,8 @@
         )
 
     row = take(rows_s)
-    col = take(cols_s)
     count = row.shape[1]
+    cols = pltpu.roll(cols_s[...], lax.rem(LANES - CHUNK_ROWS * j, LANES), axis=1)
     offset = jnp.where((row >= low) & (row < stop), row - base, -1)
     hot = iota((WINDOW, count), 0) == offset
     left = jnp.concatenate(
@@ -232,10 +219,16 @@
         axis=0,
     )
     for g in range(TILE_COLS // span):
-        right = (iota((span, count), 0) == col - g * span).astype(F32).astype(BF16)
-        layer = lax.dot_general(
-            left, right, (((1,), (1,)), ((), ())), preferred_element_type=F32
-        )
+        target = iota((LANES, span), 1) + g * span
+        right = jnp.concatenate(
+            [
+                (target == cols[:, quarter * k + i : quarter * k + i + 1]).astype(F32).astype(BF16)
+                for k in range(CAPACITY)
+                for i in range(CHUNK_ROWS)
+            ],
+            axis=0,
+        )
+        layer = dot(left, right)
         for c in range(channels):
             raw_ref[c, pl.ds(base, WINDOW), g * span : (g + 1) * span] += layer[
                 c * WINDOW : (c + 1) * WINDOW
@@ -253,21 +246,26 @@
 
 
 def outer_kernel(
-    cells_ref, weights_ref, raw_ref, rows_s, cols_s, weights_s, wide_s, first_s, last_s, next_s
+    message_ref, raw_ref, rows_s, cols_s, weights_s, wide_s, first_s, last_s, next_s
 ):
-    senders, slots, points = cells_ref.shape
-    channels = weights_ref.shape[1] // slots
+    senders, rows_all, points = message_ref.shape
+    rows_each = rows_all // CAPACITY
+    channels = rows_each - 2
     quarter = points // 4
     chunks = quarter // CHUNK_ROWS
-    wide_s[...] = weights_ref[...].astype(F32)
-    cells = turned([cells_ref[:, k, :].astype(F32) for k in range(slots)], quarter).astype(jnp.int32)
-    rows = cells >> (TILE_COLS.bit_length() - 1)
+    wide_s[...] = message_ref[...].astype(F32)
+
+    def wide(v):
+        return widened([wide_s[:, k * rows_each + v, :] for k in range(CAPACITY)], quarter)
+
+    cells = (wide(channels) + HALF) * (2 * HALF) + (wide(channels + 1) + HALF)
+    cols_s[...] = cells.astype(jnp.int32) & (TILE_COLS - 1)
+    rows = jnp.transpose(cells).astype(jnp.int32) >> (TILE_COLS.bit_length() - 1)
     rows_s[...] = rows
-    cols_s[...] = cells & (TILE_COLS - 1)
     for c in range(channels):
-        weights_s[c] = turned([wide_s[:, k * channels + c, :] for k in range(slots)], quarter)
+        weights_s[c] = jnp.transpose(wide(c))
     low, high = rows[:quarter], rows[:quarter]
-    for k in range(1, slots):
+    for k in range(1, CAPACITY):
         low = jnp.minimum(low, rows[quarter * k : quarter * (k + 1)])
         high = jnp.maximum(high, rows[quarter * k : quarter * (k + 1)])
     low = jnp.min(low, axis=1, keepdims=True)
@@ -309,9 +307,9 @@
     lax.fori_loop(0, chunks, rest, 0)
 
 
-def outer(cells, weights):
-    senders, slots, points = cells.shape
-    channels = weights.shape[1] // slots
+def outer(message):
+    senders, rows_all, points = message.shape
+    channels = rows_all // CAPACITY - 2
     vmem = pl.BlockSpec(memory_space=pltpu.VMEM)
     turns = points // 4 // CHUNK_ROWS
     return pl.pallas_call(
@@ -323,12 +321,12 @@
             jax.ShapeDtypeStruct((LANES, LANES), jnp.int32),
             jax.ShapeDtypeStruct((channels, LANES, LANES), F32),
         ),
-        in_specs=[vmem] * 2,
+        in_specs=[vmem],
         out_specs=(vmem,) * 4,
-        scratch_shapes=[pltpu.VMEM((senders, slots * channels, points), F32)]
+        scratch_shapes=[pltpu.VMEM(message.shape, F32)]
         + [pltpu.SMEM((turns,), jnp.int32)] * 3,
         compiler_params=pltpu.CompilerParams(vmem_limit_bytes=16 << 20),
-    )(cells, weights)
+    )(message)
 
 
 def split(value):
@@ -362,7 +360,7 @@
 
 def inner_kernel(
     rows_n, cols_n, spread_hbm, raw_ref, rows_s, cols_s, weights_s,
-    out_ref, tall, above, below, spread_ref, acc, side, send_sem, recv_sem, load_sem
+    out_ref, tall, above, below, spread_ref, acc, send_sem, recv_sem, load_sem
 ):
     channels, height, width = raw_ref.shape
     my_row, my_col = lax.axis_index("row"), lax.axis_index("col")
@@ -428,15 +426,20 @@
             tall[c, :, cols] = along_rows(high, low, acc[c, :, cols])
         return carry
 
+    def partner(c):
+        return remote(4 + c, tall.at[c, :, near], tall.at[c, :, beyond], peers[4])
+
+    def next_rows(c, carry):
+        own_rows(c, carry)
+        partner(c - 1).start()
+        return carry
+
     own_rows(0, 0)
-    partner = remote(4, acc.at[:, :, near], side, peers[4])
-    partner.start()
-    lax.fori_loop(1, channels, own_rows, 0)
-    partner.wait_recv()
+    lax.fori_loop(1, channels, next_rows, 0)
+    partner(channels - 1).start()
 
     def inner_cols(c, carry):
-        high, low = row_band(c)
-        tall[c, :, width:] = along_rows(high, low, side[c])
+        partner(c).wait_recv()
         band, high = col_band(spread_ref[1, c])
         rows = slice(REACH, height - REACH)
 
@@ -453,7 +456,7 @@
     lax.fori_loop(0, channels, inner_cols, 0)
     for copy in halo:
         copy.wait_recv()
-    for copy in halo + [partner]:
+    for copy in halo + [partner(c) for c in range(channels)]:
         copy.wait_send()
 
 
@@ -474,9 +477,8 @@
         scratch_shapes=[
             pltpu.SMEM(spread.shape, F32),
             pltpu.VMEM(raw.shape, F32),
-            pltpu.VMEM((channels, height, LANES), F32),
-            pltpu.SemaphoreType.DMA((5,)),
-            pltpu.SemaphoreType.DMA((5,)),
+            pltpu.SemaphoreType.DMA((4 + channels,)),
+            pltpu.SemaphoreType.DMA((4 + channels,)),
             pltpu.SemaphoreType.DMA,
         ],
         compiler_params=pltpu.CompilerParams(
@@ -558,8 +560,8 @@
 
 def shards(cell_index, weights, block_tile, spread):
     rows_n, cols_n = lax.axis_size("row"), lax.axis_size("col")
-    cells, points = exchange(cell_index, weights, block_tile, rows_n, cols_n)
-    raw, rows, cols, values = outer(cells, points)
+    message = exchange(cell_index, weights, block_tile, rows_n, cols_n)
+    raw, rows, cols, values = outer(message)
     done = inner(spread, raw, rows, cols, values, rows_n, cols_n)
     return finish(spread, *done, rows_n, cols_n)
 

time: 48.5 us -> 48.3 us (level)
  no operation moved by 1% of the time
where the time goes in v5:
time: 48.3 us; the launch traced here: 48.2 us
  Pallas kernels  48 us (99%)
    pallas_call x1, Pallas kernels, exchange(): pl.pallas_call(functools.partial(exchange_kernel, rows_n, cols_n), name='...  28.7 us
    pallas_call x1, Pallas kernels, inner(): pl.pallas_call(functools.partial(inner_kernel, rows_n, cols_n), name='inn...  12.7 us
    pallas_call x1, Pallas kernels, outer(): pl.pallas_call(outer_kernel, name='outer', out_shape=(jax.ShapeDtypeStruc...  3.79 us
    pallas_call x1, Pallas kernels, finish(): pl.pallas_call(functools.partial(finish_kernel, rows_n, cols_n), name='fi...  2.77 us

profile of v5, /device:TPU:69, one launch (start us, length us, event | category | flops | bytes accessed | tf_op | source)
XLA Modules:
  0.0 48.2 jit_solution(1675689865995439889)
XLA Ops:
  0.0 0.0 copy-start
  0.0 28.7 %exchange.1.message_ref = bf16[32,18,128]{2,1,0:T(8,128)(2,1)S(1)} custom-call(s32[32,128]{1,0:T(8,128)} %cell_hbm.1, bf16[32,512]{1,0:T(8,128)(2,1)} %weight_hbm.1, s32[1,32]{1,0:T(1,128)} %bitcast.1), custom_call_target="tpu_custom_call" | custom-call | tf_op jit(solution)/shard_map/exchange/pallas_call | solution.py:162
  28.7 3.8 %outer.1 = (f32[4,256,1024]{2,1,0:T(8,128)S(1)}, s32[128,128]{1,0:T(8,128)S(1)}, s32[128,128]{1,0:T(8,128)S(1)}, f32[4,128,128]{2,1,0:T(8,128)S(1)}) custom-call(bf16[32,18,128]{2,1,0:T(8,128)(2,1)S(1)} %exchange.1.message_ref), custom_call_target="tpu_custom_call" | custom-call | tf_op jit(solution)/shard_map/outer/pallas_call | solution.py:315
  32.5 12.7 %inner.1 = (f32[4,256,1024]{2,1,0:T(8,128)S(1)}, f32[4,256,1152]{2,1,0:T(8,128)S(1)}, f32[4,16,1152]{2,1,0:T(8,128)S(1)}, f32[4,16,1152]{2,1,0:T(8,128)S(1)}) custom-call(f32[2,4]{1,0:T(2,128)} %spread_ref.1, f32[4,256,1024]{2,1,0:T(8,128)S(1)} %get-tuple-element.13.raw_ref, s32[128,128]{1,0:T(8,128)S(1)} %get-tuple-element.14.rows_s, ...), custom_call_target="tpu_custom_call" | custom-call | tf_op jit(solution)/shard_map/inner/pallas_call | solution.py:466
  45.2 0.0 copy-done
  45.2 2.8 %finish.1 = f32[4,256,1024]{2,1,0:T(8,128)} custom-call(f32[2,4]{1,0:T(2,128)S(1)} %copy-done, f32[4,256,1024]{2,1,0:T(8,128)S(1)} %get-tuple-element.17.done_ref, f32[4,256,1152]{2,1,0:T(8,128)S(1)} %get-tuple-element.18.tall, f32[4,16,1152]{2,1,0:T(8,128)S(1)} %get-tuple-element.19.above, f32[4,16,1152]{2,1,0:T(8,128)S(1)} %get-tuple-element.20.below), custom_call_target="tpu_custom_call" | custom-call | tf_op jit(solution)/shard_map/finish/pallas_call | solution.py:546
Async XLA Ops:
  0.0 45.2 %copy-start = (f32[2,4]{1,0:T(2,128)S(1)}, f32[2,4]{1,0:T(2,128)}, u32[]{:S(2)}) copy-start(f32[2,4]{1,0:T(2,128)} %spread_ref.1) | copy-start | bytes 100

commit v6 on v5

--- a/solution.py
+++ b/solution.py
@@ -17,7 +17,7 @@
 BITS = 9
 HALF = 1 << (BITS - 1)
 CHUNK_ROWS = 2
-UNROLL = 5
+UNROLL = 3
 MESH = pl.DeviceIdType.MESH
 F32 = jnp.float32
 BF16 = jnp.bfloat16
@@ -36,7 +36,7 @@
 
 
 def exchange_kernel(
-    rows_n, cols_n, cell_hbm, weight_hbm, tile_hbm, message_out,
+    rows_n, cols_n, cell_hbm, weight_hbm, tile_hbm, message_out, zeros_out,
     cell_ref, weight_ref, tile_ref, values, keys_t, sorted_points, send_message,
     send_sem, recv_sem, local_sem
 ):
@@ -132,6 +132,7 @@
         for v in range(rows_each):
             send_message[:, k * rows_each + v, :] = sorted_points[:, v, part].astype(BF16)
 
+    zeros_out[...] = jnp.zeros_like(zeros_out)
     own = pltpu.make_async_copy(send_message.at[me], message_out.at[me], local_sem.at[3])
     pl.semaphore_wait(barrier, peers - 1)
     copies = []
@@ -162,9 +163,12 @@
     return pl.pallas_call(
         functools.partial(exchange_kernel, rows_n, cols_n),
         name="exchange",
-        out_shape=jax.ShapeDtypeStruct(message, BF16),
+        out_shape=(
+            jax.ShapeDtypeStruct(message, BF16),
+            jax.ShapeDtypeStruct((channels, TILE_ROWS, TILE_COLS), F32),
+        ),
         in_specs=[pl.BlockSpec(memory_space=pltpu.MemorySpace.HBM)] * 3,
-        out_specs=pl.BlockSpec(memory_space=pltpu.VMEM),
+        out_specs=(pl.BlockSpec(memory_space=pltpu.VMEM),) * 2,
         scratch_shapes=[
             pltpu.VMEM(cell_index.shape, jnp.int32),
             pltpu.VMEM(weights.shape, BF16),
@@ -246,7 +250,7 @@
 
 
 def outer_kernel(
-    message_ref, raw_ref, rows_s, cols_s, weights_s, wide_s, first_s, last_s, next_s
+    message_ref, zeros_ref, raw_ref, rows_s, cols_s, weights_s, wide_s, first_s, last_s, next_s
 ):
     senders, rows_all, points = message_ref.shape
     rows_each = rows_all // CAPACITY
@@ -279,7 +283,6 @@
         first_s[j] = first
         last_s[j] = functools.reduce(jnp.maximum, highs)
         next_s[j] = jnp.where(first < done, first, done + WINDOW)
-    raw_ref[...] = jnp.zeros_like(raw_ref)
 
     def add(j, low, stop):
         base = pl.multiple_of(jnp.minimum(low, TILE_ROWS - WINDOW), 8)
@@ -307,7 +310,7 @@
     lax.fori_loop(0, chunks, rest, 0)
 
 
-def outer(message):
+def outer(message, zeros):
     senders, rows_all, points = message.shape
     channels = rows_all // CAPACITY - 2
     vmem = pl.BlockSpec(memory_space=pltpu.VMEM)
@@ -321,12 +324,13 @@
             jax.ShapeDtypeStruct((LANES, LANES), jnp.int32),
             jax.ShapeDtypeStruct((channels, LANES, LANES), F32),
         ),
-        in_specs=[vmem],
+        in_specs=[vmem] * 2,
+        input_output_aliases={1: 0},
         out_specs=(vmem,) * 4,
         scratch_shapes=[pltpu.VMEM(message.shape, F32)]
         + [pltpu.SMEM((turns,), jnp.int32)] * 3,
         compiler_params=pltpu.CompilerParams(vmem_limit_bytes=16 << 20),
-    )(message)
+    )(message, zeros)
 
 
 def split(value):
@@ -375,6 +379,17 @@
     peers = [at(prev, my_col), at(following, my_col), at(prev, other), at(following, other), at(my_row, other)]
     for peer in peers:
         pl.semaphore_signal(barrier, inc=1, device_id=peer, device_id_type=MESH)
+    load = pltpu.make_async_copy(spread_hbm, spread_ref, load_sem)
+    load.start()
+    acc[...] = raw_ref[...]
+    tall_rows, begin, end = inner_chunks(LANES // 4 // CHUNK_ROWS)
+
+    def chunk(j, carry):
+        base = pl.multiple_of(tall_rows * j - LEAD, 8)
+        add_window(acc, rows_s, cols_s, weights_s, j, base, base + WINDOW, base)
+        return carry
+
+    chunk(begin, 0)
     pl.semaphore_wait(barrier, len(peers))
     near = pl.ds(pl.multiple_of((1 - my_col) * (width - LANES), LANES), LANES)
     main = pl.ds(0, width)
@@ -395,18 +410,7 @@
     ]
     for copy in halo:
         copy.start()
-    load = pltpu.make_async_copy(spread_hbm, spread_ref, load_sem)
-    load.start()
-
-    acc[...] = raw_ref[...]
-    tall_rows, begin, end = inner_chunks(LANES // 4 // CHUNK_ROWS)
-
-    def chunk(j, carry):
-        base = pl.multiple_of(tall_rows * j - LEAD, 8)
-        add_window(acc, rows_s, cols_s, weights_s, j, base, base + WINDOW, base)
-        return carry
-
-    lax.fori_loop(begin, end, chunk, 0, unroll=UNROLL)
+    lax.fori_loop(begin + 1, end, chunk, 0, unroll=UNROLL)
 
     def row_band(c):
         return split(tap(iota((height, height), 1) - iota((height, height), 0), spread_ref[0, c]))
@@ -560,8 +564,7 @@
 
 def shards(cell_index, weights, block_tile, spread):
     rows_n, cols_n = lax.axis_size("row"), lax.axis_size("col")
-    message = exchange(cell_index, weights, block_tile, rows_n, cols_n)
-    raw, rows, cols, values = outer(message)
+    raw, rows, cols, values = outer(*exchange(cell_index, weights, block_tile, rows_n, cols_n))
     done = inner(spread, raw, rows, cols, values, rows_n, cols_n)
     return finish(spread, *done, rows_n, cols_n)
 

time: 48.3 us -> 47.4 us (0.981)
  Pallas kernels: 48 us -> 47.1 us
    pallas_call x1, Pallas kernels: 12.7 us -> 11.9 us  [inner(): pl.pallas_call(functools.partial(inner_kernel, rows_n, cols_n), name='inn...]
where the time goes in v6:
time: 47.4 us; the launch traced here: 47.3 us
  Pallas kernels  47.1 us (99%)
    pallas_call x1, Pallas kernels, exchange(): pl.pallas_call(functools.partial(exchange_kernel, rows_n, cols_n), name='...  28.8 us
    pallas_call x1, Pallas kernels, inner(): pl.pallas_call(functools.partial(inner_kernel, rows_n, cols_n), name='inn...  11.9 us
    pallas_call x1, Pallas kernels, outer(): pl.pallas_call(outer_kernel, name='outer', out_shape=(jax.ShapeDtypeStruc...  3.53 us
    pallas_call x1, Pallas kernels, finish(): pl.pallas_call(functools.partial(finish_kernel, rows_n, cols_n), name='fi...  2.77 us

profile of v6, /device:TPU:69, one launch (start us, length us, event | category | flops | bytes accessed | tf_op | source)
XLA Modules:
  0.0 47.3 jit_solution(12727854643541215633)
XLA Ops:
  0.0 28.8 %exchange.1 = (bf16[32,18,128]{2,1,0:T(8,128)(2,1)S(1)}, f32[4,256,1024]{2,1,0:T(8,128)S(1)}) custom-call(s32[32,128]{1,0:T(8,128)} %cell_hbm.1, bf16[32,512]{1,0:T(8,128)(2,1)} %weight_hbm.1, s32[1,32]{1,0:T(1,128)} %bitcast.1), custom_call_target="tpu_custom_call" | custom-call | tf_op jit(solution)/shard_map/exchange/pallas_call | solution.py:163
  28.8 0.0 copy-start
  28.8 3.5 %outer.1 = (f32[4,256,1024]{2,1,0:T(8,128)S(1)}, s32[128,128]{1,0:T(8,128)S(1)}, s32[128,128]{1,0:T(8,128)S(1)}, f32[4,128,128]{2,1,0:T(8,128)S(1)}) custom-call(bf16[32,18,128]{2,1,0:T(8,128)(2,1)S(1)} %get-tuple-element.15.message_ref, f32[4,256,1024]{2,1,0:T(8,128)S(1)} %get-tuple-element.16.zeros_ref), custom_call_target="tpu_custom_call", output_to_operand_aliasing={{0}: (1, {})} | custom-call | tf_op jit(solution)/shard_map/outer/pallas_call | solution.py:318
  32.4 11.9 %inner.1 = (f32[4,256,1024]{2,1,0:T(8,128)S(1)}, f32[4,256,1152]{2,1,0:T(8,128)S(1)}, f32[4,16,1152]{2,1,0:T(8,128)S(1)}, f32[4,16,1152]{2,1,0:T(8,128)S(1)}) custom-call(f32[2,4]{1,0:T(2,128)} %spread_ref.1, f32[4,256,1024]{2,1,0:T(8,128)S(1)} %get-tuple-element.17.raw_ref, s32[128,128]{1,0:T(8,128)S(1)} %get-tuple-element.18.rows_s, ...), custom_call_target="tpu_custom_call" | custom-call | tf_op jit(solution)/shard_map/inner/pallas_call | solution.py:470
  44.3 0.0 copy-done
  44.3 2.8 %finish.1 = f32[4,256,1024]{2,1,0:T(8,128)} custom-call(f32[2,4]{1,0:T(2,128)S(1)} %copy-done, f32[4,256,1024]{2,1,0:T(8,128)S(1)} %get-tuple-element.21.done_ref, f32[4,256,1152]{2,1,0:T(8,128)S(1)} %get-tuple-element.22.tall, f32[4,16,1152]{2,1,0:T(8,128)S(1)} %get-tuple-element.23.above, f32[4,16,1152]{2,1,0:T(8,128)S(1)} %get-tuple-element.24.below), custom_call_target="tpu_custom_call" | custom-call | tf_op jit(solution)/shard_map/finish/pallas_call | solution.py:550
Async XLA Ops:
  28.8 15.5 %copy-start = (f32[2,4]{1,0:T(2,128)S(1)}, f32[2,4]{1,0:T(2,128)}, u32[]{:S(2)}) copy-start(f32[2,4]{1,0:T(2,128)} %spread_ref.1) | copy-start | bytes 100

commit v7 on v6

--- a/solution.py
+++ b/solution.py
@@ -250,7 +250,7 @@
 
 
 def outer_kernel(
-    message_ref, zeros_ref, raw_ref, rows_s, cols_s, weights_s, wide_s, first_s, last_s, next_s
+    cols_n, message_ref, zeros_ref, raw_ref, rows_s, cols_s, weights_s, corner_ref, wide_s, first_s, last_s, next_s
 ):
     senders, rows_all, points = message_ref.shape
     rows_each = rows_all // CAPACITY
@@ -308,25 +308,37 @@
         return carry
 
     lax.fori_loop(0, chunks, rest, 0)
-
-
-def outer(message, zeros):
+    my_col = lax.axis_index("col")
+    near = pl.ds(pl.multiple_of((1 - my_col) * (TILE_COLS - LANES), LANES), LANES)
+    for i, start in enumerate((0, TILE_ROWS - REACH)):
+        packed = jnp.zeros((REACH, LANES), F32)
+        lane = iota(packed.shape, 1)
+        for c in range(channels):
+            block = raw_ref[c, start : start + REACH, near]
+            block = pltpu.roll(block, REACH * c + REACH * (1 - my_col), axis=1)
+            mine = (lane >= REACH * c) & (lane < REACH * (c + 1))
+            packed = jnp.where(mine, block, packed)
+        corner_ref[i] = packed
+
+
+def outer(message, zeros, cols_n):
     senders, rows_all, points = message.shape
     channels = rows_all // CAPACITY - 2
     vmem = pl.BlockSpec(memory_space=pltpu.VMEM)
     turns = points // 4 // CHUNK_ROWS
     return pl.pallas_call(
-        outer_kernel,
+        functools.partial(outer_kernel, cols_n),
         name="outer",
         out_shape=(
             jax.ShapeDtypeStruct((channels, TILE_ROWS, TILE_COLS), F32),
             jax.ShapeDtypeStruct((LANES, LANES), jnp.int32),
             jax.ShapeDtypeStruct((LANES, LANES), jnp.int32),
             jax.ShapeDtypeStruct((channels, LANES, LANES), F32),
+            jax.ShapeDtypeStruct((2, REACH, LANES), F32),
         ),
         in_specs=[vmem] * 2,
         input_output_aliases={1: 0},
-        out_specs=(vmem,) * 4,
+        out_specs=(vmem,) * 5,
         scratch_shapes=[pltpu.VMEM(message.shape, F32)]
         + [pltpu.SMEM((turns,), jnp.int32)] * 3,
         compiler_params=pltpu.CompilerParams(vmem_limit_bytes=16 << 20),
@@ -363,8 +375,8 @@
 
 
 def inner_kernel(
-    rows_n, cols_n, spread_hbm, raw_ref, rows_s, cols_s, weights_s,
-    out_ref, tall, above, below, spread_ref, acc, send_sem, recv_sem, load_sem
+    rows_n, cols_n, spread_hbm, raw_ref, rows_s, cols_s, weights_s, corner_ref,
+    out_ref, tall, above, below, corners, spread_ref, acc, send_sem, recv_sem, load_sem
 ):
     channels, height, width = raw_ref.shape
     my_row, my_col = lax.axis_index("row"), lax.axis_index("col")
@@ -392,7 +404,6 @@
     chunk(begin, 0)
     pl.semaphore_wait(barrier, len(peers))
     near = pl.ds(pl.multiple_of((1 - my_col) * (width - LANES), LANES), LANES)
-    main = pl.ds(0, width)
     beyond = pl.ds(width, LANES)
     top, bottom = pl.ds(0, REACH), pl.ds(height - REACH, REACH)
 
@@ -403,10 +414,10 @@
         )
 
     halo = [
-        remote(0, raw_ref.at[:, bottom, main], above.at[:, :, main], peers[1]),
-        remote(1, raw_ref.at[:, top, main], below.at[:, :, main], peers[0]),
-        remote(2, raw_ref.at[:, bottom, near], above.at[:, :, beyond], peers[3]),
-        remote(3, raw_ref.at[:, top, near], below.at[:, :, beyond], peers[2]),
+        remote(0, raw_ref.at[:, bottom, :], above, peers[1]),
+        remote(1, raw_ref.at[:, top, :], below, peers[0]),
+        remote(2, corner_ref.at[1], corners.at[0], peers[3]),
+        remote(3, corner_ref.at[0], corners.at[1], peers[2]),
     ]
     for copy in halo:
         copy.start()
@@ -457,27 +468,29 @@
         along_cols(block, block(count), count, my_col, cols_n, band, high, store)
         return carry
 
-    lax.fori_loop(0, channels, inner_cols, 0)
+    lax.fori_loop(0, channels - 1, inner_cols, 0)
+    partner(channels - 1).wait_recv()
     for copy in halo:
         copy.wait_recv()
     for copy in halo + [partner(c) for c in range(channels)]:
         copy.wait_send()
 
 
-def inner(spread, raw, rows, cols, weights, rows_n, cols_n):
+def inner(spread, raw, rows, cols, weights, corner, rows_n, cols_n):
     channels, height, width = raw.shape
     vmem = pl.BlockSpec(memory_space=pltpu.VMEM)
     return pl.pallas_call(
         functools.partial(inner_kernel, rows_n, cols_n),
         name="inner",
         out_shape=(
-            jax.ShapeDtypeStruct(raw.shape, F32),
+            jax.ShapeDtypeStruct((channels - 1, height, width), F32),
             jax.ShapeDtypeStruct((channels, height, width + LANES), F32),
-            jax.ShapeDtypeStruct((channels, REACH, width + LANES), F32),
-            jax.ShapeDtypeStruct((channels, REACH, width + LANES), F32),
+            jax.ShapeDtypeStruct((channels, REACH, width), F32),
+            jax.ShapeDtypeStruct((channels, REACH, width), F32),
+            jax.ShapeDtypeStruct(corner.shape, F32),
         ),
-        in_specs=[pl.BlockSpec(memory_space=pltpu.MemorySpace.HBM)] + [vmem] * 4,
-        out_specs=(vmem,) * 4,
+        in_specs=[pl.BlockSpec(memory_space=pltpu.MemorySpace.HBM)] + [vmem] * 5,
+        out_specs=(vmem,) * 5,
         scratch_shapes=[
             pltpu.SMEM(spread.shape, F32),
             pltpu.VMEM(raw.shape, F32),
@@ -488,34 +501,52 @@
         compiler_params=pltpu.CompilerParams(
             collective_id=1, has_side_effects=True, vmem_limit_bytes=24 << 20
         ),
-    )(in_hbm(spread), raw, rows, cols, weights)
+    )(in_hbm(spread), raw, rows, cols, weights, corner)
 
 
 def finish_kernel(
-    rows_n, cols_n, spread_ref, done_ref, tall, above, below, out_ref, edge, inner_sem, edge_sem
+    rows_n, cols_n, spread_ref, done_ref, tall, above, below, corners, out_ref,
+    last, edge, inner_sem, edge_sem
 ):
-    channels, height, width = done_ref.shape
+    channels, height, width = out_ref.shape
     my_row, my_col = lax.axis_index("row"), lax.axis_index("col")
-    copies = []
-    for c in range(channels):
-        rows = pl.ds(REACH, height - 2 * REACH)
-        copies.append(
-            pltpu.make_async_copy(done_ref.at[c, rows], out_ref.at[c, rows], inner_sem.at[c])
-        )
-        copies[-1].start()
+    count = width // LANES
+    rows = pl.ds(REACH, height - 2 * REACH)
+    copies = [
+        pltpu.make_async_copy(done_ref.at[c, rows], out_ref.at[c, rows], inner_sem.at[c])
+        for c in range(channels - 1)
+    ]
+    for copy in copies:
+        copy.start()
+    c = channels - 1
+
+    def last_block(n):
+        return tall[c, REACH : height - REACH, n * LANES : (n + 1) * LANES]
+
+    def last_store(n, value):
+        last[:, n * LANES : (n + 1) * LANES] = value
+
+    band, high = col_band(spread_ref[1, c])
+    along_cols(last_block, last_block(count), count, my_col, cols_n, band, high, last_store)
+    copies.append(pltpu.make_async_copy(last, out_ref.at[c, rows], inner_sem.at[c]))
+    copies[-1].start()
     shape = (REACH, 3 * REACH)
     part = iota(shape, 1) >> (REACH.bit_length() - 1)
     offset = (iota(shape, 1) & (REACH - 1)) - iota(shape, 0)
     for c in range(channels):
         sides = []
-        for halo, start, shift, real in (
-            (above, 0, -REACH, my_row > 0),
-            (below, height - REACH, REACH, my_row + 1 < rows_n),
+        turn = lax.rem(my_col * (LANES - REACH) + LANES - REACH * c, LANES)
+        for i, (halo, start, shift, real) in enumerate(
+            (
+                (above, 0, -REACH, my_row > 0),
+                (below, height - REACH, REACH, my_row + 1 < rows_n),
+            )
         ):
             taps = jnp.where(real, tap(offset + shift, spread_ref[0, c]), 0.0)
             high = taps.astype(BF16).astype(F32)
             taps = jnp.where(part == 1, taps - high, high).astype(BF16)
-            x_high, x_low = split(halo[c])
+            beyond = pltpu.roll(corners[i], turn, axis=1)
+            x_high, x_low = split(jnp.concatenate([halo[c], beyond], axis=1))
             sides.append(
                 tall[c, start : start + REACH, :]
                 + dot(taps, jnp.concatenate([x_high, x_high, x_low], axis=0))
@@ -529,7 +560,6 @@
         def store(n, value):
             edge[c, :, n * LANES : (n + 1) * LANES] = value
 
-        count = width // LANES
         along_cols(block, block(count), count, my_col, cols_n, band, high, store)
         for i, start in enumerate((0, height - REACH)):
             copies.append(
@@ -544,28 +574,31 @@
         copy.wait()
 
 
-def finish(spread, done, tall, above, below, rows_n, cols_n):
-    channels, height, width = done.shape
+def finish(spread, done, tall, above, below, corners, rows_n, cols_n):
+    channels, height, wide = tall.shape
+    width = wide - LANES
     vmem = pl.BlockSpec(memory_space=pltpu.VMEM)
     return pl.pallas_call(
         functools.partial(finish_kernel, rows_n, cols_n),
         name="finish",
-        out_shape=jax.ShapeDtypeStruct(done.shape, F32),
-        in_specs=[pl.BlockSpec(memory_space=pltpu.SMEM)] + [vmem] * 4,
+        out_shape=jax.ShapeDtypeStruct((channels, height, width), F32),
+        in_specs=[pl.BlockSpec(memory_space=pltpu.SMEM)] + [vmem] * 5,
         out_specs=pl.BlockSpec(memory_space=pltpu.MemorySpace.HBM),
         scratch_shapes=[
+            pltpu.VMEM((height - 2 * REACH, width), F32),
             pltpu.VMEM((channels, 2 * REACH, width), F32),
             pltpu.SemaphoreType.DMA((channels,)),
             pltpu.SemaphoreType.DMA((2, channels)),
         ],
         compiler_params=pltpu.CompilerParams(vmem_limit_bytes=12 << 20),
-    )(spread, done, tall, above, below)
+    )(spread, done, tall, above, below, corners)
 
 
 def shards(cell_index, weights, block_tile, spread):
     rows_n, cols_n = lax.axis_size("row"), lax.axis_size("col")
-    raw, rows, cols, values = outer(*exchange(cell_index, weights, block_tile, rows_n, cols_n))
-    done = inner(spread, raw, rows, cols, values, rows_n, cols_n)
+    message, zeros = exchange(cell_index, weights, block_tile, rows_n, cols_n)
+    points = outer(message, zeros, cols_n)
+    done = inner(spread, *points, rows_n, cols_n)
     return finish(spread, *done, rows_n, cols_n)
 
 

time: 47.4 us -> 47.4 us (level)
    pallas_call x1, Pallas kernels: 11.9 us -> 11.3 us  [inner(): pl.pallas_call(functools.partial(inner_kernel, rows_n, cols_n), name='inn...]
    pallas_call x1, Pallas kernels: 2.77 us -> 3.31 us  [finish(): pl.pallas_call(functools.partial(finish_kernel, rows_n, cols_n), name='fi...]
where the time goes in v7:
time: 47.4 us; the launch traced here: 47.2 us
  Pallas kernels  47 us (99%)
    pallas_call x1, Pallas kernels, exchange(): pl.pallas_call(functools.partial(exchange_kernel, rows_n, cols_n), name='...  28.8 us
    pallas_call x1, Pallas kernels, inner(): pl.pallas_call(functools.partial(inner_kernel, rows_n, cols_n), name='inn...  11.3 us
    pallas_call x1, Pallas kernels, outer(): pl.pallas_call(functools.partial(outer_kernel, cols_n), name='outer', out...  3.62 us
    pallas_call x1, Pallas kernels, finish(): pl.pallas_call(functools.partial(finish_kernel, rows_n, cols_n), name='fi...  3.31 us

profile of v7, /device:TPU:69, one launch (start us, length us, event | category | flops | bytes accessed | tf_op | source)
XLA Modules:
  0.0 47.2 jit_solution(12670678610210149955)
XLA Ops:
  0.0 28.8 %exchange.1 = (bf16[32,18,128]{2,1,0:T(8,128)(2,1)S(1)}, f32[4,256,1024]{2,1,0:T(8,128)S(1)}) custom-call(s32[32,128]{1,0:T(8,128)} %cell_hbm.1, bf16[32,512]{1,0:T(8,128)(2,1)} %weight_hbm.1, s32[1,32]{1,0:T(1,128)} %bitcast.1), custom_call_target="tpu_custom_call" | custom-call | tf_op jit(solution)/shard_map/exchange/pallas_call | solution.py:163
  28.8 0.0 copy-start
  28.8 3.6 %outer.1 = (f32[4,256,1024]{2,1,0:T(8,128)S(1)}, s32[128,128]{1,0:T(8,128)S(1)}, s32[128,128]{1,0:T(8,128)S(1)}, f32[4,128,128]{2,1,0:T(8,128)S(1)}, f32[2,16,128]{2,1,0:T(8,128)S(1)}) custom-call(bf16[32,18,128]{2,1,0:T(8,128)(2,1)S(1)} %get-tuple-element.17.message_ref, ...), custom_call_target="tpu_custom_call", output_to_operand_aliasing={{0}: (1, {})} | custom-call | tf_op jit(solution)/shard_map/outer/pallas_call | solution.py:329
  32.5 11.3 %inner.1 = (f32[3,256,1024]{2,1,0:T(8,128)S(1)}, f32[4,256,1152]{2,1,0:T(8,128)S(1)}, f32[4,16,1024]{2,1,0:T(8,128)S(1)}, f32[4,16,1024]{2,1,0:T(8,128)S(1)}, f32[2,16,128]{2,1,0:T(8,128)S(1)}) custom-call(f32[2,4]{1,0:T(2,128)} %spread_ref.1, f32[4,256,1024]{2,1,0:T(8,128)S(1)} %get-tuple-element.19.raw_ref, s32[128,128]{1,0:T(8,128)S(1)} %get-tuple-element.20.rows_s, ...), custom_call_target="tpu_custom_call" | custom-call | tf_op jit(solution)/shard_map/inner/pallas_call | solution.py:482
  43.8 0.0 copy-done
  43.8 3.3 %finish.1 = f32[4,256,1024]{2,1,0:T(8,128)} custom-call(f32[2,4]{1,0:T(2,128)S(1)} %copy-done, f32[3,256,1024]{2,1,0:T(8,128)S(1)} %get-tuple-element.24.done_ref, f32[4,256,1152]{2,1,0:T(8,128)S(1)} %get-tuple-element.25.tall, f32[4,16,1024]{2,1,0:T(8,128)S(1)} %get-tuple-element.26.above, f32[4,16,1024]{2,1,0:T(8,128)S(1)} %get-tuple-element.27.below, ...), custom_call_target="tpu_custom_call" | custom-call | tf_op jit(solution)/shard_map/finish/pallas_call | solution.py:581
Async XLA Ops:
  28.8 14.9 %copy-start = (f32[2,4]{1,0:T(2,128)S(1)}, f32[2,4]{1,0:T(2,128)}, u32[]{:S(2)}) copy-start(f32[2,4]{1,0:T(2,128)} %spread_ref.1) | copy-start | bytes 100

commit v8 on v7

--- a/solution.py
+++ b/solution.py
@@ -239,18 +239,23 @@
             ]
 
 
+def fixed_row(j, chunks):
+    row = TILE_ROWS // chunks * j - LEAD
+    return min(max(row, REACH), TILE_ROWS - REACH - WINDOW)
+
+
 def inner_chunks(chunks):
     tall = TILE_ROWS // chunks
     inner = [
         j
         for j in range(chunks)
-        if tall * j - LEAD >= REACH and tall * j - LEAD + WINDOW <= TILE_ROWS - REACH
+        if tall * (j - 1) >= REACH and tall * (j + 2) <= TILE_ROWS - REACH
     ]
-    return tall, inner[0], inner[-1] + 1
+    return inner[0], inner[-1] + 1
 
 
 def outer_kernel(
-    cols_n, message_ref, zeros_ref, raw_ref, rows_s, cols_s, weights_s, corner_ref, wide_s, first_s, last_s, next_s
+    cols_n, message_ref, zeros_ref, raw_ref, rows_s, cols_s, weights_s, corner_ref, wide_s, first_s, last_s, next_s, done_s
 ):
     senders, rows_all, points = message_ref.shape
     rows_each = rows_all // CAPACITY
@@ -274,12 +279,13 @@
         high = jnp.maximum(high, rows[quarter * k : quarter * (k + 1)])
     low = jnp.min(low, axis=1, keepdims=True)
     high = jnp.max(high, axis=1, keepdims=True)
-    tall, begin, end = inner_chunks(chunks)
+    begin, end = inner_chunks(chunks)
     for j in range(chunks):
         lows = [low[CHUNK_ROWS * j + i, 0] for i in range(CHUNK_ROWS)]
         highs = [high[CHUNK_ROWS * j + i, 0] for i in range(CHUNK_ROWS)]
         first = (functools.reduce(jnp.minimum, lows) >> 3) << 3
-        done = tall * j - LEAD if begin <= j < end else first
+        done = fixed_row(j, chunks) if begin <= j < end else first
+        done_s[j] = done
         first_s[j] = first
         last_s[j] = functools.reduce(jnp.maximum, highs)
         next_s[j] = jnp.where(first < done, first, done + WINDOW)
@@ -297,7 +303,7 @@
     lax.fori_loop(0, chunks - (end - begin), common, 0, unroll=True)
 
     def rest(j, carry):
-        done = jnp.where((j >= begin) & (j < end), tall * j - LEAD, first_s[j])
+        done = done_s[j]
 
         def more(low):
             stop = jnp.where(low < done, jnp.minimum(low + WINDOW, done), low + WINDOW)
@@ -340,7 +346,7 @@
         input_output_aliases={1: 0},
         out_specs=(vmem,) * 5,
         scratch_shapes=[pltpu.VMEM(message.shape, F32)]
-        + [pltpu.SMEM((turns,), jnp.int32)] * 3,
+        + [pltpu.SMEM((turns,), jnp.int32)] * 4,
         compiler_params=pltpu.CompilerParams(vmem_limit_bytes=16 << 20),
     )(message, zeros)
 
@@ -394,14 +400,18 @@
     load = pltpu.make_async_copy(spread_hbm, spread_ref, load_sem)
     load.start()
     acc[...] = raw_ref[...]
-    tall_rows, begin, end = inner_chunks(LANES // 4 // CHUNK_ROWS)
+    chunks = LANES // 4 // CHUNK_ROWS
+    begin, end = inner_chunks(chunks)
+
+    def add(j, base):
+        add_window(acc, rows_s, cols_s, weights_s, j, base, base + WINDOW, base)
 
     def chunk(j, carry):
-        base = pl.multiple_of(tall_rows * j - LEAD, 8)
-        add_window(acc, rows_s, cols_s, weights_s, j, base, base + WINDOW, base)
+        add(j, pl.multiple_of(TILE_ROWS // chunks * j - LEAD, 8))
         return carry
 
-    chunk(begin, 0)
+    for j in (begin, end - 1, begin + 1):
+        add(j, fixed_row(j, chunks))
     pl.semaphore_wait(barrier, len(peers))
     near = pl.ds(pl.multiple_of((1 - my_col) * (width - LANES), LANES), LANES)
     beyond = pl.ds(width, LANES)
@@ -421,7 +431,7 @@
     ]
     for copy in halo:
         copy.start()
-    lax.fori_loop(begin + 1, end, chunk, 0, unroll=UNROLL)
+    lax.fori_loop(begin + 2, end - 1, chunk, 0, unroll=UNROLL)
 
     def row_band(c):
         return split(tap(iota((height, height), 1) - iota((height, height), 0), spread_ref[0, c]))

time: 47.4 us -> 46.6 us (0.983)
  Pallas kernels: 47 us -> 46.2 us
    pallas_call x1, Pallas kernels: 3.62 us -> 2.78 us  [outer(): pl.pallas_call(functools.partial(outer_kernel, cols_n), name='outer', out...]
where the time goes in v8:
time: 46.6 us; the launch traced here: 46.4 us
  Pallas kernels  46.2 us (99%)
    pallas_call x1, Pallas kernels, exchange(): pl.pallas_call(functools.partial(exchange_kernel, rows_n, cols_n), name='...  28.8 us
    pallas_call x1, Pallas kernels, inner(): pl.pallas_call(functools.partial(inner_kernel, rows_n, cols_n), name='inn...  11.3 us
    pallas_call x1, Pallas kernels, finish(): pl.pallas_call(functools.partial(finish_kernel, rows_n, cols_n), name='fi...  3.31 us
    pallas_call x1, Pallas kernels, outer(): pl.pallas_call(functools.partial(outer_kernel, cols_n), name='outer', out...  2.78 us

profile of v8, /device:TPU:69, one launch (start us, length us, event | category | flops | bytes accessed | tf_op | source)
XLA Modules:
  0.0 46.4 jit_solution(14825806510627601165)
XLA Ops:
  0.0 28.8 %exchange.1 = (bf16[32,18,128]{2,1,0:T(8,128)(2,1)S(1)}, f32[4,256,1024]{2,1,0:T(8,128)S(1)}) custom-call(s32[32,128]{1,0:T(8,128)} %cell_hbm.1, bf16[32,512]{1,0:T(8,128)(2,1)} %weight_hbm.1, s32[1,32]{1,0:T(1,128)} %bitcast.1), custom_call_target="tpu_custom_call" | custom-call | tf_op jit(solution)/shard_map/exchange/pallas_call | solution.py:163
  28.8 0.0 copy-start
  28.8 2.8 %outer.1 = (f32[4,256,1024]{2,1,0:T(8,128)S(1)}, s32[128,128]{1,0:T(8,128)S(1)}, s32[128,128]{1,0:T(8,128)S(1)}, f32[4,128,128]{2,1,0:T(8,128)S(1)}, f32[2,16,128]{2,1,0:T(8,128)S(1)}) custom-call(bf16[32,18,128]{2,1,0:T(8,128)(2,1)S(1)} %get-tuple-element.17.message_ref, ...), custom_call_target="tpu_custom_call", output_to_operand_aliasing={{0}: (1, {})} | custom-call | tf_op jit(solution)/shard_map/outer/pallas_call | solution.py:335
  31.6 11.3 %inner.1 = (f32[3,256,1024]{2,1,0:T(8,128)S(1)}, f32[4,256,1152]{2,1,0:T(8,128)S(1)}, f32[4,16,1024]{2,1,0:T(8,128)S(1)}, f32[4,16,1024]{2,1,0:T(8,128)S(1)}, f32[2,16,128]{2,1,0:T(8,128)S(1)}) custom-call(f32[2,4]{1,0:T(2,128)} %spread_ref.1, f32[4,256,1024]{2,1,0:T(8,128)S(1)} %get-tuple-element.19.raw_ref, s32[128,128]{1,0:T(8,128)S(1)} %get-tuple-element.20.rows_s, ...), custom_call_target="tpu_custom_call" | custom-call | tf_op jit(solution)/shard_map/inner/pallas_call | solution.py:492
  43.0 0.0 copy-done
  43.0 3.3 %finish.1 = f32[4,256,1024]{2,1,0:T(8,128)} custom-call(f32[2,4]{1,0:T(2,128)S(1)} %copy-done, f32[3,256,1024]{2,1,0:T(8,128)S(1)} %get-tuple-element.24.done_ref, f32[4,256,1152]{2,1,0:T(8,128)S(1)} %get-tuple-element.25.tall, f32[4,16,1024]{2,1,0:T(8,128)S(1)} %get-tuple-element.26.above, f32[4,16,1024]{2,1,0:T(8,128)S(1)} %get-tuple-element.27.below, ...), custom_call_target="tpu_custom_call" | custom-call | tf_op jit(solution)/shard_map/finish/pallas_call | solution.py:591
Async XLA Ops:
  28.8 14.1 %copy-start = (f32[2,4]{1,0:T(2,128)S(1)}, f32[2,4]{1,0:T(2,128)}, u32[]{:S(2)}) copy-start(f32[2,4]{1,0:T(2,128)} %spread_ref.1) | copy-start | bytes 100

commit v9 on v8

--- a/solution.py
+++ b/solution.py
@@ -17,7 +17,7 @@
 BITS = 9
 HALF = 1 << (BITS - 1)
 CHUNK_ROWS = 2
-UNROLL = 3
+UNROLL = 9
 MESH = pl.DeviceIdType.MESH
 F32 = jnp.float32
 BF16 = jnp.bfloat16
@@ -460,7 +460,7 @@
         return carry
 
     own_rows(0, 0)
-    lax.fori_loop(1, channels, next_rows, 0)
+    lax.fori_loop(1, channels, next_rows, 0, unroll=True)
     partner(channels - 1).start()
 
     def inner_cols(c, carry):
@@ -478,7 +478,7 @@
         along_cols(block, block(count), count, my_col, cols_n, band, high, store)
         return carry
 
-    lax.fori_loop(0, channels - 1, inner_cols, 0)
+    lax.fori_loop(0, channels - 1, inner_cols, 0, unroll=True)
     partner(channels - 1).wait_recv()
     for copy in halo:
         copy.wait_recv()

time: 46.6 us -> 45.9 us (0.985)
  Pallas kernels: 46.2 us -> 45.5 us
    pallas_call x1, Pallas kernels: 11.3 us -> 10.4 us  [inner(): pl.pallas_call(functools.partial(inner_kernel, rows_n, cols_n), name='inn...]
where the time goes in v9:
time: 45.9 us; the launch traced here: 45.7 us
  Pallas kernels  45.5 us (99%)
    pallas_call x1, Pallas kernels, exchange(): pl.pallas_call(functools.partial(exchange_kernel, rows_n, cols_n), name='...  28.8 us
    pallas_call x1, Pallas kernels, inner(): pl.pallas_call(functools.partial(inner_kernel, rows_n, cols_n), name='inn...  10.4 us
    pallas_call x1, Pallas kernels, finish(): pl.pallas_call(functools.partial(finish_kernel, rows_n, cols_n), name='fi...  3.31 us
    pallas_call x1, Pallas kernels, outer(): pl.pallas_call(functools.partial(outer_kernel, cols_n), name='outer', out...  2.96 us

profile of v9, /device:TPU:69, one launch (start us, length us, event | category | flops | bytes accessed | tf_op | source)
XLA Modules:
  0.0 45.7 jit_solution(6912808776007919282)
XLA Ops:
  0.0 28.8 %exchange.1 = (bf16[32,18,128]{2,1,0:T(8,128)(2,1)S(1)}, f32[4,256,1024]{2,1,0:T(8,128)S(1)}) custom-call(s32[32,128]{1,0:T(8,128)} %cell_hbm.1, bf16[32,512]{1,0:T(8,128)(2,1)} %weight_hbm.1, s32[1,32]{1,0:T(1,128)} %bitcast.1), custom_call_target="tpu_custom_call" | custom-call | tf_op jit(solution)/shard_map/exchange/pallas_call | solution.py:163
  28.8 0.0 copy-start
  28.8 3.0 %outer.1 = (f32[4,256,1024]{2,1,0:T(8,128)S(1)}, s32[128,128]{1,0:T(8,128)S(1)}, s32[128,128]{1,0:T(8,128)S(1)}, f32[4,128,128]{2,1,0:T(8,128)S(1)}, f32[2,16,128]{2,1,0:T(8,128)S(1)}) custom-call(bf16[32,18,128]{2,1,0:T(8,128)(2,1)S(1)} %get-tuple-element.17.message_ref, ...), custom_call_target="tpu_custom_call", output_to_operand_aliasing={{0}: (1, {})} | custom-call | tf_op jit(solution)/shard_map/outer/pallas_call | solution.py:335
  31.8 10.4 %inner.1 = (f32[3,256,1024]{2,1,0:T(8,128)S(1)}, f32[4,256,1152]{2,1,0:T(8,128)S(1)}, f32[4,16,1024]{2,1,0:T(8,128)S(1)}, f32[4,16,1024]{2,1,0:T(8,128)S(1)}, f32[2,16,128]{2,1,0:T(8,128)S(1)}) custom-call(f32[2,4]{1,0:T(2,128)} %spread_ref.1, f32[4,256,1024]{2,1,0:T(8,128)S(1)} %get-tuple-element.19.raw_ref, s32[128,128]{1,0:T(8,128)S(1)} %get-tuple-element.20.rows_s, ...), custom_call_target="tpu_custom_call" | custom-call | tf_op jit(solution)/shard_map/inner/pallas_call | solution.py:492
  42.2 0.0 copy-done
  42.2 3.3 %finish.1 = f32[4,256,1024]{2,1,0:T(8,128)} custom-call(f32[2,4]{1,0:T(2,128)S(1)} %copy-done, f32[3,256,1024]{2,1,0:T(8,128)S(1)} %get-tuple-element.24.done_ref, f32[4,256,1152]{2,1,0:T(8,128)S(1)} %get-tuple-element.25.tall, f32[4,16,1024]{2,1,0:T(8,128)S(1)} %get-tuple-element.26.above, f32[4,16,1024]{2,1,0:T(8,128)S(1)} %get-tuple-element.27.below, ...), custom_call_target="tpu_custom_call" | custom-call | tf_op jit(solution)/shard_map/finish/pallas_call | solution.py:591
Async XLA Ops:
  28.8 13.4 %copy-start = (f32[2,4]{1,0:T(2,128)S(1)}, f32[2,4]{1,0:T(2,128)}, u32[]{:S(2)}) copy-start(f32[2,4]{1,0:T(2,128)} %spread_ref.1) | copy-start | bytes 100

commit v10 on v9

--- a/solution.py
+++ b/solution.py
@@ -35,15 +35,39 @@
     return lax.dot_general(a, b, (((1,), (0,)), ((), ())), preferred_element_type=F32)
 
 
+def split(value):
+    high = value.astype(BF16)
+    return high, (value - high.astype(F32)).astype(BF16)
+
+
+def tap(offset, width):
+    near = jnp.abs(offset) <= REACH
+    far = offset.astype(F32)
+    return jnp.where(near, jnp.exp(-(far * far) / (2.0 * width * width)), 0.0)
+
+
+def col_band(width):
+    source = iota((2 * LANES, LANES), 0)
+    source = jnp.where(source < LANES + LANES // 2, source, source - 2 * LANES)
+    high, low = split(tap(source - iota((2 * LANES, LANES), 1), width))
+    return jnp.concatenate([high, low], axis=1)
+
+
 def exchange_kernel(
-    rows_n, cols_n, cell_hbm, weight_hbm, tile_hbm, message_out, zeros_out,
-    cell_ref, weight_ref, tile_ref, values, keys_t, sorted_points, send_message,
+    rows_n, cols_n, cell_hbm, weight_hbm, tile_hbm, spread_hbm,
+    message_out, zeros_out, row_bands, col_bands, halo_taps,
+    cell_ref, weight_ref, tile_ref, spread_ref, values, keys_t, sorted_points, send_message,
     send_sem, recv_sem, local_sem
 ):
     loads = [
         pltpu.make_async_copy(source, target, local_sem.at[i])
         for i, (source, target) in enumerate(
-            ((cell_hbm, cell_ref), (weight_hbm, weight_ref), (tile_hbm, tile_ref))
+            (
+                (cell_hbm, cell_ref),
+                (weight_hbm, weight_ref),
+                (tile_hbm, tile_ref),
+                (spread_hbm, spread_ref),
+            )
         )
     ]
     for load in loads:
@@ -132,8 +156,7 @@
         for v in range(rows_each):
             send_message[:, k * rows_each + v, :] = sorted_points[:, v, part].astype(BF16)
 
-    zeros_out[...] = jnp.zeros_like(zeros_out)
-    own = pltpu.make_async_copy(send_message.at[me], message_out.at[me], local_sem.at[3])
+    own = pltpu.make_async_copy(send_message.at[me], message_out.at[me], local_sem.at[4])
     pl.semaphore_wait(barrier, peers - 1)
     copies = []
     for i, (row, col) in enumerate(targets):
@@ -148,6 +171,20 @@
         copy.start()
         copies.append(copy)
     own.start()
+    zeros_out[...] = jnp.zeros_like(zeros_out)
+    square = (TILE_ROWS, TILE_ROWS)
+    shape = (REACH, 3 * REACH)
+    part = iota(shape, 1) >> (REACH.bit_length() - 1)
+    offset = (iota(shape, 1) & (REACH - 1)) - iota(shape, 0)
+    for c in range(channels):
+        high, low = split(tap(iota(square, 1) - iota(square, 0), spread_ref[0, c]))
+        row_bands[c, :TILE_ROWS] = high
+        row_bands[c, TILE_ROWS:] = low
+        col_bands[c] = col_band(spread_ref[1, c])
+        for i, (shift, real) in enumerate(((-REACH, my_row > 0), (REACH, my_row + 1 < rows_n))):
+            taps = jnp.where(real, tap(offset + shift, spread_ref[0, c]), 0.0)
+            high = taps.astype(BF16).astype(F32)
+            halo_taps[c, i] = jnp.where(part == 1, taps - high, high).astype(BF16)
     own.wait()
     for copy in copies:
         copy.wait_recv()
@@ -155,7 +192,7 @@
         copy.wait_send()
 
 
-def exchange(cell_index, weights, block_tile, rows_n, cols_n):
+def exchange(cell_index, weights, block_tile, spread, rows_n, cols_n):
     blocks, points = cell_index.shape
     channels = weights.shape[1] // points
     peers = rows_n * cols_n
@@ -166,25 +203,29 @@
         out_shape=(
             jax.ShapeDtypeStruct(message, BF16),
             jax.ShapeDtypeStruct((channels, TILE_ROWS, TILE_COLS), F32),
+            jax.ShapeDtypeStruct((channels, 2 * TILE_ROWS, TILE_ROWS), BF16),
+            jax.ShapeDtypeStruct((channels, 2 * LANES, 2 * LANES), BF16),
+            jax.ShapeDtypeStruct((channels, 2, REACH, 3 * REACH), BF16),
         ),
-        in_specs=[pl.BlockSpec(memory_space=pltpu.MemorySpace.HBM)] * 3,
-        out_specs=(pl.BlockSpec(memory_space=pltpu.VMEM),) * 2,
+        in_specs=[pl.BlockSpec(memory_space=pltpu.MemorySpace.HBM)] * 4,
+        out_specs=(pl.BlockSpec(memory_space=pltpu.VMEM),) * 5,
         scratch_shapes=[
             pltpu.VMEM(cell_index.shape, jnp.int32),
             pltpu.VMEM(weights.shape, BF16),
             pltpu.VMEM((1, blocks), jnp.int32),
+            pltpu.SMEM(spread.shape, F32),
             pltpu.VMEM((channels + 2, peers, CAPACITY * points), F32),
             pltpu.VMEM((CAPACITY * points, points), F32),
             pltpu.VMEM((peers, 8, CAPACITY * points), F32),
             pltpu.VMEM(message, BF16),
             pltpu.SemaphoreType.DMA((peers - 1,)),
             pltpu.SemaphoreType.DMA((peers - 1,)),
-            pltpu.SemaphoreType.DMA((4,)),
+            pltpu.SemaphoreType.DMA((5,)),
         ],
         compiler_params=pltpu.CompilerParams(
             collective_id=0, has_side_effects=True, vmem_limit_bytes=8 << 20
         ),
-    )(*(in_hbm(x) for x in (cell_index, weights, block_tile.reshape(1, -1))))
+    )(*(in_hbm(x) for x in (cell_index, weights, block_tile.reshape(1, -1), spread)))
 
 
 def widened(slots, quarter):
@@ -351,25 +392,7 @@
     )(message, zeros)
 
 
-def split(value):
-    high = value.astype(BF16)
-    return high, (value - high.astype(F32)).astype(BF16)
-
-
-def tap(offset, width):
-    near = jnp.abs(offset) <= REACH
-    far = offset.astype(F32)
-    return jnp.where(near, jnp.exp(-(far * far) / (2.0 * width * width)), 0.0)
-
-
-def col_band(width):
-    source = iota((2 * LANES, LANES), 0)
-    source = jnp.where(source < LANES + LANES // 2, source, source - 2 * LANES)
-    high, low = split(tap(source - iota((2 * LANES, LANES), 1), width))
-    return jnp.concatenate([high, low], axis=1), high
-
-
-def along_cols(block, beyond, count, my_col, cols_n, band, high, store):
+def along_cols(block, beyond, count, my_col, cols_n, band, store):
     for n in range(count):
         own = block(n)
         before = block(n - 1) if n else jnp.where(my_col > 0, beyond, 0.0)
@@ -377,12 +400,12 @@
         edge = jnp.where(iota(own.shape, 1) < LANES // 2, after, before)
         x_high, x_low = split(jnp.concatenate([own, edge], axis=1))
         both = dot(x_high, band)
-        store(n, both[:, :LANES] + both[:, LANES:] + dot(x_low, high))
+        store(n, both[:, :LANES] + both[:, LANES:] + dot(x_low, band[:, :LANES]))
 
 
 def inner_kernel(
-    rows_n, cols_n, spread_hbm, raw_ref, rows_s, cols_s, weights_s, corner_ref,
-    out_ref, tall, above, below, corners, spread_ref, acc, send_sem, recv_sem, load_sem
+    rows_n, cols_n, row_bands, col_bands, raw_ref, rows_s, cols_s, weights_s, corner_ref,
+    out_ref, tall, above, below, corners, acc, send_sem, recv_sem
 ):
     channels, height, width = raw_ref.shape
     my_row, my_col = lax.axis_index("row"), lax.axis_index("col")
@@ -397,8 +420,6 @@
     peers = [at(prev, my_col), at(following, my_col), at(prev, other), at(following, other), at(my_row, other)]
     for peer in peers:
         pl.semaphore_signal(barrier, inc=1, device_id=peer, device_id_type=MESH)
-    load = pltpu.make_async_copy(spread_hbm, spread_ref, load_sem)
-    load.start()
     acc[...] = raw_ref[...]
     chunks = LANES // 4 // CHUNK_ROWS
     begin, end = inner_chunks(chunks)
@@ -433,22 +454,15 @@
         copy.start()
     lax.fori_loop(begin + 2, end - 1, chunk, 0, unroll=UNROLL)
 
-    def row_band(c):
-        return split(tap(iota((height, height), 1) - iota((height, height), 0), spread_ref[0, c]))
-
-    def along_rows(high, low, x):
-        x_high, x_low = split(x)
-        both = dot(jnp.concatenate([high, low], axis=0), x_high)
-        return both[:height] + both[height:] + dot(high, x_low)
-
     step = 2 * LANES
-    load.wait()
 
     def own_rows(c, carry):
-        high, low = row_band(c)
+        bands = row_bands[c]
         for g in range(width // step):
             cols = slice(g * step, (g + 1) * step)
-            tall[c, :, cols] = along_rows(high, low, acc[c, :, cols])
+            x_high, x_low = split(acc[c, :, cols])
+            both = dot(bands, x_high)
+            tall[c, :, cols] = both[:height] + both[height:] + dot(bands[:height], x_low)
         return carry
 
     def partner(c):
@@ -465,7 +479,6 @@
 
     def inner_cols(c, carry):
         partner(c).wait_recv()
-        band, high = col_band(spread_ref[1, c])
         rows = slice(REACH, height - REACH)
 
         def block(n):
@@ -475,7 +488,7 @@
             out_ref[c, rows, n * LANES : (n + 1) * LANES] = value
 
         count = width // LANES
-        along_cols(block, block(count), count, my_col, cols_n, band, high, store)
+        along_cols(block, block(count), count, my_col, cols_n, col_bands[c], store)
         return carry
 
     lax.fori_loop(0, channels - 1, inner_cols, 0, unroll=True)
@@ -486,7 +499,7 @@
         copy.wait_send()
 
 
-def inner(spread, raw, rows, cols, weights, corner, rows_n, cols_n):
+def inner(row_bands, col_bands, raw, rows, cols, weights, corner, rows_n, cols_n):
     channels, height, width = raw.shape
     vmem = pl.BlockSpec(memory_space=pltpu.VMEM)
     return pl.pallas_call(
@@ -499,27 +512,25 @@
             jax.ShapeDtypeStruct((channels, REACH, width), F32),
             jax.ShapeDtypeStruct(corner.shape, F32),
         ),
-        in_specs=[pl.BlockSpec(memory_space=pltpu.MemorySpace.HBM)] + [vmem] * 5,
+        in_specs=[vmem] * 7,
         out_specs=(vmem,) * 5,
         scratch_shapes=[
-            pltpu.SMEM(spread.shape, F32),
             pltpu.VMEM(raw.shape, F32),
             pltpu.SemaphoreType.DMA((4 + channels,)),
             pltpu.SemaphoreType.DMA((4 + channels,)),
-            pltpu.SemaphoreType.DMA,
         ],
         compiler_params=pltpu.CompilerParams(
             collective_id=1, has_side_effects=True, vmem_limit_bytes=24 << 20
         ),
-    )(in_hbm(spread), raw, rows, cols, weights, corner)
+    )(row_bands, col_bands, raw, rows, cols, weights, corner)
 
 
 def finish_kernel(
-    rows_n, cols_n, spread_ref, done_ref, tall, above, below, corners, out_ref,
+    cols_n, col_bands, halo_taps, done_ref, tall, above, below, corners, out_ref,
     last, edge, inner_sem, edge_sem
 ):
     channels, height, width = out_ref.shape
-    my_row, my_col = lax.axis_index("row"), lax.axis_index("col")
+    my_col = lax.axis_index("col")
     count = width // LANES
     rows = pl.ds(REACH, height - 2 * REACH)
     copies = [
@@ -536,33 +547,20 @@
     def last_store(n, value):
         last[:, n * LANES : (n + 1) * LANES] = value
 
-    band, high = col_band(spread_ref[1, c])
-    along_cols(last_block, last_block(count), count, my_col, cols_n, band, high, last_store)
+    along_cols(last_block, last_block(count), count, my_col, cols_n, col_bands[c], last_store)
     copies.append(pltpu.make_async_copy(last, out_ref.at[c, rows], inner_sem.at[c]))
     copies[-1].start()
-    shape = (REACH, 3 * REACH)
-    part = iota(shape, 1) >> (REACH.bit_length() - 1)
-    offset = (iota(shape, 1) & (REACH - 1)) - iota(shape, 0)
     for c in range(channels):
         sides = []
         turn = lax.rem(my_col * (LANES - REACH) + LANES - REACH * c, LANES)
-        for i, (halo, start, shift, real) in enumerate(
-            (
-                (above, 0, -REACH, my_row > 0),
-                (below, height - REACH, REACH, my_row + 1 < rows_n),
-            )
-        ):
-            taps = jnp.where(real, tap(offset + shift, spread_ref[0, c]), 0.0)
-            high = taps.astype(BF16).astype(F32)
-            taps = jnp.where(part == 1, taps - high, high).astype(BF16)
+        for i, (halo, start) in enumerate(((above, 0), (below, height - REACH))):
             beyond = pltpu.roll(corners[i], turn, axis=1)
             x_high, x_low = split(jnp.concatenate([halo[c], beyond], axis=1))
             sides.append(
                 tall[c, start : start + REACH, :]
-                + dot(taps, jnp.concatenate([x_high, x_high, x_low], axis=0))
+                + dot(halo_taps[c, i], jnp.concatenate([x_high, x_high, x_low], axis=0))
             )
         rows = jnp.concatenate(sides, axis=0)
-        band, high = col_band(spread_ref[1, c])
 
         def block(n):
             return rows[:, n * LANES : (n + 1) * LANES]
@@ -570,7 +568,7 @@
         def store(n, value):
             edge[c, :, n * LANES : (n + 1) * LANES] = value
 
-        along_cols(block, block(count), count, my_col, cols_n, band, high, store)
+        along_cols(block, block(count), count, my_col, cols_n, col_bands[c], store)
         for i, start in enumerate((0, height - REACH)):
             copies.append(
                 pltpu.make_async_copy(
@@ -584,15 +582,15 @@
         copy.wait()
 
 
-def finish(spread, done, tall, above, below, corners, rows_n, cols_n):
+def finish(col_bands, halo_taps, done, tall, above, below, corners, cols_n):
     channels, height, wide = tall.shape
     width = wide - LANES
     vmem = pl.BlockSpec(memory_space=pltpu.VMEM)
     return pl.pallas_call(
-        functools.partial(finish_kernel, rows_n, cols_n),
+        functools.partial(finish_kernel, cols_n),
         name="finish",
         out_shape=jax.ShapeDtypeStruct((channels, height, width), F32),
-        in_specs=[pl.BlockSpec(memory_space=pltpu.SMEM)] + [vmem] * 5,
+        in_specs=[vmem] * 7,
         out_specs=pl.BlockSpec(memory_space=pltpu.MemorySpace.HBM),
         scratch_shapes=[
             pltpu.VMEM((height - 2 * REACH, width), F32),
@@ -601,15 +599,17 @@
             pltpu.SemaphoreType.DMA((2, channels)),
         ],
         compiler_params=pltpu.CompilerParams(vmem_limit_bytes=12 << 20),
-    )(spread, done, tall, above, below, corners)
+    )(col_bands, halo_taps, done, tall, above, below, corners)
 
 
 def shards(cell_index, weights, block_tile, spread):
     rows_n, cols_n = lax.axis_size("row"), lax.axis_size("col")
-    message, zeros = exchange(cell_index, weights, block_tile, rows_n, cols_n)
+    message, zeros, row_bands, col_bands, halo_taps = exchange(
+        cell_index, weights, block_tile, spread, rows_n, cols_n
+    )
     points = outer(message, zeros, cols_n)
-    done = inner(spread, *points, rows_n, cols_n)
-    return finish(spread, *done, rows_n, cols_n)
+    done = inner(row_bands, col_bands, *points, rows_n, cols_n)
+    return finish(col_bands, halo_taps, *done, cols_n)
 
 
 def solution(mesh):

time: 45.9 us -> 45.4 us (0.989)
  Pallas kernels: 45.5 us -> 45 us
    pallas_call x1, Pallas kernels: 3.31 us -> 2.71 us  [finish(): pl.pallas_call(functools.partial(finish_kernel, cols_n), name='finish', o...]
where the time goes in v10:
time: 45.4 us; the launch traced here: 45.2 us
  Pallas kernels  45 us (99%)
    pallas_call x1, Pallas kernels, exchange(): pl.pallas_call(functools.partial(exchange_kernel, rows_n, cols_n), name='...  28.7 us
    pallas_call x1, Pallas kernels, inner(): pl.pallas_call(functools.partial(inner_kernel, rows_n, cols_n), name='inn...  10.7 us
    pallas_call x1, Pallas kernels, outer(): pl.pallas_call(functools.partial(outer_kernel, cols_n), name='outer', out...  2.96 us
    pallas_call x1, Pallas kernels, finish(): pl.pallas_call(functools.partial(finish_kernel, cols_n), name='finish', o...  2.71 us

profile of v10, /device:TPU:69, one launch (start us, length us, event | category | flops | bytes accessed | tf_op | source)
XLA Modules:
  0.0 45.2 jit_solution(11823784443822332488)
XLA Ops:
  0.0 28.7 %exchange.1 = (bf16[32,18,128]{2,1,0:T(8,128)(2,1)S(1)}, f32[4,256,1024]{2,1,0:T(8,128)S(1)}, bf16[4,512,256]{2,1,0:T(8,128)(2,1)S(1)}, bf16[4,256,256]{2,1,0:T(8,128)(2,1)S(1)}, bf16[4,2,16,48]{3,2,1,0:T(8,128)(2,1)S(1)}) custom-call(s32[32,128]{1,0:T(8,128)} %cell_hbm.1, bf16[32,512]{1,0:T(8,128)(2,1)} %weight_hbm.1, s32[1,32]{1,0:T(1,128)} %bitcast.1, ...), custom_call_target="tpu_custom_call" | custom-call | tf_op jit(solution)/shard_map/exchange/pallas_call | solution.py:200
  28.7 3.0 %outer.1 = (f32[4,256,1024]{2,1,0:T(8,128)S(1)}, s32[128,128]{1,0:T(8,128)S(1)}, s32[128,128]{1,0:T(8,128)S(1)}, f32[4,128,128]{2,1,0:T(8,128)S(1)}, f32[2,16,128]{2,1,0:T(8,128)S(1)}) custom-call(bf16[32,18,128]{2,1,0:T(8,128)(2,1)S(1)} %get-tuple-element.23.message_ref, ...), custom_call_target="tpu_custom_call", output_to_operand_aliasing={{0}: (1, {})} | custom-call | tf_op jit(solution)/shard_map/outer/pallas_call | solution.py:376
  31.7 10.7 %inner.1 = (f32[3,256,1024]{2,1,0:T(8,128)S(1)}, f32[4,256,1152]{2,1,0:T(8,128)S(1)}, f32[4,16,1024]{2,1,0:T(8,128)S(1)}, f32[4,16,1024]{2,1,0:T(8,128)S(1)}, f32[2,16,128]{2,1,0:T(8,128)S(1)}) custom-call(bf16[4,512,256]{2,1,0:T(8,128)(2,1)S(1)} %get-tuple-element.22.row_bands, bf16[4,256,256]{2,1,0:T(8,128)(2,1)S(1)} %get-tuple-element.20.col_bands, ...), custom_call_target="tpu_custom_call" | custom-call | tf_op jit(solution)/shard_map/inner/pallas_call | solution.py:505
  42.4 2.7 %finish.1 = f32[4,256,1024]{2,1,0:T(8,128)} custom-call(bf16[4,256,256]{2,1,0:T(8,128)(2,1)S(1)} %get-tuple-element.20.col_bands, bf16[4,2,16,48]{3,2,1,0:T(8,128)(2,1)S(1)} %get-tuple-element.21.halo_taps, f32[3,256,1024]{2,1,0:T(8,128)S(1)} %get-tuple-element.30.done_ref, f32[4,256,1152]{2,1,0:T(8,128)S(1)} %get-tuple-element.31.tall, ...), custom_call_target="tpu_custom_call" | custom-call | tf_op jit(solution)/shard_map/finish/pallas_call | solution.py:589

commit v11 on v10

--- a/solution.py
+++ b/solution.py
@@ -431,7 +431,7 @@
         add(j, pl.multiple_of(TILE_ROWS // chunks * j - LEAD, 8))
         return carry
 
-    for j in (begin, end - 1, begin + 1):
+    for j in (begin, end - 1):
         add(j, fixed_row(j, chunks))
     pl.semaphore_wait(barrier, len(peers))
     near = pl.ds(pl.multiple_of((1 - my_col) * (width - LANES), LANES), LANES)
@@ -452,6 +452,7 @@
     ]
     for copy in halo:
         copy.start()
+    add(begin + 1, fixed_row(begin + 1, chunks))
     lax.fori_loop(begin + 2, end - 1, chunk, 0, unroll=UNROLL)
 
     step = 2 * LANES

time: 45.4 us -> 45.6 us (level)
  no operation moved by 1% of the time
where the time goes in v11:
time: 45.6 us; the launch traced here: 45.3 us
  Pallas kernels  45.2 us (99%)
    pallas_call x1, Pallas kernels, exchange(): pl.pallas_call(functools.partial(exchange_kernel, rows_n, cols_n), name='...  28.7 us
    pallas_call x1, Pallas kernels, inner(): pl.pallas_call(functools.partial(inner_kernel, rows_n, cols_n), name='inn...  10.8 us
    pallas_call x1, Pallas kernels, outer(): pl.pallas_call(functools.partial(outer_kernel, cols_n), name='outer', out...  2.96 us
    pallas_call x1, Pallas kernels, finish(): pl.pallas_call(functools.partial(finish_kernel, cols_n), name='finish', o...  2.71 us

profile of v11, /device:TPU:69, one launch (start us, length us, event | category | flops | bytes accessed | tf_op | source)
XLA Modules:
  0.0 45.3 jit_solution(12800306616968863768)
XLA Ops:
  0.0 28.7 %exchange.1 = (bf16[32,18,128]{2,1,0:T(8,128)(2,1)S(1)}, f32[4,256,1024]{2,1,0:T(8,128)S(1)}, bf16[4,512,256]{2,1,0:T(8,128)(2,1)S(1)}, bf16[4,256,256]{2,1,0:T(8,128)(2,1)S(1)}, bf16[4,2,16,48]{3,2,1,0:T(8,128)(2,1)S(1)}) custom-call(s32[32,128]{1,0:T(8,128)} %cell_hbm.1, bf16[32,512]{1,0:T(8,128)(2,1)} %weight_hbm.1, s32[1,32]{1,0:T(1,128)} %bitcast.1, ...), custom_call_target="tpu_custom_call" | custom-call | tf_op jit(solution)/shard_map/exchange/pallas_call | solution.py:200
  28.7 3.0 %outer.1 = (f32[4,256,1024]{2,1,0:T(8,128)S(1)}, s32[128,128]{1,0:T(8,128)S(1)}, s32[128,128]{1,0:T(8,128)S(1)}, f32[4,128,128]{2,1,0:T(8,128)S(1)}, f32[2,16,128]{2,1,0:T(8,128)S(1)}) custom-call(bf16[32,18,128]{2,1,0:T(8,128)(2,1)S(1)} %get-tuple-element.23.message_ref, ...), custom_call_target="tpu_custom_call", output_to_operand_aliasing={{0}: (1, {})} | custom-call | tf_op jit(solution)/shard_map/outer/pallas_call | solution.py:376
  31.7 10.8 %inner.1 = (f32[3,256,1024]{2,1,0:T(8,128)S(1)}, f32[4,256,1152]{2,1,0:T(8,128)S(1)}, f32[4,16,1024]{2,1,0:T(8,128)S(1)}, f32[4,16,1024]{2,1,0:T(8,128)S(1)}, f32[2,16,128]{2,1,0:T(8,128)S(1)}) custom-call(bf16[4,512,256]{2,1,0:T(8,128)(2,1)S(1)} %get-tuple-element.22.row_bands, bf16[4,256,256]{2,1,0:T(8,128)(2,1)S(1)} %get-tuple-element.20.col_bands, ...), custom_call_target="tpu_custom_call" | custom-call | tf_op jit(solution)/shard_map/inner/pallas_call | solution.py:506
  42.5 2.7 %finish.1 = f32[4,256,1024]{2,1,0:T(8,128)} custom-call(bf16[4,256,256]{2,1,0:T(8,128)(2,1)S(1)} %get-tuple-element.20.col_bands, bf16[4,2,16,48]{3,2,1,0:T(8,128)(2,1)S(1)} %get-tuple-element.21.halo_taps, f32[3,256,1024]{2,1,0:T(8,128)S(1)} %get-tuple-element.30.done_ref, f32[4,256,1152]{2,1,0:T(8,128)S(1)} %get-tuple-element.31.tall, ...), custom_call_target="tpu_custom_call" | custom-call | tf_op jit(solution)/shard_map/finish/pallas_call | solution.py:590
